TPU v7x, 32 devices: a whole 2x2x4 slice. The times are simulated.
32 devices in a mesh: bvec: 4 (over y, x), row: 2 (over core), col: 4 (over z).
Axes of the slice: x: 2, y: 2, z: 4, core: 2. Of those that a mesh axis runs over, the one named last changes fastest.
Arguments:
- m_matrices: float32 [4, 2, 2048, 2048], P('bvec', None, 'row', 'col'), may hold values from -2 to 2, as said below
- bvec_index: int32 [4], replicated, may hold values from 0 to 5
- weight_table: float32 [6], replicated, may hold values from 0.25 to 2
- grad_prev: float32 [2048, 2048], P('row', 'col'), may hold values from -4 to 4, as said below
- dir_prev: float32 [2048, 2048], P('row', 'col'), may hold values from -4 to 4, as said below
Outputs:
- spread: float32 [], replicated
- trial_spread: float32 [], replicated
- gradient: float32 [2048, 2048], P('row', 'col')
- direction: float32 [2048, 2048], P('row', 'col')
- trial_diag: float32 [4, 2, 2048], replicated
Inputs may be any that keep to these rules, and one draw needn't show every extreme that they name: Each matrix m_matrices[b, p] is symmetric. grad_prev is antisymmetric. dir_prev is antisymmetric.
All inputs are finite; a program needn't handle non-finite values.
Results may differ from a plain program's by a relative error of at most 0.0003.
Values sent between devices are 32-bit elements; how exact they have to be, the bound alone decides.
No kernel may reach another device: no remote copies, remote signals or barrier semaphores. Data moves between devices by JAX's collectives and lax.ppermute only.
A program may use at most 128 MiB of HBM per device.

v0:
```python
import jax
import jax.numpy as jnp
from jax import lax
from jax.sharding import PartitionSpec as P

TAYLOR = 8


STEP_SCALE = 1.75
HIGHEST = lax.Precision.HIGHEST


def product(left, right):
    return jnp.dot(left, right, precision=HIGHEST, preferred_element_type=jnp.float32)


def lookup_weights(bvec_index, weight_table):
    table_slots = jnp.arange(weight_table.shape[0], dtype=jnp.int32)
    return jnp.sum(
        jnp.where(table_slots[None, :] == bvec_index[:, None], weight_table[None, :], 0.0), axis=1
    )


def shards(m_matrices, bvec_index, weight_table, grad_prev, dir_prev):
    per_group = m_matrices.shape[0]
    local_rows = m_matrices.shape[2]
    local_cols = m_matrices.shape[3]
    matrix_order = local_rows * lax.axis_size("row")
    group_index = lax.axis_index("bvec")
    row_start = lax.axis_index("row") * local_rows
    col_start = lax.axis_index("col") * local_cols
    weight_all = lookup_weights(bvec_index, weight_table)
    weight_own = lax.dynamic_slice_in_dim(weight_all, group_index * per_group, per_group)
    row_ids = row_start + jnp.arange(local_rows, dtype=jnp.int32)
    col_ids = col_start + jnp.arange(local_cols, dtype=jnp.int32)
    on_diag = (row_ids[:, None] == col_ids[None, :]).astype(jnp.float32)
    own_diag = jnp.sum(m_matrices * on_diag, axis=2)
    share_diag = lax.psum(own_diag, "row")
    diagonal = lax.all_gather(share_diag, "col", axis=2, tiled=True)
    row_diag = lax.dynamic_slice_in_dim(diagonal, row_start, local_rows, 2)
    spread_own = (
        jnp.sum(weight_own[:, None] * (1.0 - diagonal[:, 0] ** 2 - diagonal[:, 1] ** 2))
        / matrix_order
    )
    leader = (lax.axis_index("row") == 0) & (lax.axis_index("col") == 0)
    spread_term = jnp.where(leader, spread_own, 0.0)
    differ = row_diag[:, :, :, None] - share_diag[:, :, None, :]
    weighted = 2.0 * weight_own[:, None, None] * jnp.sum(m_matrices * differ, axis=1)
    grad_part = jnp.sum(weighted, axis=0)
    gradient = lax.psum(grad_part, "bvec")
    counted = jnp.where(group_index == 0, 1.0, 0.0)
    grad_square = counted * jnp.sum(gradient * gradient)
    prev_square = counted * jnp.sum(grad_prev * grad_prev)
    cross_term = counted * jnp.sum(gradient * dir_prev)
    dir_square = counted * jnp.sum(dir_prev * dir_prev)
    totals = lax.psum(
        (spread_term, grad_square, prev_square, cross_term, dir_square), ("bvec", "row", "col")
    )
    spread = totals[0]
    beta_factor = totals[1] / (1.0 + totals[2])
    direction = beta_factor * dir_prev - gradient
    dir_norm = jnp.maximum(
        totals[1] - 2.0 * beta_factor * totals[3] + beta_factor * beta_factor * totals[4], 0.0
    )
    generator = STEP_SCALE * direction / jnp.sqrt(1.0 + dir_norm / matrix_order)
    block_ids = col_start + jnp.arange(local_cols, dtype=jnp.int32)
    eye_block = (row_ids[:, None] == block_ids[None, :]).astype(jnp.float32)
    horner_start = eye_block + generator / TAYLOR
    columns = lax.all_gather(generator, "row", axis=0, tiled=True)

    def accumulate(section):
        return product(section, columns)

    def horner_step(counter, current):
        folded = accumulate(lax.all_gather(current, "col", axis=1, tiled=True))
        divisor = (TAYLOR - 1 - counter).astype(jnp.float32)
        return eye_block + folded / divisor

    expmap = lax.fori_loop(0, TAYLOR - 1, horner_step, horner_start)
    expmap_cols = lax.all_gather(expmap, "row", axis=0, tiled=True)
    section = lax.all_gather(m_matrices, "col", axis=3, tiled=True)
    flattened = section.reshape((-1, section.shape[3]))
    rotated = product(flattened, expmap_cols).reshape(
        jnp.zeros(m_matrices.shape, jnp.float32).shape
    )
    trial_part = jnp.sum(expmap[None, None] * rotated, axis=2)
    trial_share = lax.psum(trial_part, "row")
    trial_group = lax.all_gather(trial_share, "col", axis=2, tiled=True)
    trial_diag = lax.all_gather(trial_group, "bvec", axis=0, tiled=True)
    trial_spread = (
        jnp.sum(weight_all[:, None] * (1.0 - trial_diag[:, 0] ** 2 - trial_diag[:, 1] ** 2))
        / matrix_order
    )
    return (spread, trial_spread, gradient, direction, trial_diag)


def solution(mesh):
    placed = (P("bvec", None, "row", "col"), P(), P(), P("row", "col"), P("row", "col"))
    return jax.shard_map(
        shards,
        mesh=mesh,
        in_specs=placed,
        out_specs=(P(), P(), P("row", "col"), P("row", "col"), P()),
        check_vma=False,
    )
```

profile of v0, /device:TPU:0, one launch (start us, length us, event | category | flops | bytes accessed | tf_op | source)
XLA Modules:
  0.0 1767.3 jit_solution(4512609184158823346)
XLA Ops:
  12.9 14.7 all_gather.25
  39.0 65.1 %all-reduce.3.cloned.1.call-done = f32[1024,512]{1,0:T(8,128)} async-done(((f32[1024,512]{1,0:T(8,128)}), f32[1024,512]{1,0:T(8,128)}) %all-reduce.3.cloned.1.call-update) | async-done | bytes 2097168 | tf_op jit(solution)/shard_map/psum | solution.py:50
  108.8 39.4 %all-reduce = (f32[]{:T(128)}, f32[]{:T(128)}, f32[]{:T(128)}, f32[]{:T(128)}, f32[]{:T(128)}) all-reduce(f32[]{:T(128)S(6)} %select_n.20, f32[]{:T(128)S(6)} %mul.139, f32[]{:T(128)S(6)} %mul.141, f32[]{:T(128)S(6)} %mul.148, f32[]{:T(128)S(6)} %mul.152), channel_id=1, replica_groups=mesh['bvec'=4,'row'=2,'col'=4] {'bvec','row','col'}, use_global_device_ids=true, to_apply=%region_4.5 | all-reduce | flops 5 | bytes 40 | tf_op jit(solution)/shard_map/psum | solution.py:56
  156.3 14.8 all-gather.5.cloned.1.call-done
  171.2 1178.3 %while.14 = (s32[]{:T(128)}, f32[1024,512]{1,0:T(8,128)S(1)}, f32[2048,512]{1,0:T(8,128)}, s32[512]{0:T(512)S(1)}, s32[1024]{0:T(1024)S(1)}, /*index=5*/s32[]{:T(128)}, s32[]{:T(128)}) while((s32[]{:T(128)}, f32[1024,512]{1,0:T(8,128)S(1)}, f32[2048,512]{1,0:T(8,128)}, s32[512]{0:T(512)S(1)}, s32[1024]{0:T(1024)S(1)}, ...), condition=%wide.region_16.17_spmd.clone, body=%wide.region_15.16_spmd.clone.sunk | while | flops 12886999040 | bytes 54532272 | solution.py:79
  172.5 152.4 %all-gather.11.cloned.1.call-done = f32[1024,2048]{1,0:T(8,128)} async-done(((f32[1024,512]{1,0:T(8,128)}), f32[1024,2048]{1,0:T(8,128)}) %all-gather.11.cloned.1.call-update) | async-done | bytes 8388624 | tf_op jit(solution)/shard_map/while/body/eval_jaxpr/all_gather | solution.py:75
  324.9 17.2 convert_add_fusion.2
  343.5 149.1 %all-gather.11.cloned.1.call-done = f32[1024,2048]{1,0:T(8,128)} async-done(((f32[1024,512]{1,0:T(8,128)}), f32[1024,2048]{1,0:T(8,128)}) %all-gather.11.cloned.1.call-update) | async-done | bytes 8388624 | tf_op jit(solution)/shard_map/while/body/eval_jaxpr/all_gather | solution.py:75
  492.7 17.2 convert_add_fusion.2
  511.2 149.1 %all-gather.11.cloned.1.call-done = f32[1024,2048]{1,0:T(8,128)} async-done(((f32[1024,512]{1,0:T(8,128)}), f32[1024,2048]{1,0:T(8,128)}) %all-gather.11.cloned.1.call-update) | async-done | bytes 8388624 | tf_op jit(solution)/shard_map/while/body/eval_jaxpr/all_gather | solution.py:75
  660.4 17.2 convert_add_fusion.2
  679.0 149.1 %all-gather.11.cloned.1.call-done = f32[1024,2048]{1,0:T(8,128)} async-done(((f32[1024,512]{1,0:T(8,128)}), f32[1024,2048]{1,0:T(8,128)}) %all-gather.11.cloned.1.call-update) | async-done | bytes 8388624 | tf_op jit(solution)/shard_map/while/body/eval_jaxpr/all_gather | solution.py:75
  828.1 17.2 convert_add_fusion.2
  846.7 149.5 %all-gather.11.cloned.1.call-done = f32[1024,2048]{1,0:T(8,128)} async-done(((f32[1024,512]{1,0:T(8,128)}), f32[1024,2048]{1,0:T(8,128)}) %all-gather.11.cloned.1.call-update) | async-done | bytes 8388624 | tf_op jit(solution)/shard_map/while/body/eval_jaxpr/all_gather | solution.py:75
  996.1 17.2 convert_add_fusion.2
  1014.7 149.5 %all-gather.11.cloned.1.call-done = f32[1024,2048]{1,0:T(8,128)} async-done(((f32[1024,512]{1,0:T(8,128)}), f32[1024,2048]{1,0:T(8,128)}) %all-gather.11.cloned.1.call-update) | async-done | bytes 8388624 | tf_op jit(solution)/shard_map/while/body/eval_jaxpr/all_gather | solution.py:75
  1164.2 17.2 convert_add_fusion.2
  1182.8 149.4 %all-gather.11.cloned.1.call-done = f32[1024,2048]{1,0:T(8,128)} async-done(((f32[1024,512]{1,0:T(8,128)}), f32[1024,2048]{1,0:T(8,128)}) %all-gather.11.cloned.1.call-update) | async-done | bytes 8388624 | tf_op jit(solution)/shard_map/while/body/eval_jaxpr/all_gather | solution.py:75
  1332.2 17.2 convert_add_fusion.2
  1354.2 9.8 all-gather.7.cloned.1.call-done
  1364.0 289.5 %all-gather.9.cloned.1.call-done = f32[1,2,1024,2048]{3,2,1,0:T(8,128)} async-done(((f32[1,2,1024,512]{3,2,1,0:T(8,128)}), f32[1,2,1024,2048]{3,2,1,0:T(8,128)}) %all-gather.9.cloned.1.call-update) | async-done | bytes 16777232 | tf_op jit(solution)/shard_map/all_gather | solution.py:81
  1653.5 57.2 %convolution_bitcast_fusion = f32[2048,512]{0,1:T(8,128)} fusion(f32[2048,512]{1,0:T(8,128)} %all-gather.7.cloned.1.call-done, f32[2048,2048]{1,0:T(8,128)} %bitcast.27), kind=kOutput, calls=%fused_computation.5 | convolution fusion | flops 25769803776 | bytes 25165824 | tf_op jit(solution)/shard_map/dot_general | solution.py:14
  1725.9 21.9 %all_gather.29 = f32[1,2,2048]{1,2,0:T(8,128)S(1)} all-gather(f32[1,2,512]{1,2,0:T(8,128)S(1)} %psum.63), channel_id=1, replica_groups=mesh['bvec'=4,'row'=2,'col'=4] {'col'}, dimensions={2}, use_global_device_ids=true | all-gather | bytes 20480 | tf_op jit(solution)/shard_map/all_gather | solution.py:88
  1748.1 8.2 all_gather.30
  (73 shorter events, 54.7 us)
Async XLA Ops:
  7.2 97.0 %all-reduce.3.cloned.1.call-start = ((), (), s32[]{:S(2)}) async-start(), calls=%async_computation | async-start | bytes 4194304 | tf_op jit(solution)/shard_map/psum | solution.py:50
  7.5 20.2 %copy-start.6 = (f32[6]{0:T(128)S(1)}, f32[6]{0:T(128)}, u32[]{:S(2)}) copy-start(f32[6]{0:T(128)} %param.9) | copy-start | bytes 76
  7.5 20.2 %copy-start.7 = (s32[4]{0:T(128)S(1)}, s32[4]{0:T(128)}, u32[]{:S(2)}) copy-start(s32[4]{0:T(128)} %param.8) | copy-start | bytes 52
  33.5 70.7 %copy-start.5 = (f32[1024,512]{1,0:T(8,128)S(1)}, f32[1024,512]{1,0:T(8,128)}, u32[]{:S(2)}) copy-start(f32[1024,512]{1,0:T(8,128)} %param.11) | copy-start | bytes 6291460
  33.5 137.7 %all-gather.5.cloned.1.call-start = ((), (), s32[]{:S(2)}) async-start(), calls=%async_computation.1 | async-start | bytes 6291456 | tf_op jit(solution)/shard_map/all_gather | solution.py:69
  171.2 153.8 %all-gather.11.cloned.1.call-start = ((), (), s32[]{:S(2)}) async-start(), calls=%async_computation.4 | async-start | bytes 10485760 | tf_op jit(solution)/shard_map/while/body/eval_jaxpr/all_gather | solution.py:75
  342.2 1.3 copy-start
  342.2 150.5 %all-gather.11.cloned.1.call-start = ((), (), s32[]{:S(2)}) async-start(), calls=%async_computation.4 | async-start | bytes 10485760 | tf_op jit(solution)/shard_map/while/body/eval_jaxpr/all_gather | solution.py:75
  509.9 1.3 copy-start
  509.9 150.5 %all-gather.11.cloned.1.call-start = ((), (), s32[]{:S(2)}) async-start(), calls=%async_computation.4 | async-start | bytes 10485760 | tf_op jit(solution)/shard_map/while/body/eval_jaxpr/all_gather | solution.py:75
  677.6 1.3 copy-start
  677.6 150.5 %all-gather.11.cloned.1.call-start = ((), (), s32[]{:S(2)}) async-start(), calls=%async_computation.4 | async-start | bytes 10485760 | tf_op jit(solution)/shard_map/while/body/eval_jaxpr/all_gather | solution.py:75
  845.3 1.3 copy-start
  845.3 150.8 %all-gather.11.cloned.1.call-start = ((), (), s32[]{:S(2)}) async-start(), calls=%async_computation.4 | async-start | bytes 10485760 | tf_op jit(solution)/shard_map/while/body/eval_jaxpr/all_gather | solution.py:75
  1013.4 1.3 copy-start
  1013.4 150.8 %all-gather.11.cloned.1.call-start = ((), (), s32[]{:S(2)}) async-start(), calls=%async_computation.4 | async-start | bytes 10485760 | tf_op jit(solution)/shard_map/while/body/eval_jaxpr/all_gather | solution.py:75
  1181.4 1.3 copy-start
  1181.4 150.8 %all-gather.11.cloned.1.call-start = ((), (), s32[]{:S(2)}) async-start(), calls=%async_computation.4 | async-start | bytes 10485760 | tf_op jit(solution)/shard_map/while/body/eval_jaxpr/all_gather | solution.py:75
  1349.4 1.3 copy-start.1
  1349.5 14.5 all-gather.7.cloned.1.call-start
  1350.8 1.6 copy-start.2
  1350.8 302.7 %all-gather.9.cloned.1.call-start = ((), (), s32[]{:S(2)}) async-start(), calls=%async_computation.3 | async-start | bytes 20971520 | tf_op jit(solution)/shard_map/all_gather | solution.py:81
  1710.7 6.7 copy-start.4
  1721.7 36.0 %copy-start.3 = (f32[1024,512]{1,0:T(8,128)S(1)}, f32[1024,512]{1,0:T(8,128)}, u32[]{:S(2)}) copy-start(f32[1024,512]{1,0:T(8,128)} %all-reduce.3.cloned.1.call-done) | copy-start | bytes 6291460
  (1 other events, 1.3 us)
Sparse Core Ops, SparseCore 0:
  33.6 70.4 all-reduce.2
  156.5 14.6 all-gather.4
  174.1 150.7 all-gather.10
  344.8 147.7 all-gather.10
  512.5 147.7 all-gather.10
  680.3 147.7 all-gather.10
  848.3 147.7 all-gather.10
  1016.4 147.7 all-gather.10
  1184.4 147.7 all-gather.10
  1352.1 11.8 all-gather.6
  1365.5 287.9 all-gather.8
where the time goes:
time: 1770 us
  waiting for transfers between devices  1430 us (81%)
  matrix products  178 us (10%)
  blocking collectives  91 us (5%)
  other arithmetic  24.3 us (1%)
  between operations  22.9 us (1%)
  local copies, waits for them, and re-layouts  22.4 us (1%)
    all_gather x7, waiting for transfers between devices, horner_step(): folded = accumulate(lax.all_gather(current, 'col', axis=1, tiled=True))  1050 us
    all_gather x1, waiting for transfers between devices, shards(): section = lax.all_gather(m_matrices, 'col', axis=3, tiled=True)  290 us
    dot_general x8, matrix products, product(): jnp.dot(left, right, precision=HIGHEST, preferred_element_type=jnp.float32)  178 us
    psum x1, waiting for transfers between devices, shards(): gradient = lax.psum(grad_part, 'bvec')  65.1 us
    psum x1, blocking collectives, shards(): lax.psum((spread_term, grad_square, prev_square, cross_term, dir_square),...  39.4 us
  transfers between devices with their start and end apart: 11, of which 11 were waited for; matrix products, arithmetic and copies ran while one was open for 0% of the time, Pallas kernels for 0%

commit v1 on v0

--- a/solution.py
+++ b/solution.py
@@ -1,17 +1,363 @@
 import jax
 import jax.numpy as jnp
 from jax import lax
+from jax.experimental import pallas as pl
+from jax.experimental.pallas import tpu as pltpu
 from jax.sharding import PartitionSpec as P
 
+
 TAYLOR = 8
-
-
 STEP_SCALE = 1.75
 HIGHEST = lax.Precision.HIGHEST
-
-
-def product(left, right):
-    return jnp.dot(left, right, precision=HIGHEST, preferred_element_type=jnp.float32)
+AXES = ("bvec", "row", "col")
+ANY = pl.BlockSpec(memory_space=pl.ANY)
+SMEM = pl.BlockSpec(memory_space=pltpu.SMEM)
+VMEM = pl.BlockSpec(memory_space=pltpu.VMEM)
+VMEM_LIMIT = 62 * 1024 * 1024
+
+
+def split_bf16(x):
+    high = x.astype(jnp.bfloat16)
+    low = (x - high.astype(jnp.float32)).astype(jnp.bfloat16)
+    return high, low
+
+
+def dot(a, b):
+    return jnp.dot(a, b, preferred_element_type=jnp.float32)
+
+
+def above(n):
+    return lax.broadcasted_iota(jnp.int32, (n, n), 1) > lax.broadcasted_iota(jnp.int32, (n, n), 0)
+
+
+def pack_block(part, o, value, low_half):
+    n = value.shape[0] // 2
+
+    def put(i, rows):
+        part[i // 2, i % 2 * n:(i % 2 + 1) * n, :] = rows
+
+    if o == 0:
+        mixed = jnp.where(above(n), value[:n, :n], value[n:, n:])
+        put(0, jnp.concatenate([mixed, value[:n, n:]], axis=1))
+    elif o == 4:
+        put(7, jnp.where(low_half, value[:n, :], value[:, n:].T))
+    else:
+        put(2 * o - 1, value[:n])
+        put(2 * o, value[n:])
+
+
+def unpack_diagonal(rows):
+    n = rows.shape[0]
+    mixed, corner = rows[:, :n], rows[:, n:]
+    upper = jnp.where(above(n), mixed, 0.0)
+    below = lax.broadcasted_iota(jnp.int32, (n, n), 1) < lax.broadcasted_iota(jnp.int32, (n, n), 0)
+    lower = jnp.where(below, mixed, 0.0)
+    return upper - upper.T, corner, -corner.T, lower - lower.T
+
+
+def term_kernel(ids, weight, diags, own, other, o0, o1, o2, o3, chosen, mre, mim, part, sem, out_sem, chosen_sem):
+    b, r, z = ids[0], ids[1], ids[2]
+    size = mre.shape[-1]
+    per_core = own.shape[1] // size
+    blocks = 2 * per_core
+    kept = mre.shape[0]
+    per_chip = own.shape[2] // size
+    groups = blocks // per_chip
+    j = z * per_chip + r
+    lanes = pl.ds(pl.multiple_of(r * size, size), size)
+    for o in range(kept):
+        block = lax.rem(j + o, blocks)
+        rows = pl.ds(pl.multiple_of(lax.rem(block, per_core) * size, size), size)
+        mine = lax.div(block, per_core) == r
+        for ref, cond in ((own, mine), (other, jnp.logical_not(mine))):
+            @pl.when(cond)
+            def _(ref=ref, o=o, rows=rows):
+                pltpu.make_async_copy(ref.at[0, rows, lanes], mre.at[o], sem.at[0, o]).start()
+                pltpu.make_async_copy(ref.at[1, rows, lanes], mim.at[o], sem.at[1, o]).start()
+
+    def piece(block, p):
+        slot = lax.rem(z - lax.div(block, per_chip) + groups, groups)
+        half = lax.rem(block, per_chip)
+        row = diags[slot, pl.ds(p, 1), :]
+        return jnp.where(half == 0, row[:, :size], row[:, size:])
+
+    factor = 2.0 * weight[0]
+    re_own, im_own = piece(j, 0), piece(j, 1)
+    low_half = j < blocks // 2
+    copies = []
+    for o in range(kept):
+        block = lax.rem(j + o, blocks)
+        re_rows = jnp.broadcast_to(piece(block, 0), (size, size)).T
+        im_rows = jnp.broadcast_to(piece(block, 1), (size, size)).T
+        pltpu.make_async_copy(own.at[0, pl.ds(0, size), pl.ds(0, size)], mre.at[o], sem.at[0, o]).wait()
+        pltpu.make_async_copy(own.at[0, pl.ds(0, size), pl.ds(0, size)], mim.at[o], sem.at[1, o]).wait()
+        kept_copies = [pltpu.make_async_copy(buf.at[o], chosen.at[p, o], chosen_sem.at[p, o]) for p, buf in enumerate((mre, mim))]
+        for copy in kept_copies:
+            copy.start()
+        copies += kept_copies
+        value = factor * (mre[o] * (re_rows - re_own) + mim[o] * (im_rows - im_own))
+        pack_block(part, o, value, low_half)
+    for k, out in enumerate((o0, o1, o2, o3)):
+        copy = pltpu.make_async_copy(part.at[jnp.bitwise_xor(b, k)], out, out_sem.at[k])
+        copy.start()
+        copies.append(copy)
+    for copy in copies:
+        copy.wait()
+
+
+def quarter_kernel(ids, own, other, out, half, buf, sem):
+    r, z, h = ids[1], ids[2], ids[4]
+    size = buf.shape[2]
+    per_core = own.shape[0] // size
+    blocks = 2 * per_core
+    per_chip = own.shape[1] // size
+    j = z * per_chip + r
+    lanes = pl.ds(pl.multiple_of(r * size, size), size)
+    for o in range(5):
+        block = lax.rem(j + o, blocks)
+        rows = pl.ds(pl.multiple_of(lax.rem(block, per_core) * size, size), size)
+        mine = lax.div(block, per_core) == r
+        for ref, cond in ((own, mine), (other, jnp.logical_not(mine))):
+            @pl.when(cond)
+            def _(ref=ref, rows=rows, o=o):
+                pltpu.make_async_copy(ref.at[rows, lanes], buf.at[o], sem.at[o]).start()
+    for o in range(5):
+        pltpu.make_async_copy(own.at[pl.ds(0, size), pl.ds(0, size)], buf.at[o], sem.at[o]).wait()
+        pack_block(out, o, buf[o], j < blocks // 2)
+    half[...] = jnp.where(h == 0, out[0:2], out[2:4])
+
+
+def group_copies(ids, ins, dst, sem, place):
+    r, z = ids[1], ids[2]
+    groups = len(ins) // 2
+    quarter = ins[0].shape[1]
+    out = []
+    for i, ref in enumerate(ins):
+        s, c = i % groups, i // groups
+        j = lax.rem(z - s + groups, groups) * 2 + (r if c == 0 else 1 - r)
+        for k in range(4):
+            rows = pl.ds(pl.multiple_of(place(s, k) * quarter, quarter), quarter)
+            out.append(pltpu.make_async_copy(ref.at[k], dst.at[j, rows], sem.at[i]))
+    return out
+
+
+def terms_place(ids):
+    return lambda s, k: jnp.bitwise_xor(ids[0], k)
+
+
+def shared_place(ids):
+    h = ids[4]
+    return lambda s, k: k if s == 0 else (2 * h + k if k < 2 else 2 * (1 - h) + k - 2)
+
+
+def solve_kernel(ids, prev_square, *refs):
+    groups = (len(refs) - 9) // 4
+    g_in, d_in = refs[:2 * groups], refs[2 * groups:4 * groups]
+    beta_out, exp_out, pg, pd, ahi, alo, hhi, hlo, sem = refs[4 * groups:]
+    own_block = ids[3]
+    order = ahi.shape[0]
+    blocks, _, size = pg.shape
+
+    g_copies = group_copies(ids, g_in, pg, sem.at[0], terms_place(ids))
+    d_copies = group_copies(ids, d_in, pd, sem.at[1], shared_place(ids))
+    for c in g_copies + d_copies:
+        c.start()
+    strip = size // 2
+
+    def fold(x):
+        return jnp.sum(x.reshape(-1, 8, size), axis=0)
+
+    quarter = g_in[0].shape[1]
+
+    def arrive(which, i):
+        for k in range(4):
+            at = pl.ds(k * quarter, quarter)
+            pltpu.make_async_copy(g_in[0].at[k], pg.at[0, at], sem.at[which, i]).wait()
+        core = lax.div(i, groups)
+        column = lax.rem(ids[2] - lax.rem(i, groups) + groups, groups) * 2
+        return column + jnp.where(core == 0, ids[1], 1 - ids[1])
+
+    def norm_body(i, acc):
+        jj = arrive(0, i)
+        for t in range(0, pg.shape[1], size):
+            v = pg[jj, t:t + size, :]
+            acc = acc + fold(v * v)
+        return acc
+
+    zero = jnp.zeros((8, size), jnp.float32)
+    beta = 2.0 * jnp.sum(lax.fori_loop(0, blocks, norm_body, zero)) / (1.0 + prev_square[0])
+    beta_out[...] = jnp.full(beta_out.shape, beta, jnp.float32)
+
+    def store(row, col, v):
+        high, low = split_bf16(v)
+        rows = pl.ds(pl.multiple_of(row, strip), v.shape[0])
+        cols = pl.ds(pl.multiple_of(col, strip), v.shape[1])
+        ahi[rows, cols] = high
+        alo[rows, cols] = low
+
+    def dir_body(i, acc):
+        jj = arrive(1, i)
+        base = jj * size
+        for t in range(8):
+            at = slice(t * strip, (t + 1) * strip)
+            v = beta * pd[jj, at, :] - pg[jj, at, :]
+            acc = acc + fold(v * v)
+            if t == 0:
+                first_q, second_q, third_q, fourth_q = unpack_diagonal(v)
+                store(base, base, first_q)
+                store(base, base + strip, second_q)
+                store(base + strip, base, third_q)
+                store(base + strip, base + strip, fourth_q)
+            elif t == 7:
+                low_half = jj < blocks // 2
+                v = jnp.where(low_half, v, -v)
+                high_block = jnp.where(low_half, jj + blocks // 2, jj) * size + jnp.where(low_half, 0, strip)
+                low_block = jnp.where(low_half, jj, jj - blocks // 2) * size
+                store(high_block, low_block, v)
+                store(low_block, high_block, -v.T)
+            else:
+                row = lax.rem(jj + (t + 1) // 2, blocks) * size + (t + 1) % 2 * strip
+                store(row, base, v)
+                store(base, row, -v.T)
+        return acc
+
+    dir_square = 2.0 * jnp.sum(lax.fori_loop(0, blocks, dir_body, zero))
+    scale = STEP_SCALE / jnp.sqrt(jnp.full((1, size), 1.0 + dir_square / order, jnp.float32))
+
+    tile = min(1024, order)
+    own_cols = pl.ds(pl.multiple_of(own_block * size, size), size)
+
+    def eye_rows(start, count):
+        rid = lax.broadcasted_iota(jnp.int32, (count, size), 0) + start
+        cid = lax.broadcasted_iota(jnp.int32, (count, size), 1) + own_block * size
+        return (rid == cid).astype(jnp.float32)
+
+    def first(i, carry):
+        start = pl.multiple_of(i * size, size)
+        rows = pl.ds(start, size)
+        a = ahi[rows, own_cols].astype(jnp.float32) + alo[rows, own_cols].astype(jnp.float32)
+        high, low = split_bf16(eye_rows(start, size) + a * (scale / TAYLOR))
+        hhi[0, rows, :] = high
+        hlo[0, rows, :] = low
+        return carry
+
+    lax.fori_loop(0, order // size, first, 0)
+
+    def step(counter, carry):
+        now = lax.rem(counter, 2)
+        divisor = (TAYLOR - 1 - counter).astype(jnp.float32)
+        inverse = scale / jnp.full((1, size), divisor, jnp.float32)
+        bh = hhi[now]
+        bl = hlo[now]
+
+        def rows_body(i, c):
+            start = pl.multiple_of(i * tile, tile)
+            rows = pl.ds(start, tile)
+            ah, al = ahi[rows, :], alo[rows, :]
+            value = eye_rows(start, tile) + (dot(ah, bh) + dot(ah, bl) + dot(al, bh)) * inverse
+
+            @pl.when(counter < TAYLOR - 2)
+            def _():
+                high, low = split_bf16(value)
+                hhi[1 - now, rows, :] = high
+                hlo[1 - now, rows, :] = low
+
+            @pl.when(counter == TAYLOR - 2)
+            def _():
+                exp_out[rows, :] = value
+
+            return c
+
+        return lax.fori_loop(0, order // tile, rows_body, carry)
+
+    lax.fori_loop(0, TAYLOR - 1, step, 0)
+
+
+def output_kernel(ids, beta, dprev, *refs):
+    g_in = refs[:-4]
+    grad_out, dir_out, pg, sem = refs[-4:]
+    r, z = ids[1], ids[2]
+    blocks, _, size = pg.shape
+    per_core = grad_out.shape[0] // size
+    per_chip = grad_out.shape[1] // size
+    for c in group_copies(ids, g_in, pg, sem, terms_place(ids)):
+        c.start()
+    for c in group_copies(ids, g_in, pg, sem, terms_place(ids)):
+        c.wait()
+
+    def out_body(t, carry):
+        i, jx = lax.div(t, per_chip), lax.rem(t, per_chip)
+        rb, cb = r * per_core + i, z * per_chip + jx
+        o = lax.rem(rb - cb + blocks, blocks)
+        rows = pl.ds(pl.multiple_of(i * size, size), size)
+        cols = pl.ds(pl.multiple_of(jx * size, size), size)
+
+        n = size // 2
+
+        @pl.when(o == 0)
+        def _():
+            first_q, second_q, third_q, fourth_q = unpack_diagonal(pg[cb, :n, :])
+            grad_out[rows, cols] = jnp.concatenate(
+                [jnp.concatenate([first_q, second_q], axis=1), jnp.concatenate([third_q, fourth_q], axis=1)], axis=0)
+
+        @pl.when((o > 0) & (o < 4))
+        def _():
+            grad_out[rows, cols] = pg[cb, pl.ds(pl.multiple_of(o * size - n, n), size), :]
+
+        @pl.when(o > 4)
+        def _():
+            grad_out[rows, cols] = -pg[rb, pl.ds(pl.multiple_of((blocks - o) * size - n, n), size), :].T
+
+        @pl.when((o == 4) & (rb > cb))
+        def _():
+            grad_out[rows, cols] = jnp.concatenate([pg[cb, 7 * n:, :], -pg[rb, 7 * n:, :]], axis=0)
+
+        @pl.when((o == 4) & (rb < cb))
+        def _():
+            grad_out[rows, cols] = jnp.concatenate([-pg[rb, 7 * n:, :], pg[cb, 7 * n:, :]], axis=0).T
+
+        dir_out[rows, cols] = beta[0, 0] * dprev[rows, cols] - grad_out[rows, cols]
+        return carry
+
+    lax.fori_loop(0, per_core * per_chip, out_body, 0)
+
+
+def trial_kernel(ids, exp_lo, exp_hi, m0, m1, m2, m3, out, ehi, elo, mbuf, sem):
+    r, z = ids[1], ids[2]
+    half = exp_lo.shape[0]
+    width = exp_lo.shape[1]
+    size = m0.shape[2]
+    blocks = 2 * half // size
+    work = [(i, p) for i in range(4) for p in range(2)]
+    sources = (m0, m1, m2, m3)
+
+    def copy(n):
+        i, p = work[n]
+        return pltpu.make_async_copy(sources[i].at[p], mbuf.at[n % 3], sem.at[n % 3])
+
+    copy(0).start()
+    copy(1).start()
+    for h, ref in enumerate((exp_lo, exp_hi)):
+        high, low = split_bf16(ref[...])
+        ehi[h * half:(h + 1) * half, :] = high
+        elo[h * half:(h + 1) * half, :] = low
+    totals = [jnp.zeros((8, width), jnp.float32) for _ in range(2)]
+    for n, (i, p) in enumerate(work):
+        if n + 2 < len(work):
+            copy(n + 2).start()
+        copy(n).wait()
+        chip = z if i < 2 else jnp.bitwise_xor(z, 1)
+        j = chip * 2 + (r if i % 2 == 0 else 1 - r)
+        own = pl.ds(pl.multiple_of(j * size, size), size)
+        bh, bl = ehi[own, :], elo[own, :]
+        for o in range(5):
+            high, low = split_bf16(mbuf[n % 3, o])
+            z_o = dot(high, bh) + dot(high, bl) + dot(low, bh)
+            at = pl.ds(pl.multiple_of(lax.rem(j + o, blocks) * size, size), size)
+            e = ehi[at, :].astype(jnp.float32) + elo[at, :].astype(jnp.float32)
+            term = jnp.sum((e * z_o).reshape(-1, 8, width), axis=0)
+            totals[p] = totals[p] + (term if o in (0, 4) else 2.0 * term)
+    out[...] = jnp.concatenate([jnp.sum(t, axis=0, keepdims=True) for t in totals], axis=0)
 
 
 def lookup_weights(bvec_index, weight_table):
@@ -19,6 +365,154 @@
     return jnp.sum(
         jnp.where(table_slots[None, :] == bvec_index[:, None], weight_table[None, :], 0.0), axis=1
     )
+
+
+def paired(counts, m_matrices, bvec_index, weight_table, grad_prev, dir_prev):
+    n_b, n_row, n_col = counts
+    local_rows, local_cols = m_matrices.shape[2], m_matrices.shape[3]
+    order = local_rows * n_row
+    size = local_cols // n_row
+    b, r, z = (lax.axis_index(a).astype(jnp.int32) for a in AXES)
+    parity = jnp.bitwise_xor(b, b >> 1) & 1
+    own_block = (z % 2) * 4 + parity * 2 + r
+    ids = jnp.stack([b, r, z, own_block, parity]).astype(jnp.int32)
+
+    def send(x, where):
+        pairs = []
+        for bb in range(n_b):
+            for rr in range(n_row):
+                for zz in range(n_col):
+                    tb, tr, tz = where(bb, rr, zz)
+                    pairs.append(((bb * n_row + rr) * n_col + zz, (tb * n_row + tr) * n_col + tz))
+        return lax.ppermute(x, AXES, pairs)
+
+    core = lambda bb, rr, zz: (bb, 1 - rr, zz)
+    over_b = lambda k: (lambda bb, rr, zz: (bb ^ k, rr, zz))
+    over_z = lambda s: (lambda bb, rr, zz: (bb, rr, (zz + s) % n_col))
+    flip_z = lambda k: (lambda bb, rr, zz: (bb, rr, zz ^ k))
+
+    weight_all = lookup_weights(bvec_index, weight_table)
+    weight_own = lax.dynamic_slice_in_dim(weight_all, b, 1)
+    m = m_matrices[0]
+
+    d_oth = send(dir_prev, core)
+    start = (z % 2) * local_cols
+    square = lax.dynamic_slice_in_dim(m, start, local_cols, 1)
+    holder = (z // 2 == r)
+    eye = jnp.eye(local_cols, dtype=jnp.bool_)
+    own_diag = jnp.sum(jnp.where(eye & holder, square, 0.0), axis=1)
+    prev_part = jnp.sum(grad_prev * grad_prev)
+    packet = jnp.concatenate([own_diag, jnp.full((1, local_cols), prev_part)], axis=0)
+    packet = packet + send(packet, core)
+    m_oth = send(m, core)
+    diags = jnp.stack([packet] + [send(packet, over_z(s)) for s in range(1, n_col)])
+    prev_square = jnp.sum(diags[:, 2, :1], axis=0)
+    spread_own = weight_own[0] * jnp.sum(1.0 - diags[:, 0] ** 2 - diags[:, 1] ** 2) / order
+
+    quarter = jax.ShapeDtypeStruct((size, size), jnp.float32)
+    d_own, d_half = pl.pallas_call(
+        quarter_kernel, out_shape=[jax.ShapeDtypeStruct((n, size, size), jnp.float32) for n in (4, 2)],
+        in_specs=[SMEM, ANY, ANY], out_specs=[VMEM] * 2,
+        scratch_shapes=[pltpu.VMEM((5, size, size), jnp.float32), pltpu.SemaphoreType.DMA((5,))],
+        cost_estimate=pl.CostEstimate(flops=0, bytes_accessed=1 << 20, transcendentals=0),
+    )(ids, dir_prev, d_oth)
+    d_by_z = {s: send(d_half, over_z(s)) for s in (1, 3, 2)}
+    terms = pl.pallas_call(
+        term_kernel, out_shape=[quarter] * 4 + [jax.ShapeDtypeStruct((2, 5, size, size), jnp.float32)],
+        in_specs=[SMEM, SMEM, VMEM, ANY, ANY], out_specs=[ANY] * 5,
+        scratch_shapes=[pltpu.VMEM((5, size, size), jnp.float32), pltpu.VMEM((5, size, size), jnp.float32),
+                        pltpu.VMEM((4, size, size), jnp.float32),
+                        pltpu.SemaphoreType.DMA((2, 5)), pltpu.SemaphoreType.DMA((4,)),
+                        pltpu.SemaphoreType.DMA((2, 5))],
+        cost_estimate=pl.CostEstimate(flops=10**9, bytes_accessed=1 << 22, transcendentals=0),
+    )(ids, weight_own, diags, m, m_oth)
+    parts = [send(terms[k], over_b(k)) for k in range(1, n_b)]
+    g_quarter = ((terms[0] + parts[0]) + parts[1]) + parts[2]
+
+    d_groups = [d_own] + [
+        jnp.concatenate([d_by_z[s], send(d_by_z[s][:1], over_b(1)), send(d_by_z[s][1:], over_b(2))])
+        for s in range(1, n_col)
+    ]
+    d_groups = d_groups + [send(g, core) for g in d_groups]
+    g_by_z = {0: g_quarter}
+    for s in (1, 3, 2):
+        g_by_z[s] = send(g_quarter, over_z(s))
+    g_groups = []
+    for s in range(n_col):
+        piece = g_by_z[s]
+        over_x = send(piece, over_b(1))
+        over_y = send(piece, over_b(2))
+        if s in (1, 2):
+            across = send(over_y, over_b(1))
+        else:
+            across = send(over_x, over_b(2))
+        g_groups.append(jnp.stack([piece, over_x, over_y, across]))
+    g_groups = g_groups + [send(g, core) for g in g_groups]
+    chosen_z = send(terms[4], flip_z(1))
+
+    f32 = jnp.float32
+    held = pltpu.VMEM((2 * n_col, 4 * size, size), f32)
+    beta, exp_own = pl.pallas_call(
+        solve_kernel,
+        out_shape=[jax.ShapeDtypeStruct((8, 128), f32), jax.ShapeDtypeStruct((order, size), f32)],
+        in_specs=[SMEM, SMEM] + [ANY] * (4 * n_col), out_specs=[VMEM] * 2,
+        scratch_shapes=[held, held,
+                        pltpu.VMEM((order, order), jnp.bfloat16), pltpu.VMEM((order, order), jnp.bfloat16),
+                        pltpu.VMEM((2, order, size), jnp.bfloat16), pltpu.VMEM((2, order, size), jnp.bfloat16),
+                        pltpu.SemaphoreType.DMA((2, 2 * n_col))],
+        compiler_params=pltpu.CompilerParams(vmem_limit_bytes=VMEM_LIMIT),
+        cost_estimate=pl.CostEstimate(flops=7 * 3 * 2 * order * order * size, bytes_accessed=1 << 25, transcendentals=0),
+    )(ids, prev_square, *g_groups, *d_groups)
+    outputs = pl.pallas_call(
+        output_kernel, out_shape=[jax.ShapeDtypeStruct((local_rows, local_cols), f32)] * 2,
+        in_specs=[SMEM, SMEM, VMEM] + [ANY] * (2 * n_col), out_specs=[VMEM] * 2,
+        scratch_shapes=[held, pltpu.SemaphoreType.DMA((2 * n_col,))],
+        compiler_params=pltpu.CompilerParams(vmem_limit_bytes=VMEM_LIMIT),
+        cost_estimate=pl.CostEstimate(flops=10**9, bytes_accessed=1 << 24, transcendentals=0),
+    )
+    grad, direction = outputs(ids, beta[:1], dir_prev, *g_groups)
+
+    exp_own, chosen_z = lax.optimization_barrier((exp_own, chosen_z))
+    chosen_set = (terms[4], send(terms[4], core), chosen_z, send(chosen_z, core))
+    top, bottom = exp_own[:order // 2], exp_own[order // 2:]
+    top_in = send(top, over_b(1))
+    bottom_in = send(bottom, over_b(2))
+
+    def trial(lo, hi):
+        return pl.pallas_call(
+            trial_kernel, out_shape=jax.ShapeDtypeStruct((2, size), f32),
+            in_specs=[SMEM, VMEM, VMEM] + [ANY] * 4, out_specs=VMEM,
+            scratch_shapes=[pltpu.VMEM((order, size), jnp.bfloat16), pltpu.VMEM((order, size), jnp.bfloat16),
+                            pltpu.VMEM((3, 5, size, size), f32), pltpu.SemaphoreType.DMA((3,))],
+            compiler_params=pltpu.CompilerParams(vmem_limit_bytes=VMEM_LIMIT // 2),
+            cost_estimate=pl.CostEstimate(flops=3 * 2 * order * order * size, bytes_accessed=1 << 24, transcendentals=0),
+        )(ids, lo, hi, *chosen_set)
+
+    t_own = trial(top, bottom)
+    top_in, bottom_in, grad, direction = lax.optimization_barrier((top_in, bottom_in, grad, direction))
+    t_in = trial(top_in, bottom_in)
+
+    def ordered(bit, mine, theirs):
+        return jnp.where(bit == 0, jnp.stack([mine, theirs]), jnp.stack([theirs, mine]))
+
+    t = ordered(parity, t_own, t_in)
+    t = t + send(t, flip_z(2))
+    t = ordered(z % 2, t, send(t, flip_z(1)))
+    t = ordered(r, t, send(t, core))
+    t = jnp.transpose(t, (3, 1, 2, 0, 4)).reshape(2, order)
+    t = jnp.concatenate([t, jnp.full((1, order), spread_own)], axis=0)
+    t = ordered(b & 1, t, send(t, over_b(1)))
+    t = ordered(b >> 1, t, send(t, over_b(2))).reshape(n_b, 3, order)
+    trial_diag = t[:, :2]
+    spread = jnp.sum(t[:, 2, 0])
+    trial_spread = (
+        jnp.sum(weight_all[:, None] * (1.0 - trial_diag[:, 0] ** 2 - trial_diag[:, 1] ** 2)) / order
+    )
+    return (spread, trial_spread, grad, direction, trial_diag)
+
+
+def product(left, right):
+    return jnp.dot(left, right, precision=HIGHEST, preferred_element_type=jnp.float32)
 
 
 def shards(m_matrices, bvec_index, weight_table, grad_prev, dir_prev):
@@ -96,8 +590,14 @@
 
 def solution(mesh):
     placed = (P("bvec", None, "row", "col"), P(), P(), P("row", "col"), P("row", "col"))
+    counts = tuple(mesh.shape[a] for a in AXES)
+    special = counts == (4, 2, 4)
+
+    def named(*args):
+        return paired(counts, *args)
+
     return jax.shard_map(
-        shards,
+        named if special else shards,
         mesh=mesh,
         in_specs=placed,
         out_specs=(P(), P(), P("row", "col"), P("row", "col"), P()),

time: 1770 us -> 283 us (0.16)
  waiting for transfers between devices: 1430 us -> 111 us
  matrix products: 178 us -> 0 us
  Pallas kernels: 0 us -> 97.4 us
  blocking collectives: 91 us -> 0 us
  starting transfers between devices: 0.41 us -> 50.9 us
  between operations: 22.9 us -> 4.29 us
    all_gather x10 -> x0, waiting for transfers between devices: 1360 us -> none  [the longest x7 1050 us: horner_step(): folded = accumulate(lax.all_gather(current, 'col', axis=1, tiled=True))]
    dot_general x8 -> x0, matrix products: 178 us -> none  [product(): jnp.dot(left, right, precision=HIGHEST, preferred_element_type=jnp.float32)]
    ppermute x0 -> x51, waiting for transfers between devices: none -> 111 us  [send(): return lax.ppermute(x, AXES, pairs)]
    pallas_call x0 -> x6, Pallas kernels: none -> 97.4 us  [the longest x1 63.4 us: paired(): pl.pallas_call(solve_kernel, out_shape=[jax.ShapeDtypeStruct((8, 128), f3...]
    psum x1 -> x0, waiting for transfers between devices: 65.1 us -> none  [shards(): gradient = lax.psum(grad_part, 'bvec')]
    ppermute x0 -> x51, starting transfers between devices: none -> 50.9 us  [send(): return lax.ppermute(x, AXES, pairs)]
    psum x3 -> x0, blocking collectives: 46.1 us -> none  [the longest x1 39.4 us: shards(): lax.psum((spread_term, grad_square, prev_square, cross_term, dir_square),...]
    all_gather x3 -> x0, blocking collectives: 44.8 us -> none  [the longest x1 21.9 us: shards(): trial_group = lax.all_gather(trial_share, 'col', axis=2, tiled=True)]
  transfers between devices with their start and end apart: 11 -> 51, of which waited for: 11 -> 26; matrix products, arithmetic and copies ran while one was open for 0% -> 5% of each run, Pallas kernels for 0% -> 28%
where the time goes in v1:
time: 283 us
  waiting for transfers between devices  111 us (39%)
  Pallas kernels  97.4 us (34%)
  starting transfers between devices  50.9 us (18%)
  local copies, waits for them, and re-layouts  10 us (4%)
  other arithmetic  9.32 us (3%)
  between operations  4.29 us (2%)
    ppermute x51, waiting for transfers between devices, send(): return lax.ppermute(x, AXES, pairs)  111 us
    pallas_call x1, Pallas kernels, paired(): pl.pallas_call(solve_kernel, out_shape=[jax.ShapeDtypeStruct((8, 128), f3...  63.4 us
    ppermute x51, starting transfers between devices, send(): return lax.ppermute(x, AXES, pairs)  50.9 us
    pallas_call x2, Pallas kernels, trial(): pl.pallas_call(trial_kernel, out_shape=jax.ShapeDtypeStruct((2, size), f3...  18 us
    pallas_call x1, Pallas kernels, paired(): grad, direction = outputs(ids, beta[:1], dir_prev, *g_groups)  8.11 us
  transfers between devices with their start and end apart: 51, of which 26 were waited for; matrix products, arithmetic and copies ran while one was open for 5% of the time, Pallas kernels for 28%

profile of v1, /device:TPU:0, one launch (start us, length us, event | category | flops | bytes accessed | tf_op | source)
XLA Modules:
  0.0 282.8 jit_solution(1896341131236725713)
XLA Ops:
  4.8 6.4 %collective-permute-done.27.other = f32[1024,512]{1,0:T(8,128)S(1)} collective-permute-done((f32[1024,512]{1,0:T(8,128)}, f32[1024,512]{1,0:T(8,128)S(1)}, u32[]{:S(2)}, u32[]{:S(2)}) %collective-permute-start.27) | collective-permute-done | bytes 2097184 | tf_op jit(solution)/shard_map/ppermute | solution.py:387
  12.5 3.2 %shard_map.93 = (f32[4,256,256]{2,1,0:T(8,128)}, f32[2,256,256]{2,1,0:T(8,128)}) custom-call(s32[5]{0:T(128)} %stack.180.ids, f32[1024,512]{1,0:T(8,128)} %dprev.1, f32[1024,512]{1,0:T(8,128)} %copy-done.5), custom_call_target="tpu_custom_call" | custom-call | bytes 1048576 | tf_op jit(solution)/shard_map/pallas_call | solution.py:413
  15.8 5.0 %collective-permute-start.34 = (f32[2,256,256]{2,1,0:T(8,128)}, f32[2,256,256]{2,1,0:T(8,128)S(1)}, u32[]{:S(2)}, u32[]{:S(2)}) collective-permute-start(f32[2,256,256]{2,1,0:T(8,128)} %get-tuple-element.27), channel_id=1, source_target_pairs={{0,3},{1,0},{2,1},{3,2},{4,7},{5,4},{6,5},{7,6},{8,11},{9,8},{10,9... | collective-permute-start | bytes 1572872 | tf_op jit(solution)/shard_map/ppermute | solution.py:387
  27.3 5.7 %collective-permute-done.3 = f32[3,512]{1,0:T(4,128)S(1)} collective-permute-done((f32[3,512]{1,0:T(4,128)S(1)}, f32[3,512]{1,0:T(4,128)S(1)}, u32[]{:S(2)}, u32[]{:S(2)}) %collective-permute-start.3) | collective-permute-done | bytes 6176 | tf_op jit(solution)/shard_map/ppermute | solution.py:387
  35.8 3.5 %collective-permute-start.28 = (f32[2,256,256]{2,1,0:T(8,128)S(1)}, f32[2,256,256]{2,1,0:T(8,128)S(1)}, u32[]{:S(2)}, u32[]{:S(2)}) collective-permute-start(f32[2,256,256]{2,1,0:T(8,128)S(1)} %copy-done.20), channel_id=1, source_target_pairs={{0,1},{1,2},{2,3},{3,0},{4,5},{5,6},{6,7},{7,4},{8,9},{9,10},{10,1... | collective-permute-start | bytes 1572872 | tf_op jit(solution)/shard_map/ppermute | solution.py:387
  40.9 4.7 %shard_map.92 = (f32[256,256]{1,0:T(8,128)}, f32[256,256]{1,0:T(8,128)}, f32[256,256]{1,0:T(8,128)}, f32[256,256]{1,0:T(8,128)}, f32[2,5,256,256]{3,2,1,0:T(8,128)}) custom-call(s32[5]{0:T(128)} %stack.180.ids, f32[1]{0:T(128)} %dynamic_slice.10.weight, f32[4,3,512]{2,1,0:T(4,128)} %pad_maximum_fusion.4.diags, f32[2,1024,512]{2,1,0:T(8,128)} %bitcast.64, ...), custom_call_target="tpu_custom_call" | custom-call | flops 1000000000 | bytes 4194304 | tf_op jit(solution)/shard_map/pallas_call | solution.py:420
  47.7 21.6 %collective-permute-done.31 = f32[2,256,256]{2,1,0:T(8,128)S(1)} collective-permute-done((f32[2,256,256]{2,1,0:T(8,128)S(1)}, f32[2,256,256]{2,1,0:T(8,128)S(1)}, u32[]{:S(2)}, u32[]{:S(2)}) %collective-permute-start.31) | collective-permute-done | bytes 524320 | tf_op jit(solution)/shard_map/ppermute | solution.py:387
  74.5 5.1 %collective-permute-done.7 = f32[256,256]{1,0:T(8,128)S(1)} collective-permute-done((f32[256,256]{1,0:T(8,128)}, f32[256,256]{1,0:T(8,128)S(1)}, u32[]{:S(2)}, u32[]{:S(2)}) %collective-permute-start.7) | collective-permute-done | bytes 262176 | tf_op jit(solution)/shard_map/ppermute | solution.py:387
  85.2 5.6 %collective-permute-done.32 = f32[1,256,256]{2,1,0:T(8,128)S(1)} collective-permute-done((f32[1,256,256]{2,1,0:T(8,128)S(1)}, f32[1,256,256]{2,1,0:T(8,128)S(1)}, u32[]{:S(2)}, u32[]{:S(2)}) %collective-permute-start.32) | collective-permute-done | bytes 262176 | tf_op jit(solution)/shard_map/ppermute | solution.py:387
  95.9 8.7 %collective-permute-done.15 = f32[256,256]{1,0:T(8,128)S(1)} collective-permute-done((f32[256,256]{1,0:T(8,128)S(1)}, f32[256,256]{1,0:T(8,128)S(1)}, u32[]{:S(2)}, u32[]{:S(2)}) %collective-permute-start.15) | collective-permute-done | bytes 262176 | tf_op jit(solution)/shard_map/ppermute | solution.py:387
  109.3 3.2 %collective-permute-done.20 = f32[256,256]{1,0:T(8,128)S(1)} collective-permute-done((f32[256,256]{1,0:T(8,128)S(1)}, f32[256,256]{1,0:T(8,128)S(1)}, u32[]{:S(2)}, u32[]{:S(2)}) %collective-permute-start.20) | collective-permute-done | bytes 262176 | tf_op jit(solution)/shard_map/ppermute | solution.py:387
  115.8 4.3 %collective-permute-done.13 = f32[256,256]{1,0:T(8,128)S(1)} collective-permute-done((f32[256,256]{1,0:T(8,128)S(1)}, f32[256,256]{1,0:T(8,128)S(1)}, u32[]{:S(2)}, u32[]{:S(2)}) %collective-permute-start.13) | collective-permute-done | bytes 262176 | tf_op jit(solution)/shard_map/ppermute | solution.py:387
  121.1 3.9 %collective-permute-done.10 = f32[256,256]{1,0:T(8,128)S(1)} collective-permute-done((f32[256,256]{1,0:T(8,128)S(1)}, f32[256,256]{1,0:T(8,128)S(1)}, u32[]{:S(2)}, u32[]{:S(2)}) %collective-permute-start.10) | collective-permute-done | bytes 262176 | tf_op jit(solution)/shard_map/ppermute | solution.py:387
  128.3 5.8 %collective-permute-done.18 = f32[256,256]{1,0:T(8,128)S(1)} collective-permute-done((f32[256,256]{1,0:T(8,128)S(1)}, f32[256,256]{1,0:T(8,128)S(1)}, u32[]{:S(2)}, u32[]{:S(2)}) %collective-permute-start.18) | collective-permute-done | bytes 262176 | tf_op jit(solution)/shard_map/ppermute | solution.py:387
  134.7 3.4 %collective-permute-done.12 = f32[256,256]{1,0:T(8,128)S(1)} collective-permute-done((f32[256,256]{1,0:T(8,128)S(1)}, f32[256,256]{1,0:T(8,128)S(1)}, u32[]{:S(2)}, u32[]{:S(2)}) %collective-permute-start.12) | collective-permute-done | bytes 262176 | tf_op jit(solution)/shard_map/ppermute | solution.py:387
  138.1 2.8 collective-permute-done.14
  143.6 4.0 %collective-permute-start.41 = (f32[2,5,256,256]{3,2,1,0:T(8,128)}, f32[2,5,256,256]{3,2,1,0:T(8,128)}, u32[]{:S(2)}, u32[]{:S(2)}) collective-permute-start(f32[2,5,256,256]{3,2,1,0:T(8,128)} %get-tuple-element.29.m0), channel_id=1, source_target_pairs={{0,1},{1,0},{2,3},{3,2},{4,5},{5,4},{6,7},{7,6},{8,9},{9,8},{10,11... | collective-permute-start | bytes 7864328 | tf_op jit(solution)/shard_map/ppermute | solution.py:387
  149.9 63.4 %shard_map.94 = (f32[8,128]{1,0:T(8,128)}, f32[2048,256]{1,0:T(8,128)}) custom-call(s32[5]{0:T(128)} %stack.180.ids, f32[1]{0:T(128)} %bitcast.10.prev_square, f32[4,256,256]{2,1,0:T(8,128)} %copy-done.1, f32[4,256,256]{2,1,0:T(8,128)} %copy-done.4, f32[4,256,256]{2,1,0:T(8,128)} %copy-done.3, f32[4,256,256]{2,1,0:T(8,128)} %copy-done.2, ...), custom_call_target="tpu_custom_call" | custom-call | flops 45097156608 | bytes 33554432 | tf_op jit(solution)/shard_map/pallas_call | solution.py:455
  219.1 8.1 %shard_map.96 = (f32[1024,512]{1,0:T(8,128)}, f32[1024,512]{1,0:T(8,128)}) custom-call(s32[5]{0:T(128)} %stack.180.ids, f32[1,128]{1,0:T(1,128)} %slice.59.beta, f32[1024,512]{1,0:T(8,128)} %dprev.1, f32[4,256,256]{2,1,0:T(8,128)} %copy-done.1, f32[4,256,256]{2,1,0:T(8,128)} %copy-done.4, f32[4,256,256]{2,1,0:T(8,128)} %copy-done.3, ...), custom_call_target="tpu_custom_call" | custom-call | flops 1000000000 | bytes 16777216 | tf_op jit(solution)/shard_map/pallas_call | solution.py:473
  227.2 14.5 %collective-permute-done.45.exp_hi = f32[1024,256]{1,0:T(8,128)} collective-permute-done((f32[1024,256]{1,0:T(8,128)S(1)}, f32[1024,256]{1,0:T(8,128)}, u32[]{:S(2)}, u32[]{:S(2)}) %collective-permute-start.45) | collective-permute-done | bytes 1048608 | tf_op jit(solution)/shard_map/ppermute | solution.py:387
  242.0 8.9 %shard_map.95 = f32[2,256]{1,0:T(2,128)S(1)} custom-call(s32[5]{0:T(128)S(1)} %copy-done, f32[1024,256]{1,0:T(8,128)} %get-tuple-element.40.exp_lo, f32[1024,256]{1,0:T(8,128)S(1)} %get-tuple-element.39.exp_hi, f32[2,5,256,256]{3,2,1,0:T(8,128)} %get-tuple-element.29.m0, f32[2,5,256,256]{3,2,1,0:T(8,128)} %collective-permute-done.42.m1, ...), custom_call_target="tpu_custom_call" | custom-call | flops 6442450944 | bytes 16777216 | tf_op jit(solution)/shard_map/pallas_call | solution.py:482
  250.8 9.2 %shard_map.97 = f32[2,256]{1,0:T(2,128)S(1)} custom-call(s32[5]{0:T(128)S(1)} %copy-done, f32[1024,256]{1,0:T(8,128)} %collective-permute-done.44.exp_lo, f32[1024,256]{1,0:T(8,128)} %collective-permute-done.45.exp_hi, f32[2,5,256,256]{3,2,1,0:T(8,128)} %get-tuple-element.29.m0, f32[2,5,256,256]{3,2,1,0:T(8,128)} %collective-permute-done.42.m1, ...), custom_call_target="tpu_custom_call" | custom-call | flops 6442450944 | bytes 16777216 | tf_op jit(solution)/shard_map/pallas_call | solution.py:482
  260.0 3.0 %collective-permute-start.46 = (f32[2,2,256]{2,1,0:T(2,128)S(1)}, f32[2,2,256]{2,1,0:T(2,128)S(1)}, u32[]{:S(2)}, u32[]{:S(2)}) collective-permute-start(f32[2,2,256]{2,1,0:T(2,128)S(1)} %maximum_select_fusion.6), channel_id=1, source_target_pairs={{0,2},{1,3},{2,0},{3,1},{4,6},{5,7},{6,4},{7,5},{8,10},{9,11},{10,... | collective-permute-start | bytes 12296 | tf_op jit(solution)/shard_map/ppermute | solution.py:387
  265.0 2.8 collective-permute-start.47
  (177 shorter events, 71.9 us)
Async XLA Ops:
  0.6 40.3 %collective-permute-start.4 = (f32[2,1024,512]{2,1,0:T(8,128)}, f32[2,1024,512]{2,1,0:T(8,128)}, u32[]{:S(2)}, u32[]{:S(2)}) collective-permute-start(f32[2,1024,512]{2,1,0:T(8,128)} %bitcast.63), channel_id=1, source_target_pairs={{0,4},{1,5},{2,6},{3,7},{4,0},{5,1},{6,2},{7,3},{8,12},{9,13},{10,... | collective-permute-start | bytes 12582920 | tf_op jit(solution)/shard_map/ppermute | solution.py:387
  15.8 23.5 %collective-permute-start.34 = (f32[2,256,256]{2,1,0:T(8,128)}, f32[2,256,256]{2,1,0:T(8,128)S(1)}, u32[]{:S(2)}, u32[]{:S(2)}) collective-permute-start(f32[2,256,256]{2,1,0:T(8,128)} %get-tuple-element.27), channel_id=1, source_target_pairs={{0,3},{1,0},{2,1},{3,2},{4,7},{5,4},{6,5},{7,6},{8,11},{9,8},{10,9... | collective-permute-start | bytes 1572872 | tf_op jit(solution)/shard_map/ppermute | solution.py:387
  33.0 36.3 %collective-permute-start.31 = (f32[2,256,256]{2,1,0:T(8,128)S(1)}, f32[2,256,256]{2,1,0:T(8,128)S(1)}, u32[]{:S(2)}, u32[]{:S(2)}) collective-permute-start(f32[2,256,256]{2,1,0:T(8,128)S(1)} %copy-done.20), channel_id=1, source_target_pairs={{0,2},{1,3},{2,0},{3,1},{4,6},{5,7},{6,4},{7,5},{8,10},{9,11},{10,... | collective-permute-start | bytes 1572872 | tf_op jit(solution)/shard_map/ppermute | solution.py:387
  35.8 35.9 %collective-permute-start.28 = (f32[2,256,256]{2,1,0:T(8,128)S(1)}, f32[2,256,256]{2,1,0:T(8,128)S(1)}, u32[]{:S(2)}, u32[]{:S(2)}) collective-permute-start(f32[2,256,256]{2,1,0:T(8,128)S(1)} %copy-done.20), channel_id=1, source_target_pairs={{0,1},{1,2},{2,3},{3,0},{4,5},{5,6},{6,7},{7,4},{8,9},{9,10},{10,1... | collective-permute-start | bytes 1572872 | tf_op jit(solution)/shard_map/ppermute | solution.py:387
  39.3 41.8 %collective-permute-start.36 = (f32[1,256,256]{2,1,0:T(8,128)S(1)}, f32[1,256,256]{2,1,0:T(8,128)S(1)}, u32[]{:S(2)}, u32[]{:S(2)}) collective-permute-start(f32[1,256,256]{2,1,0:T(8,128)S(1)} %get-tuple-element.41), channel_id=1, source_target_pairs={{0,16},{1,17},{2,18},{3,19},{4,20},{5,21},{6,22},{7,23},{8,24},{9,... | collective-permute-start | bytes 786440 | tf_op jit(solution)/shard_map/ppermute | solution.py:387
  45.6 26.8 %collective-permute-start.5 = (f32[256,256]{1,0:T(8,128)}, f32[256,256]{1,0:T(8,128)S(1)}, u32[]{:S(2)}, u32[]{:S(2)}) collective-permute-start(f32[256,256]{1,0:T(8,128)} %get-tuple-element.23), channel_id=1, source_target_pairs={{0,8},{1,9},{2,10},{3,11},{4,12},{5,13},{6,14},{7,15},{8,0},{9,1},... | collective-permute-start | bytes 786440 | tf_op jit(solution)/shard_map/ppermute | solution.py:387
  47.2 25.8 %collective-permute-start.6 = (f32[256,256]{1,0:T(8,128)}, f32[256,256]{1,0:T(8,128)S(1)}, u32[]{:S(2)}, u32[]{:S(2)}) collective-permute-start(f32[256,256]{1,0:T(8,128)} %get-tuple-element.24), channel_id=1, source_target_pairs={{0,16},{1,17},{2,18},{3,19},{4,20},{5,21},{6,22},{7,23},{8,24},{9,... | collective-permute-start | bytes 786440 | tf_op jit(solution)/shard_map/ppermute | solution.py:387
  71.7 13.5 %collective-permute-start.35 = (f32[1,256,256]{2,1,0:T(8,128)S(1)}, f32[1,256,256]{2,1,0:T(8,128)S(1)}, u32[]{:S(2)}, u32[]{:S(2)}) collective-permute-start(f32[1,256,256]{2,1,0:T(8,128)S(1)} %get-tuple-element.42), channel_id=1, source_target_pairs={{0,8},{1,9},{2,10},{3,11},{4,12},{5,13},{6,14},{7,15},{8,0},{9,1},... | collective-permute-start | bytes 786440 | tf_op jit(solution)/shard_map/ppermute | solution.py:387
  73.0 17.9 %collective-permute-start.32 = (f32[1,256,256]{2,1,0:T(8,128)S(1)}, f32[1,256,256]{2,1,0:T(8,128)S(1)}, u32[]{:S(2)}, u32[]{:S(2)}) collective-permute-start(f32[1,256,256]{2,1,0:T(8,128)S(1)} %get-tuple-element.44), channel_id=1, source_target_pairs={{0,8},{1,9},{2,10},{3,11},{4,12},{5,13},{6,14},{7,15},{8,0},{9,1},... | collective-permute-start | bytes 786440 | tf_op jit(solution)/shard_map/ppermute | solution.py:387
  85.2 19.4 %collective-permute-start.15 = (f32[256,256]{1,0:T(8,128)S(1)}, f32[256,256]{1,0:T(8,128)S(1)}, u32[]{:S(2)}, u32[]{:S(2)}) collective-permute-start(f32[256,256]{1,0:T(8,128)S(1)} %add_add_fusion), channel_id=1, source_target_pairs={{0,2},{1,3},{2,0},{3,1},{4,6},{5,7},{6,4},{7,5},{8,10},{9,11},{10,... | collective-permute-start | bytes 786440 | tf_op jit(solution)/shard_map/ppermute | solution.py:387
  90.8 15.2 %collective-permute-start.11 = (f32[256,256]{1,0:T(8,128)S(1)}, f32[256,256]{1,0:T(8,128)S(1)}, u32[]{:S(2)}, u32[]{:S(2)}) collective-permute-start(f32[256,256]{1,0:T(8,128)S(1)} %add_add_fusion), channel_id=1, source_target_pairs={{0,1},{1,2},{2,3},{3,0},{4,5},{5,6},{6,7},{7,4},{8,9},{9,10},{10,1... | collective-permute-start | bytes 786440 | tf_op jit(solution)/shard_map/ppermute | solution.py:387
  90.8 15.7 %collective-permute-start.9 = (f32[256,256]{1,0:T(8,128)S(1)}, f32[256,256]{1,0:T(8,128)S(1)}, u32[]{:S(2)}, u32[]{:S(2)}) collective-permute-start(f32[256,256]{1,0:T(8,128)S(1)} %add_add_fusion), channel_id=1, source_target_pairs={{0,16},{1,17},{2,18},{3,19},{4,20},{5,21},{6,22},{7,23},{8,24},{9,... | collective-permute-start | bytes 786440 | tf_op jit(solution)/shard_map/ppermute | solution.py:387
  93.9 13.2 %collective-permute-start.8 = (f32[256,256]{1,0:T(8,128)S(1)}, f32[256,256]{1,0:T(8,128)S(1)}, u32[]{:S(2)}, u32[]{:S(2)}) collective-permute-start(f32[256,256]{1,0:T(8,128)S(1)} %add_add_fusion), channel_id=1, source_target_pairs={{0,8},{1,9},{2,10},{3,11},{4,12},{5,13},{6,14},{7,15},{8,0},{9,1},... | collective-permute-start | bytes 786440 | tf_op jit(solution)/shard_map/ppermute | solution.py:387
  95.4 13.4 %collective-permute-start.21 = (f32[256,256]{1,0:T(8,128)S(1)}, f32[256,256]{1,0:T(8,128)S(1)}, u32[]{:S(2)}, u32[]{:S(2)}) collective-permute-start(f32[256,256]{1,0:T(8,128)S(1)} %collective-permute-done.19), channel_id=1, source_target_pairs={{0,16},{1,17},{2,18},{3,19},{4,20},{5,21},{6,22},{7,23},{8,24},{9,... | collective-permute-start | bytes 786440 | tf_op jit(solution)/shard_map/ppermute | solution.py:387
  107.1 13.0 %collective-permute-start.13 = (f32[256,256]{1,0:T(8,128)S(1)}, f32[256,256]{1,0:T(8,128)S(1)}, u32[]{:S(2)}, u32[]{:S(2)}) collective-permute-start(f32[256,256]{1,0:T(8,128)S(1)} %collective-permute-done.11), channel_id=1, source_target_pairs={{0,16},{1,17},{2,18},{3,19},{4,20},{5,21},{6,22},{7,23},{8,24},{9,... | collective-permute-start | bytes 786440 | tf_op jit(solution)/shard_map/ppermute | solution.py:387
  108.8 16.2 %collective-permute-start.10 = (f32[256,256]{1,0:T(8,128)S(1)}, f32[256,256]{1,0:T(8,128)S(1)}, u32[]{:S(2)}, u32[]{:S(2)}) collective-permute-start(f32[256,256]{1,0:T(8,128)S(1)} %collective-permute-done.8), channel_id=1, source_target_pairs={{0,16},{1,17},{2,18},{3,19},{4,20},{5,21},{6,22},{7,23},{8,24},{9,... | collective-permute-start | bytes 786440 | tf_op jit(solution)/shard_map/ppermute | solution.py:387
  112.5 28.5 %collective-permute-start.37 = (f32[4,256,256]{2,1,0:T(8,128)S(1)}, f32[4,256,256]{2,1,0:T(8,128)S(1)}, u32[]{:S(2)}, u32[]{:S(2)}) collective-permute-start(f32[4,256,256]{2,1,0:T(8,128)S(1)} %copy-done.15), channel_id=1, source_target_pairs={{0,4},{1,5},{2,6},{3,7},{4,0},{5,1},{6,2},{7,3},{8,12},{9,13},{10,... | collective-permute-start | bytes 3145736 | tf_op jit(solution)/shard_map/ppermute | solution.py:387
  115.2 26.4 %collective-permute-start.38 = (f32[4,256,256]{2,1,0:T(8,128)S(1)}, f32[4,256,256]{2,1,0:T(8,128)S(1)}, u32[]{:S(2)}, u32[]{:S(2)}) collective-permute-start(f32[4,256,256]{2,1,0:T(8,128)S(1)} %constant_dynamic-update-slice_fusion.refs_9_), channel_id=1, source_target_pairs={{0,4},{1,5},{2,6},{3,7},{4,0},{5,1},{6,2},{7,3},{8,12},{9,13},{10,... | collective-permute-start | bytes 3145736 | tf_op jit(solution)/shard_map/ppermute | solution.py:387
  115.3 26.4 %collective-permute-start.39 = (f32[4,256,256]{2,1,0:T(8,128)S(1)}, f32[4,256,256]{2,1,0:T(8,128)S(1)}, u32[]{:S(2)}, u32[]{:S(2)}) collective-permute-start(f32[4,256,256]{2,1,0:T(8,128)S(1)} %constant_dynamic-update-slice_fusion.3.refs_10_), channel_id=1, source_target_pairs={{0,4},{1,5},{2,6},{3,7},{4,0},{5,1},{6,2},{7,3},{8,12},{9,13},{10,... | collective-permute-start | bytes 3145736 | tf_op jit(solution)/shard_map/ppermute | solution.py:387
  142.9 99.1 %collective-permute-start.42 = (f32[2,5,256,256]{3,2,1,0:T(8,128)}, f32[2,5,256,256]{3,2,1,0:T(8,128)}, u32[]{:S(2)}, u32[]{:S(2)}) collective-permute-start(f32[2,5,256,256]{3,2,1,0:T(8,128)} %get-tuple-element.29.m0), channel_id=1, source_target_pairs={{0,4},{1,5},{2,6},{3,7},{4,0},{5,1},{6,2},{7,3},{8,12},{9,13},{10,... | collective-permute-start | bytes 7864328 | tf_op jit(solution)/shard_map/ppermute | solution.py:387
  143.6 69.7 %collective-permute-start.41 = (f32[2,5,256,256]{3,2,1,0:T(8,128)}, f32[2,5,256,256]{3,2,1,0:T(8,128)}, u32[]{:S(2)}, u32[]{:S(2)}) collective-permute-start(f32[2,5,256,256]{3,2,1,0:T(8,128)} %get-tuple-element.29.m0), channel_id=1, source_target_pairs={{0,1},{1,0},{2,3},{3,2},{4,5},{5,4},{6,7},{7,6},{8,9},{9,8},{10,11... | collective-permute-start | bytes 7864328 | tf_op jit(solution)/shard_map/ppermute | solution.py:387
  213.2 28.7 %collective-permute-start.43 = (f32[2,5,256,256]{3,2,1,0:T(8,128)}, f32[2,5,256,256]{3,2,1,0:T(8,128)}, u32[]{:S(2)}, u32[]{:S(2)}) collective-permute-start(f32[2,5,256,256]{3,2,1,0:T(8,128)} %collective-permute-done.41.m2), channel_id=1, source_target_pairs={{0,4},{1,5},{2,6},{3,7},{4,0},{5,1},{6,2},{7,3},{8,12},{9,13},{10,... | collective-permute-start | bytes 7864328 | tf_op jit(solution)/shard_map/ppermute | solution.py:387
  216.0 25.7 %collective-permute-start.45 = (f32[1024,256]{1,0:T(8,128)S(1)}, f32[1024,256]{1,0:T(8,128)}, u32[]{:S(2)}, u32[]{:S(2)}) collective-permute-start(f32[1024,256]{1,0:T(8,128)S(1)} %get-tuple-element.39.exp_hi), channel_id=1, source_target_pairs={{0,16},{1,17},{2,18},{3,19},{4,20},{5,21},{6,22},{7,23},{8,24},{9,... | collective-permute-start | bytes 3145736 | tf_op jit(solution)/shard_map/ppermute | solution.py:387
  216.4 25.6 %collective-permute-start.44 = (f32[1024,256]{1,0:T(8,128)}, f32[1024,256]{1,0:T(8,128)}, u32[]{:S(2)}, u32[]{:S(2)}) collective-permute-start(f32[1024,256]{1,0:T(8,128)} %get-tuple-element.40.exp_lo), channel_id=1, source_target_pairs={{0,8},{1,9},{2,10},{3,11},{4,12},{5,13},{6,14},{7,15},{8,0},{9,1},... | collective-permute-start | bytes 3145736 | tf_op jit(solution)/shard_map/ppermute | solution.py:387
  (50 other events, 478.0 us)

commit v2 on v1

--- a/solution.py
+++ b/solution.py
@@ -53,6 +53,35 @@
     below = lax.broadcasted_iota(jnp.int32, (n, n), 1) < lax.broadcasted_iota(jnp.int32, (n, n), 0)
     lower = jnp.where(below, mixed, 0.0)
     return upper - upper.T, corner, -corner.T, lower - lower.T
+
+
+def packet_kernel(ids, m, prev, out, square, gprev, sem):
+    r, z = ids[1], ids[2]
+    n = square.shape[1]
+    per_core = m.shape[1] // n
+    rows = pl.ds(pl.multiple_of(lax.rem(z, per_core) * n, n), n)
+    squares = [pltpu.make_async_copy(m.at[p, rows, :], square.at[p], sem.at[p]) for p in range(2)]
+    other = pltpu.make_async_copy(prev, gprev, sem.at[2])
+    holder = lax.div(z, per_core) == r
+    other.start()
+
+    @pl.when(holder)
+    def _():
+        for c in squares:
+            c.start()
+        on_diag = lax.broadcasted_iota(jnp.int32, (n, n), 0) == lax.broadcasted_iota(jnp.int32, (n, n), 1)
+        for p, c in enumerate(squares):
+            c.wait()
+            out[p:p + 1, :] = jnp.sum(jnp.where(on_diag, square[p], 0.0), axis=0, keepdims=True)
+
+    @pl.when(jnp.logical_not(holder))
+    def _():
+        out[0:2, :] = jnp.zeros((2, n), jnp.float32)
+
+    other.wait()
+    g = gprev[...]
+    total = jnp.sum(jnp.sum((g * g).reshape(-1, 8, n), axis=0))
+    out[2:3, :] = jnp.full((1, n), total, jnp.float32)
 
 
 def term_kernel(ids, weight, diags, own, other, o0, o1, o2, o3, chosen, mre, mim, part, sem, out_sem, chosen_sem):
@@ -81,7 +110,7 @@
         row = diags[slot, pl.ds(p, 1), :]
         return jnp.where(half == 0, row[:, :size], row[:, size:])
 
-    factor = 2.0 * weight[0]
+    factor = 2.0 * weight[b]
     re_own, im_own = piece(j, 0), piece(j, 1)
     low_half = j < blocks // 2
     copies = []
@@ -151,9 +180,9 @@
 
 
 def solve_kernel(ids, prev_square, *refs):
-    groups = (len(refs) - 9) // 4
+    groups = (len(refs) - 11) // 4
     g_in, d_in = refs[:2 * groups], refs[2 * groups:4 * groups]
-    beta_out, exp_out, pg, pd, ahi, alo, hhi, hlo, sem = refs[4 * groups:]
+    beta_out, exp_a, exp_b, exp_c, pg, pd, ahi, alo, hhi, hlo, sem = refs[4 * groups:]
     own_block = ids[3]
     order = ahi.shape[0]
     blocks, _, size = pg.shape
@@ -262,10 +291,16 @@
                 hhi[1 - now, rows, :] = high
                 hlo[1 - now, rows, :] = low
 
-            @pl.when(counter == TAYLOR - 2)
-            def _():
-                exp_out[rows, :] = value
-
+            for t in range(order // tile):
+                @pl.when((counter == TAYLOR - 2) & (i == t))
+                def _(t=t):
+                    begin = 0
+                    for ref in (exp_a, exp_b, exp_c):
+                        end = begin + ref.shape[0]
+                        lo, hi = max(begin, t * tile), min(end, (t + 1) * tile)
+                        if lo < hi:
+                            ref[lo - begin:hi - begin, :] = value[lo - t * tile:hi - t * tile]
+                        begin = end
             return c
 
         return lax.fori_loop(0, order // tile, rows_body, carry)
@@ -316,18 +351,17 @@
         def _():
             grad_out[rows, cols] = jnp.concatenate([-pg[rb, 7 * n:, :], pg[cb, 7 * n:, :]], axis=0).T
 
-        dir_out[rows, cols] = beta[0, 0] * dprev[rows, cols] - grad_out[rows, cols]
+        dir_out[rows, cols] = beta[0:1, 0:1] * dprev[rows, cols] - grad_out[rows, cols]
         return carry
 
     lax.fori_loop(0, per_core * per_chip, out_body, 0)
 
 
-def trial_kernel(ids, exp_lo, exp_hi, m0, m1, m2, m3, out, ehi, elo, mbuf, sem):
+def trial_kernel(ids, exp_a, exp_b, exp_c, m0, m1, m2, m3, out, e, ehi, elo, mbuf, sem):
     r, z = ids[1], ids[2]
-    half = exp_lo.shape[0]
-    width = exp_lo.shape[1]
+    width = exp_a.shape[1]
     size = m0.shape[2]
-    blocks = 2 * half // size
+    blocks = e.shape[0] // size
     work = [(i, p) for i in range(4) for p in range(2)]
     sources = (m0, m1, m2, m3)
 
@@ -337,10 +371,14 @@
 
     copy(0).start()
     copy(1).start()
-    for h, ref in enumerate((exp_lo, exp_hi)):
+    begin = 0
+    for ref in (exp_a, exp_b, exp_c):
         high, low = split_bf16(ref[...])
-        ehi[h * half:(h + 1) * half, :] = high
-        elo[h * half:(h + 1) * half, :] = low
+        rows = slice(begin, begin + ref.shape[0])
+        e[rows, :] = ref[...]
+        ehi[rows, :] = high
+        elo[rows, :] = low
+        begin += ref.shape[0]
     totals = [jnp.zeros((8, width), jnp.float32) for _ in range(2)]
     for n, (i, p) in enumerate(work):
         if n + 2 < len(work):
@@ -352,12 +390,25 @@
         bh, bl = ehi[own, :], elo[own, :]
         for o in range(5):
             high, low = split_bf16(mbuf[n % 3, o])
-            z_o = dot(high, bh) + dot(high, bl) + dot(low, bh)
+            value = dot(high, bh) + dot(high, bl) + dot(low, bh)
             at = pl.ds(pl.multiple_of(lax.rem(j + o, blocks) * size, size), size)
-            e = ehi[at, :].astype(jnp.float32) + elo[at, :].astype(jnp.float32)
-            term = jnp.sum((e * z_o).reshape(-1, 8, width), axis=0)
+            term = jnp.sum((e[at, :] * value).reshape(-1, 8, width), axis=0)
             totals[p] = totals[p] + (term if o in (0, 4) else 2.0 * term)
     out[...] = jnp.concatenate([jnp.sum(t, axis=0, keepdims=True) for t in totals], axis=0)
+
+
+def closing_kernel(ids, weights, *refs):
+    diag_out, sums = refs[-2:]
+    order = diag_out.shape[2]
+    spread, trial = jnp.float32(0.0), jnp.float32(0.0)
+    for k, ref in enumerate(refs[:-2]):
+        group = jnp.bitwise_xor(ids[0], k)
+        re, im = ref[0:1, :], ref[1:2, :]
+        diag_out[group] = ref[0:2, :]
+        spread = spread + ref[2, 0]
+        trial = trial + weights[group] * jnp.sum(1.0 - re * re - im * im)
+    sums[0] = spread
+    sums[1] = trial / order
 
 
 def lookup_weights(bvec_index, weight_table):
@@ -374,7 +425,8 @@
     size = local_cols // n_row
     b, r, z = (lax.axis_index(a).astype(jnp.int32) for a in AXES)
     parity = jnp.bitwise_xor(b, b >> 1) & 1
-    own_block = (z % 2) * 4 + parity * 2 + r
+    half_id = jnp.bitwise_xor(parity, z >> 1) & 1
+    own_block = (z % 2) * 4 + half_id * 2 + r
     ids = jnp.stack([b, r, z, own_block, parity]).astype(jnp.int32)
 
     def send(x, where):
@@ -396,26 +448,27 @@
     m = m_matrices[0]
 
     d_oth = send(dir_prev, core)
-    start = (z % 2) * local_cols
-    square = lax.dynamic_slice_in_dim(m, start, local_cols, 1)
-    holder = (z // 2 == r)
-    eye = jnp.eye(local_cols, dtype=jnp.bool_)
-    own_diag = jnp.sum(jnp.where(eye & holder, square, 0.0), axis=1)
-    prev_part = jnp.sum(grad_prev * grad_prev)
-    packet = jnp.concatenate([own_diag, jnp.full((1, local_cols), prev_part)], axis=0)
+    packet = pl.pallas_call(
+        packet_kernel, out_shape=jax.ShapeDtypeStruct((3, local_cols), jnp.float32),
+        in_specs=[SMEM, ANY, ANY], out_specs=VMEM,
+        scratch_shapes=[pltpu.VMEM((2, local_cols, local_cols), jnp.float32), pltpu.VMEM(grad_prev.shape, jnp.float32),
+                        pltpu.SemaphoreType.DMA((3,))],
+        cost_estimate=pl.CostEstimate(flops=10**6, bytes_accessed=1 << 22, transcendentals=0),
+    )(ids, m, grad_prev)
     packet = packet + send(packet, core)
     m_oth = send(m, core)
-    diags = jnp.stack([packet] + [send(packet, over_z(s)) for s in range(1, n_col)])
-    prev_square = jnp.sum(diags[:, 2, :1], axis=0)
-    spread_own = weight_own[0] * jnp.sum(1.0 - diags[:, 0] ** 2 - diags[:, 1] ** 2) / order
-
-    quarter = jax.ShapeDtypeStruct((size, size), jnp.float32)
     d_own, d_half = pl.pallas_call(
         quarter_kernel, out_shape=[jax.ShapeDtypeStruct((n, size, size), jnp.float32) for n in (4, 2)],
         in_specs=[SMEM, ANY, ANY], out_specs=[VMEM] * 2,
         scratch_shapes=[pltpu.VMEM((5, size, size), jnp.float32), pltpu.SemaphoreType.DMA((5,))],
         cost_estimate=pl.CostEstimate(flops=0, bytes_accessed=1 << 20, transcendentals=0),
     )(ids, dir_prev, d_oth)
+    packet, d_half = lax.optimization_barrier((packet, d_half))
+    diags = jnp.stack([packet] + [send(packet, over_z(s)) for s in range(1, n_col)])
+    prev_square = jnp.sum(diags[:, 2, :1], axis=0)
+    spread_own = weight_own[0] * jnp.sum(1.0 - diags[:, 0] ** 2 - diags[:, 1] ** 2) / order
+
+    quarter = jax.ShapeDtypeStruct((size, size), jnp.float32)
     d_by_z = {s: send(d_half, over_z(s)) for s in (1, 3, 2)}
     terms = pl.pallas_call(
         term_kernel, out_shape=[quarter] * 4 + [jax.ShapeDtypeStruct((2, 5, size, size), jnp.float32)],
@@ -425,7 +478,7 @@
                         pltpu.SemaphoreType.DMA((2, 5)), pltpu.SemaphoreType.DMA((4,)),
                         pltpu.SemaphoreType.DMA((2, 5))],
         cost_estimate=pl.CostEstimate(flops=10**9, bytes_accessed=1 << 22, transcendentals=0),
-    )(ids, weight_own, diags, m, m_oth)
+    )(ids, weight_all, diags, m, m_oth)
     parts = [send(terms[k], over_b(k)) for k in range(1, n_b)]
     g_quarter = ((terms[0] + parts[0]) + parts[1]) + parts[2]
 
@@ -452,10 +505,12 @@
 
     f32 = jnp.float32
     held = pltpu.VMEM((2 * n_col, 4 * size, size), f32)
-    beta, exp_own = pl.pallas_call(
+    by_plane = 13 * order // 32 // 8 * 8
+    shares = (by_plane, by_plane, order - 2 * by_plane)
+    beta, *exp_own = pl.pallas_call(
         solve_kernel,
-        out_shape=[jax.ShapeDtypeStruct((8, 128), f32), jax.ShapeDtypeStruct((order, size), f32)],
-        in_specs=[SMEM, SMEM] + [ANY] * (4 * n_col), out_specs=[VMEM] * 2,
+        out_shape=[jax.ShapeDtypeStruct((8, 128), f32)] + [jax.ShapeDtypeStruct((n, size), f32) for n in shares],
+        in_specs=[SMEM, SMEM] + [ANY] * (4 * n_col), out_specs=[VMEM] * 4,
         scratch_shapes=[held, held,
                         pltpu.VMEM((order, order), jnp.bfloat16), pltpu.VMEM((order, order), jnp.bfloat16),
                         pltpu.VMEM((2, order, size), jnp.bfloat16), pltpu.VMEM((2, order, size), jnp.bfloat16),
@@ -465,50 +520,45 @@
     )(ids, prev_square, *g_groups, *d_groups)
     outputs = pl.pallas_call(
         output_kernel, out_shape=[jax.ShapeDtypeStruct((local_rows, local_cols), f32)] * 2,
-        in_specs=[SMEM, SMEM, VMEM] + [ANY] * (2 * n_col), out_specs=[VMEM] * 2,
+        in_specs=[SMEM, VMEM, VMEM] + [ANY] * (2 * n_col), out_specs=[VMEM] * 2,
         scratch_shapes=[held, pltpu.SemaphoreType.DMA((2 * n_col,))],
         compiler_params=pltpu.CompilerParams(vmem_limit_bytes=VMEM_LIMIT),
         cost_estimate=pl.CostEstimate(flops=10**9, bytes_accessed=1 << 24, transcendentals=0),
     )
-    grad, direction = outputs(ids, beta[:1], dir_prev, *g_groups)
-
-    exp_own, chosen_z = lax.optimization_barrier((exp_own, chosen_z))
+    grad, direction = outputs(ids, beta, dir_prev, *g_groups)
+
+    *exp_own, chosen_z = lax.optimization_barrier((*exp_own, chosen_z))
     chosen_set = (terms[4], send(terms[4], core), chosen_z, send(chosen_z, core))
-    top, bottom = exp_own[:order // 2], exp_own[order // 2:]
-    top_in = send(top, over_b(1))
-    bottom_in = send(bottom, over_b(2))
-
-    def trial(lo, hi):
-        return pl.pallas_call(
-            trial_kernel, out_shape=jax.ShapeDtypeStruct((2, size), f32),
-            in_specs=[SMEM, VMEM, VMEM] + [ANY] * 4, out_specs=VMEM,
-            scratch_shapes=[pltpu.VMEM((order, size), jnp.bfloat16), pltpu.VMEM((order, size), jnp.bfloat16),
-                            pltpu.VMEM((3, 5, size, size), f32), pltpu.SemaphoreType.DMA((3,))],
-            compiler_params=pltpu.CompilerParams(vmem_limit_bytes=VMEM_LIMIT // 2),
-            cost_estimate=pl.CostEstimate(flops=3 * 2 * order * order * size, bytes_accessed=1 << 24, transcendentals=0),
-        )(ids, lo, hi, *chosen_set)
-
-    t_own = trial(top, bottom)
-    top_in, bottom_in, grad, direction = lax.optimization_barrier((top_in, bottom_in, grad, direction))
-    t_in = trial(top_in, bottom_in)
+    exp_in = [send(exp_own[0], over_b(1)), send(exp_own[1], over_b(2)), send(exp_own[2], flip_z(2))]
+
+    trial = pl.pallas_call(
+        trial_kernel, out_shape=jax.ShapeDtypeStruct((2, size), f32),
+        in_specs=[SMEM, VMEM, VMEM, VMEM] + [ANY] * 4, out_specs=VMEM,
+        scratch_shapes=[pltpu.VMEM((order, size), f32), pltpu.VMEM((order, size), jnp.bfloat16),
+                        pltpu.VMEM((order, size), jnp.bfloat16),
+                        pltpu.VMEM((3, 5, size, size), f32), pltpu.SemaphoreType.DMA((3,))],
+        compiler_params=pltpu.CompilerParams(vmem_limit_bytes=VMEM_LIMIT // 2),
+        cost_estimate=pl.CostEstimate(flops=3 * 2 * order * order * size, bytes_accessed=1 << 24, transcendentals=0),
+    )
+    t_own = trial(ids, *exp_own, *chosen_set)
+    *exp_in, grad, direction = lax.optimization_barrier((*exp_in, grad, direction))
+    t_in = trial(ids, *exp_in, *chosen_set)
 
     def ordered(bit, mine, theirs):
         return jnp.where(bit == 0, jnp.stack([mine, theirs]), jnp.stack([theirs, mine]))
 
-    t = ordered(parity, t_own, t_in)
-    t = t + send(t, flip_z(2))
-    t = ordered(z % 2, t, send(t, flip_z(1)))
+    t = ordered(half_id, t_own, t_in)
+    over = [send(t, flip_z(k)) for k in (2, 1, 3)]
+    t = ordered(z % 2, t + over[0], over[1] + over[2])
     t = ordered(r, t, send(t, core))
     t = jnp.transpose(t, (3, 1, 2, 0, 4)).reshape(2, order)
     t = jnp.concatenate([t, jnp.full((1, order), spread_own)], axis=0)
-    t = ordered(b & 1, t, send(t, over_b(1)))
-    t = ordered(b >> 1, t, send(t, over_b(2))).reshape(n_b, 3, order)
-    trial_diag = t[:, :2]
-    spread = jnp.sum(t[:, 2, 0])
-    trial_spread = (
-        jnp.sum(weight_all[:, None] * (1.0 - trial_diag[:, 0] ** 2 - trial_diag[:, 1] ** 2)) / order
-    )
-    return (spread, trial_spread, grad, direction, trial_diag)
+    every = [t] + [send(t, over_b(k)) for k in range(1, n_b)]
+    trial_diag, sums = pl.pallas_call(
+        closing_kernel, out_shape=[jax.ShapeDtypeStruct((n_b, 2, order), f32), jax.ShapeDtypeStruct((2,), f32)],
+        in_specs=[SMEM, SMEM] + [VMEM] * n_b, out_specs=[VMEM, SMEM],
+    )(ids, weight_all, *every)
+    return (sums[0], sums[1], grad, direction, trial_diag)
 
 
 def product(left, right):

time: 283 us -> 277 us (0.979)
  waiting for transfers between devices: 111 us -> 106 us
  Pallas kernels: 97.4 us -> 102 us
  other arithmetic: 9.32 us -> 4.93 us
  starting transfers between devices: 50.9 us -> 54.1 us
    reduce_sum x4 -> x0, other arithmetic: 5.89 us -> none  [the longest x1 2.74 us: paired(): prev_part = jnp.sum(grad_prev * grad_prev)]
    pallas_call x3 -> x5, Pallas kernels: 26.1 us -> 31 us  [the longest x1 9.13 us: paired(): t_in = trial(ids, *exp_in, *chosen_set)]
    ppermute x51 -> x54, waiting for transfers between devices: 111 us -> 106 us  [send(): return lax.ppermute(x, AXES, pairs)]
    ppermute x51 -> x54, starting transfers between devices: 50.9 us -> 54.1 us  [send(): return lax.ppermute(x, AXES, pairs)]
    slice x3 -> x1, local copies, waits for them, and re-layouts: 4.53 us -> 1.29 us  [paired(): return (sums[0], sums[1], grad, direction, trial_diag)]
  transfers between devices with their start and end apart: 51 -> 54, of which waited for: 26 -> 27; matrix products, arithmetic and copies ran while one was open for 5% -> 2% of each run, Pallas kernels for 28% -> 30%
where the time goes in v2:
time: 277 us
  waiting for transfers between devices  106 us (38%)
  Pallas kernels  102 us (37%)
  starting transfers between devices  54.1 us (20%)
  local copies, waits for them, and re-layouts  7.67 us (3%)
  other arithmetic  4.93 us (2%)
    ppermute x54, waiting for transfers between devices, send(): return lax.ppermute(x, AXES, pairs)  106 us
    pallas_call x1, Pallas kernels, paired(): pl.pallas_call(solve_kernel, out_shape=[jax.ShapeDtypeStruct((8, 128), f3...  63.4 us
    ppermute x54, starting transfers between devices, send(): return lax.ppermute(x, AXES, pairs)  54.1 us
    pallas_call x1, Pallas kernels, paired(): t_in = trial(ids, *exp_in, *chosen_set)  9.13 us
    pallas_call x1, Pallas kernels, paired(): grad, direction = outputs(ids, beta, dir_prev, *g_groups)  8.42 us
    pallas_call x1, Pallas kernels, paired(): t_own = trial(ids, *exp_own, *chosen_set)  8.15 us
  transfers between devices with their start and end apart: 54, of which 27 were waited for; matrix products, arithmetic and copies ran while one was open for 2% of the time, Pallas kernels for 30%

profile of v2, /device:TPU:0, one launch (start us, length us, event | category | flops | bytes accessed | tf_op | source)
XLA Modules:
  0.0 277.0 jit_solution(14961847775839060242)
XLA Ops:
  1.8 3.8 %shard_map.92 = f32[3,512]{1,0:T(4,128)} custom-call(s32[5]{0:T(128)} %stack.146.ids, f32[2,1024,512]{2,1,0:T(8,128)} %bitcast.48, f32[1024,512]{1,0:T(8,128)} %prev.1), custom_call_target="tpu_custom_call" | custom-call | flops 1000000 | bytes 4194304 | tf_op jit(solution)/shard_map/pallas_call | solution.py:451
  5.8 5.4 %collective-permute-done = f32[3,512]{1,0:T(4,128)S(1)} collective-permute-done((f32[3,512]{1,0:T(4,128)}, f32[3,512]{1,0:T(4,128)S(1)}, u32[]{:S(2)}, u32[]{:S(2)}) %collective-permute-start) | collective-permute-done | bytes 6176 | tf_op jit(solution)/shard_map/ppermute | solution.py:439
  13.2 3.3 %shard_map.93 = (f32[4,256,256]{2,1,0:T(8,128)}, f32[2,256,256]{2,1,0:T(8,128)}) custom-call(s32[5]{0:T(128)} %stack.146.ids, f32[1024,512]{1,0:T(8,128)} %dprev.1, f32[1024,512]{1,0:T(8,128)} %copy-done.8), custom_call_target="tpu_custom_call" | custom-call | bytes 1048576 | tf_op jit(solution)/shard_map/pallas_call | solution.py:460
  16.5 5.0 %collective-permute-start.34 = (f32[2,256,256]{2,1,0:T(8,128)}, f32[2,256,256]{2,1,0:T(8,128)S(1)}, u32[]{:S(2)}, u32[]{:S(2)}) collective-permute-start(f32[2,256,256]{2,1,0:T(8,128)} %get-tuple-element.38), channel_id=1, source_target_pairs={{0,3},{1,0},{2,1},{3,2},{4,7},{5,4},{6,5},{7,6},{8,11},{9,8},{10,9... | collective-permute-start | bytes 1572872 | tf_op jit(solution)/shard_map/ppermute | solution.py:439
  23.5 10.1 %collective-permute-done.4 = f32[3,512]{1,0:T(4,128)S(1)} collective-permute-done((f32[3,512]{1,0:T(4,128)S(1)}, f32[3,512]{1,0:T(4,128)S(1)}, u32[]{:S(2)}, u32[]{:S(2)}) %collective-permute-start.4) | collective-permute-done | bytes 6176 | tf_op jit(solution)/shard_map/ppermute | solution.py:439
  35.8 3.5 %collective-permute-start.28 = (f32[2,256,256]{2,1,0:T(8,128)}, f32[2,256,256]{2,1,0:T(8,128)S(1)}, u32[]{:S(2)}, u32[]{:S(2)}) collective-permute-start(f32[2,256,256]{2,1,0:T(8,128)} %get-tuple-element.38), channel_id=1, source_target_pairs={{0,1},{1,2},{2,3},{3,0},{4,5},{5,6},{6,7},{7,4},{8,9},{9,10},{10,1... | collective-permute-start | bytes 1572872 | tf_op jit(solution)/shard_map/ppermute | solution.py:439
  41.5 4.0 %shard_map.94 = (f32[256,256]{1,0:T(8,128)}, f32[256,256]{1,0:T(8,128)}, f32[256,256]{1,0:T(8,128)}, f32[256,256]{1,0:T(8,128)}, f32[2,5,256,256]{3,2,1,0:T(8,128)}) custom-call(s32[5]{0:T(128)} %stack.146.ids, f32[4]{0:T(128)} %select_reduce_fusion.weight.weights, f32[4,3,512]{2,1,0:T(4,128)} %pad_maximum_fusion.4.diags, f32[2,1024,512]{2,1,0:T(8,128)} %bitcast.49, ...), custom_call_target="tpu_custom_call" | custom-call | flops 1000000000 | bytes 4194304 | tf_op jit(solution)/shard_map/pallas_call | solution.py:473
  47.6 22.6 %collective-permute-done.31 = f32[2,256,256]{2,1,0:T(8,128)S(1)} collective-permute-done((f32[2,256,256]{2,1,0:T(8,128)}, f32[2,256,256]{2,1,0:T(8,128)S(1)}, u32[]{:S(2)}, u32[]{:S(2)}) %collective-permute-start.31) | collective-permute-done | bytes 524320 | tf_op jit(solution)/shard_map/ppermute | solution.py:439
  75.4 5.1 %collective-permute-done.8 = f32[256,256]{1,0:T(8,128)S(1)} collective-permute-done((f32[256,256]{1,0:T(8,128)}, f32[256,256]{1,0:T(8,128)S(1)}, u32[]{:S(2)}, u32[]{:S(2)}) %collective-permute-start.8) | collective-permute-done | bytes 262176 | tf_op jit(solution)/shard_map/ppermute | solution.py:439
  86.1 5.6 %collective-permute-done.32 = f32[1,256,256]{2,1,0:T(8,128)S(1)} collective-permute-done((f32[1,256,256]{2,1,0:T(8,128)S(1)}, f32[1,256,256]{2,1,0:T(8,128)S(1)}, u32[]{:S(2)}, u32[]{:S(2)}) %collective-permute-start.32) | collective-permute-done | bytes 262176 | tf_op jit(solution)/shard_map/ppermute | solution.py:439
  96.8 8.7 %collective-permute-done.16 = f32[256,256]{1,0:T(8,128)S(1)} collective-permute-done((f32[256,256]{1,0:T(8,128)S(1)}, f32[256,256]{1,0:T(8,128)S(1)}, u32[]{:S(2)}, u32[]{:S(2)}) %collective-permute-start.16) | collective-permute-done | bytes 262176 | tf_op jit(solution)/shard_map/ppermute | solution.py:439
  110.2 3.2 %collective-permute-done.21 = f32[256,256]{1,0:T(8,128)S(1)} collective-permute-done((f32[256,256]{1,0:T(8,128)S(1)}, f32[256,256]{1,0:T(8,128)S(1)}, u32[]{:S(2)}, u32[]{:S(2)}) %collective-permute-start.21) | collective-permute-done | bytes 262176 | tf_op jit(solution)/shard_map/ppermute | solution.py:439
  116.7 4.3 %collective-permute-done.14 = f32[256,256]{1,0:T(8,128)S(1)} collective-permute-done((f32[256,256]{1,0:T(8,128)S(1)}, f32[256,256]{1,0:T(8,128)S(1)}, u32[]{:S(2)}, u32[]{:S(2)}) %collective-permute-start.14) | collective-permute-done | bytes 262176 | tf_op jit(solution)/shard_map/ppermute | solution.py:439
  122.0 3.9 %collective-permute-done.11 = f32[256,256]{1,0:T(8,128)S(1)} collective-permute-done((f32[256,256]{1,0:T(8,128)S(1)}, f32[256,256]{1,0:T(8,128)S(1)}, u32[]{:S(2)}, u32[]{:S(2)}) %collective-permute-start.11) | collective-permute-done | bytes 262176 | tf_op jit(solution)/shard_map/ppermute | solution.py:439
  129.2 5.8 %collective-permute-done.19 = f32[256,256]{1,0:T(8,128)S(1)} collective-permute-done((f32[256,256]{1,0:T(8,128)S(1)}, f32[256,256]{1,0:T(8,128)S(1)}, u32[]{:S(2)}, u32[]{:S(2)}) %collective-permute-start.19) | collective-permute-done | bytes 262176 | tf_op jit(solution)/shard_map/ppermute | solution.py:439
  135.7 3.4 %collective-permute-done.13 = f32[256,256]{1,0:T(8,128)S(1)} collective-permute-done((f32[256,256]{1,0:T(8,128)S(1)}, f32[256,256]{1,0:T(8,128)S(1)}, u32[]{:S(2)}, u32[]{:S(2)}) %collective-permute-start.13) | collective-permute-done | bytes 262176 | tf_op jit(solution)/shard_map/ppermute | solution.py:439
  144.5 4.0 %collective-permute-start.41 = (f32[2,5,256,256]{3,2,1,0:T(8,128)}, f32[2,5,256,256]{3,2,1,0:T(8,128)}, u32[]{:S(2)}, u32[]{:S(2)}) collective-permute-start(f32[2,5,256,256]{3,2,1,0:T(8,128)} %get-tuple-element.42.m0), channel_id=1, source_target_pairs={{0,1},{1,0},{2,3},{3,2},{4,5},{5,4},{6,7},{7,6},{8,9},{9,8},{10,11... | collective-permute-start | bytes 7864328 | tf_op jit(solution)/shard_map/ppermute | solution.py:439
  150.8 63.4 %shard_map.95 = (f32[8,128]{1,0:T(8,128)}, f32[832,256]{1,0:T(8,128)}, f32[832,256]{1,0:T(8,128)}, f32[384,256]{1,0:T(8,128)}) custom-call(s32[5]{0:T(128)} %stack.146.ids, f32[1]{0:T(128)} %bitcast.10.prev_square, f32[4,256,256]{2,1,0:T(8,128)} %copy-done.4, f32[4,256,256]{2,1,0:T(8,128)} %copy-done.7, f32[4,256,256]{2,1,0:T(8,128)} %copy-done.6, ...), custom_call_target="tpu_custom_call" | custom-call | flops 45097156608 | bytes 33554432 | tf_op jit(solution)/shard_map/pallas_call | solution.py:510
  216.2 3.0 %collective-permute-start.46 = (f32[384,256]{1,0:T(8,128)}, f32[384,256]{1,0:T(8,128)}, u32[]{:S(2)}, u32[]{:S(2)}) collective-permute-start(f32[384,256]{1,0:T(8,128)} %get-tuple-element.45.exp_c), channel_id=1, source_target_pairs={{0,2},{1,3},{2,0},{3,1},{4,6},{5,7},{6,4},{7,5},{8,10},{9,11},{10,... | collective-permute-start | bytes 1179656 | tf_op jit(solution)/shard_map/ppermute | solution.py:439
  219.8 8.4 %shard_map.97 = (f32[1024,512]{1,0:T(8,128)}, f32[1024,512]{1,0:T(8,128)}) custom-call(s32[5]{0:T(128)} %stack.146.ids, f32[8,128]{1,0:T(8,128)} %get-tuple-element.47.beta, f32[1024,512]{1,0:T(8,128)} %dprev.1, f32[4,256,256]{2,1,0:T(8,128)} %copy-done.4, f32[4,256,256]{2,1,0:T(8,128)} %copy-done.7, f32[4,256,256]{2,1,0:T(8,128)} %copy-done.6, ...), custom_call_target="tpu_custom_call" | custom-call | flops 1000000000 | bytes 16777216 | tf_op jit(solution)/shard_map/pallas_call | solution.py:528
  228.2 8.8 %collective-permute-done.46.exp_c = f32[384,256]{1,0:T(8,128)} collective-permute-done((f32[384,256]{1,0:T(8,128)}, f32[384,256]{1,0:T(8,128)}, u32[]{:S(2)}, u32[]{:S(2)}) %collective-permute-start.46) | collective-permute-done | bytes 393248 | tf_op jit(solution)/shard_map/ppermute | solution.py:439
  238.1 8.1 %shard_map.96 = f32[2,256]{1,0:T(2,128)S(1)} custom-call(s32[5]{0:T(128)S(1)} %copy-done, f32[832,256]{1,0:T(8,128)S(1)} %copy-done.1, f32[832,256]{1,0:T(8,128)S(1)} %copy-done.2, f32[384,256]{1,0:T(8,128)S(1)} %copy-done.3, f32[2,5,256,256]{3,2,1,0:T(8,128)} %get-tuple-element.42.m0, f32[2,5,256,256]{3,2,1,0:T(8,128)} %collective-permute-done.42.m1, ...), custom_call_target="tpu_custom_call" | custom-call | flops 6442450944 | bytes 16777216 | tf_op jit(solution)/shard_map/pallas_call | solution.py:543
  246.3 9.1 %shard_map.98 = f32[2,256]{1,0:T(2,128)S(1)} custom-call(s32[5]{0:T(128)S(1)} %copy-done, f32[832,256]{1,0:T(8,128)} %collective-permute-done.44.exp_a, f32[832,256]{1,0:T(8,128)} %collective-permute-done.45.exp_b, f32[384,256]{1,0:T(8,128)} %collective-permute-done.46.exp_c, f32[2,5,256,256]{3,2,1,0:T(8,128)} %get-tuple-element.42.m0, ...), custom_call_target="tpu_custom_call" | custom-call | flops 6442450944 | bytes 16777216 | tf_op jit(solution)/shard_map/pallas_call | solution.py:545
  255.4 3.0 %collective-permute-start.47 = (f32[2,2,256]{2,1,0:T(2,128)S(1)}, f32[2,2,256]{2,1,0:T(2,128)S(1)}, u32[]{:S(2)}, u32[]{:S(2)}) collective-permute-start(f32[2,2,256]{2,1,0:T(2,128)S(1)} %maximum_select_fusion.3), channel_id=1, source_target_pairs={{0,2},{1,3},{2,0},{3,1},{4,6},{5,7},{6,4},{7,5},{8,10},{9,11},{10,... | collective-permute-start | bytes 12296 | tf_op jit(solution)/shard_map/ppermute | solution.py:439
  (184 shorter events, 69.0 us)
Async XLA Ops:
  0.6 40.9 %collective-permute-start.5 = (f32[2,1024,512]{2,1,0:T(8,128)}, f32[2,1024,512]{2,1,0:T(8,128)}, u32[]{:S(2)}, u32[]{:S(2)}) collective-permute-start(f32[2,1024,512]{2,1,0:T(8,128)} %bitcast.47), channel_id=1, source_target_pairs={{0,4},{1,5},{2,6},{3,7},{4,0},{5,1},{6,2},{7,3},{8,12},{9,13},{10,... | collective-permute-start | bytes 12582920 | tf_op jit(solution)/shard_map/ppermute | solution.py:439
  16.5 23.4 %collective-permute-start.34 = (f32[2,256,256]{2,1,0:T(8,128)}, f32[2,256,256]{2,1,0:T(8,128)S(1)}, u32[]{:S(2)}, u32[]{:S(2)}) collective-permute-start(f32[2,256,256]{2,1,0:T(8,128)} %get-tuple-element.38), channel_id=1, source_target_pairs={{0,3},{1,0},{2,1},{3,2},{4,7},{5,4},{6,5},{7,6},{8,11},{9,8},{10,9... | collective-permute-start | bytes 1572872 | tf_op jit(solution)/shard_map/ppermute | solution.py:439
  22.0 13.8 %collective-permute-start.3 = (f32[3,512]{1,0:T(4,128)S(1)}, f32[3,512]{1,0:T(4,128)S(1)}, u32[]{:S(2)}, u32[]{:S(2)}) collective-permute-start(f32[3,512]{1,0:T(4,128)S(1)} %add.37), channel_id=1, source_target_pairs={{0,2},{1,3},{2,0},{3,1},{4,6},{5,7},{6,4},{7,5},{8,10},{9,11},{10,... | collective-permute-start | bytes 18440 | tf_op jit(solution)/shard_map/ppermute | solution.py:439
  22.0 17.3 %collective-permute-start.2 = (f32[3,512]{1,0:T(4,128)S(1)}, f32[3,512]{1,0:T(4,128)S(1)}, u32[]{:S(2)}, u32[]{:S(2)}) collective-permute-start(f32[3,512]{1,0:T(4,128)S(1)} %add.37), channel_id=1, source_target_pairs={{0,1},{1,2},{2,3},{3,0},{4,5},{5,6},{6,7},{7,4},{8,9},{9,10},{10,1... | collective-permute-start | bytes 18440 | tf_op jit(solution)/shard_map/ppermute | solution.py:439
  33.7 36.5 %collective-permute-start.31 = (f32[2,256,256]{2,1,0:T(8,128)}, f32[2,256,256]{2,1,0:T(8,128)S(1)}, u32[]{:S(2)}, u32[]{:S(2)}) collective-permute-start(f32[2,256,256]{2,1,0:T(8,128)} %get-tuple-element.38), channel_id=1, source_target_pairs={{0,2},{1,3},{2,0},{3,1},{4,6},{5,7},{6,4},{7,5},{8,10},{9,11},{10,... | collective-permute-start | bytes 1572872 | tf_op jit(solution)/shard_map/ppermute | solution.py:439
  35.8 36.9 %collective-permute-start.28 = (f32[2,256,256]{2,1,0:T(8,128)}, f32[2,256,256]{2,1,0:T(8,128)S(1)}, u32[]{:S(2)}, u32[]{:S(2)}) collective-permute-start(f32[2,256,256]{2,1,0:T(8,128)} %get-tuple-element.38), channel_id=1, source_target_pairs={{0,1},{1,2},{2,3},{3,0},{4,5},{5,6},{6,7},{7,4},{8,9},{9,10},{10,1... | collective-permute-start | bytes 1572872 | tf_op jit(solution)/shard_map/ppermute | solution.py:439
  39.9 43.2 %collective-permute-start.36 = (f32[1,256,256]{2,1,0:T(8,128)S(1)}, f32[1,256,256]{2,1,0:T(8,128)S(1)}, u32[]{:S(2)}, u32[]{:S(2)}) collective-permute-start(f32[1,256,256]{2,1,0:T(8,128)S(1)} %get-tuple-element.57), channel_id=1, source_target_pairs={{0,16},{1,17},{2,18},{3,19},{4,20},{5,21},{6,22},{7,23},{8,24},{9,... | collective-permute-start | bytes 786440 | tf_op jit(solution)/shard_map/ppermute | solution.py:439
  45.5 27.8 %collective-permute-start.6 = (f32[256,256]{1,0:T(8,128)}, f32[256,256]{1,0:T(8,128)S(1)}, u32[]{:S(2)}, u32[]{:S(2)}) collective-permute-start(f32[256,256]{1,0:T(8,128)} %get-tuple-element.34), channel_id=1, source_target_pairs={{0,8},{1,9},{2,10},{3,11},{4,12},{5,13},{6,14},{7,15},{8,0},{9,1},... | collective-permute-start | bytes 786440 | tf_op jit(solution)/shard_map/ppermute | solution.py:439
  47.1 26.8 %collective-permute-start.7 = (f32[256,256]{1,0:T(8,128)}, f32[256,256]{1,0:T(8,128)S(1)}, u32[]{:S(2)}, u32[]{:S(2)}) collective-permute-start(f32[256,256]{1,0:T(8,128)} %get-tuple-element.35), channel_id=1, source_target_pairs={{0,16},{1,17},{2,18},{3,19},{4,20},{5,21},{6,22},{7,23},{8,24},{9,... | collective-permute-start | bytes 786440 | tf_op jit(solution)/shard_map/ppermute | solution.py:439
  72.7 13.5 %collective-permute-start.35 = (f32[1,256,256]{2,1,0:T(8,128)S(1)}, f32[1,256,256]{2,1,0:T(8,128)S(1)}, u32[]{:S(2)}, u32[]{:S(2)}) collective-permute-start(f32[1,256,256]{2,1,0:T(8,128)S(1)} %get-tuple-element.58), channel_id=1, source_target_pairs={{0,8},{1,9},{2,10},{3,11},{4,12},{5,13},{6,14},{7,15},{8,0},{9,1},... | collective-permute-start | bytes 786440 | tf_op jit(solution)/shard_map/ppermute | solution.py:439
  73.9 17.9 %collective-permute-start.32 = (f32[1,256,256]{2,1,0:T(8,128)S(1)}, f32[1,256,256]{2,1,0:T(8,128)S(1)}, u32[]{:S(2)}, u32[]{:S(2)}) collective-permute-start(f32[1,256,256]{2,1,0:T(8,128)S(1)} %get-tuple-element.60), channel_id=1, source_target_pairs={{0,8},{1,9},{2,10},{3,11},{4,12},{5,13},{6,14},{7,15},{8,0},{9,1},... | collective-permute-start | bytes 786440 | tf_op jit(solution)/shard_map/ppermute | solution.py:439
  86.1 19.4 %collective-permute-start.16 = (f32[256,256]{1,0:T(8,128)S(1)}, f32[256,256]{1,0:T(8,128)S(1)}, u32[]{:S(2)}, u32[]{:S(2)}) collective-permute-start(f32[256,256]{1,0:T(8,128)S(1)} %add_add_fusion), channel_id=1, source_target_pairs={{0,2},{1,3},{2,0},{3,1},{4,6},{5,7},{6,4},{7,5},{8,10},{9,11},{10,... | collective-permute-start | bytes 786440 | tf_op jit(solution)/shard_map/ppermute | solution.py:439
  91.7 15.2 %collective-permute-start.12 = (f32[256,256]{1,0:T(8,128)S(1)}, f32[256,256]{1,0:T(8,128)S(1)}, u32[]{:S(2)}, u32[]{:S(2)}) collective-permute-start(f32[256,256]{1,0:T(8,128)S(1)} %add_add_fusion), channel_id=1, source_target_pairs={{0,1},{1,2},{2,3},{3,0},{4,5},{5,6},{6,7},{7,4},{8,9},{9,10},{10,1... | collective-permute-start | bytes 786440 | tf_op jit(solution)/shard_map/ppermute | solution.py:439
  91.7 15.7 %collective-permute-start.10 = (f32[256,256]{1,0:T(8,128)S(1)}, f32[256,256]{1,0:T(8,128)S(1)}, u32[]{:S(2)}, u32[]{:S(2)}) collective-permute-start(f32[256,256]{1,0:T(8,128)S(1)} %add_add_fusion), channel_id=1, source_target_pairs={{0,16},{1,17},{2,18},{3,19},{4,20},{5,21},{6,22},{7,23},{8,24},{9,... | collective-permute-start | bytes 786440 | tf_op jit(solution)/shard_map/ppermute | solution.py:439
  109.7 16.2 %collective-permute-start.11 = (f32[256,256]{1,0:T(8,128)S(1)}, f32[256,256]{1,0:T(8,128)S(1)}, u32[]{:S(2)}, u32[]{:S(2)}) collective-permute-start(f32[256,256]{1,0:T(8,128)S(1)} %collective-permute-done.9), channel_id=1, source_target_pairs={{0,16},{1,17},{2,18},{3,19},{4,20},{5,21},{6,22},{7,23},{8,24},{9,... | collective-permute-start | bytes 786440 | tf_op jit(solution)/shard_map/ppermute | solution.py:439
  113.4 28.5 %collective-permute-start.37 = (f32[4,256,256]{2,1,0:T(8,128)S(1)}, f32[4,256,256]{2,1,0:T(8,128)S(1)}, u32[]{:S(2)}, u32[]{:S(2)}) collective-permute-start(f32[4,256,256]{2,1,0:T(8,128)S(1)} %copy-done.22), channel_id=1, source_target_pairs={{0,4},{1,5},{2,6},{3,7},{4,0},{5,1},{6,2},{7,3},{8,12},{9,13},{10,... | collective-permute-start | bytes 3145736 | tf_op jit(solution)/shard_map/ppermute | solution.py:439
  116.2 26.4 %collective-permute-start.38 = (f32[4,256,256]{2,1,0:T(8,128)S(1)}, f32[4,256,256]{2,1,0:T(8,128)S(1)}, u32[]{:S(2)}, u32[]{:S(2)}) collective-permute-start(f32[4,256,256]{2,1,0:T(8,128)S(1)} %constant_dynamic-update-slice_fusion.refs_9_), channel_id=1, source_target_pairs={{0,4},{1,5},{2,6},{3,7},{4,0},{5,1},{6,2},{7,3},{8,12},{9,13},{10,... | collective-permute-start | bytes 3145736 | tf_op jit(solution)/shard_map/ppermute | solution.py:439
  116.2 26.4 %collective-permute-start.39 = (f32[4,256,256]{2,1,0:T(8,128)S(1)}, f32[4,256,256]{2,1,0:T(8,128)S(1)}, u32[]{:S(2)}, u32[]{:S(2)}) collective-permute-start(f32[4,256,256]{2,1,0:T(8,128)S(1)} %constant_dynamic-update-slice_fusion.3.refs_10_), channel_id=1, source_target_pairs={{0,4},{1,5},{2,6},{3,7},{4,0},{5,1},{6,2},{7,3},{8,12},{9,13},{10,... | collective-permute-start | bytes 3145736 | tf_op jit(solution)/shard_map/ppermute | solution.py:439
  143.8 93.3 %collective-permute-start.42 = (f32[2,5,256,256]{3,2,1,0:T(8,128)}, f32[2,5,256,256]{3,2,1,0:T(8,128)}, u32[]{:S(2)}, u32[]{:S(2)}) collective-permute-start(f32[2,5,256,256]{3,2,1,0:T(8,128)} %get-tuple-element.42.m0), channel_id=1, source_target_pairs={{0,4},{1,5},{2,6},{3,7},{4,0},{5,1},{6,2},{7,3},{8,12},{9,13},{10,... | collective-permute-start | bytes 7864328 | tf_op jit(solution)/shard_map/ppermute | solution.py:439
  144.5 69.7 %collective-permute-start.41 = (f32[2,5,256,256]{3,2,1,0:T(8,128)}, f32[2,5,256,256]{3,2,1,0:T(8,128)}, u32[]{:S(2)}, u32[]{:S(2)}) collective-permute-start(f32[2,5,256,256]{3,2,1,0:T(8,128)} %get-tuple-element.42.m0), channel_id=1, source_target_pairs={{0,1},{1,0},{2,3},{3,2},{4,5},{5,4},{6,7},{7,6},{8,9},{9,8},{10,11... | collective-permute-start | bytes 7864328 | tf_op jit(solution)/shard_map/ppermute | solution.py:439
  214.1 23.0 %collective-permute-start.43 = (f32[2,5,256,256]{3,2,1,0:T(8,128)}, f32[2,5,256,256]{3,2,1,0:T(8,128)}, u32[]{:S(2)}, u32[]{:S(2)}) collective-permute-start(f32[2,5,256,256]{3,2,1,0:T(8,128)} %collective-permute-done.41.m2), channel_id=1, source_target_pairs={{0,4},{1,5},{2,6},{3,7},{4,0},{5,1},{6,2},{7,3},{8,12},{9,13},{10,... | collective-permute-start | bytes 7864328 | tf_op jit(solution)/shard_map/ppermute | solution.py:439
  214.2 22.8 %collective-permute-start.44 = (f32[832,256]{1,0:T(8,128)}, f32[832,256]{1,0:T(8,128)}, u32[]{:S(2)}, u32[]{:S(2)}) collective-permute-start(f32[832,256]{1,0:T(8,128)} %get-tuple-element.43.exp_a), channel_id=1, source_target_pairs={{0,8},{1,9},{2,10},{3,11},{4,12},{5,13},{6,14},{7,15},{8,0},{9,1},... | collective-permute-start | bytes 2555912 | tf_op jit(solution)/shard_map/ppermute | solution.py:439
  215.8 21.3 %collective-permute-start.45 = (f32[832,256]{1,0:T(8,128)}, f32[832,256]{1,0:T(8,128)}, u32[]{:S(2)}, u32[]{:S(2)}) collective-permute-start(f32[832,256]{1,0:T(8,128)} %get-tuple-element.44.exp_b), channel_id=1, source_target_pairs={{0,16},{1,17},{2,18},{3,19},{4,20},{5,21},{6,22},{7,23},{8,24},{9,... | collective-permute-start | bytes 2555912 | tf_op jit(solution)/shard_map/ppermute | solution.py:439
  216.2 20.8 %collective-permute-start.46 = (f32[384,256]{1,0:T(8,128)}, f32[384,256]{1,0:T(8,128)}, u32[]{:S(2)}, u32[]{:S(2)}) collective-permute-start(f32[384,256]{1,0:T(8,128)} %get-tuple-element.45.exp_c), channel_id=1, source_target_pairs={{0,2},{1,3},{2,0},{3,1},{4,6},{5,7},{6,4},{7,5},{8,10},{9,11},{10,... | collective-permute-start | bytes 1179656 | tf_op jit(solution)/shard_map/ppermute | solution.py:439
  (59 other events, 605.7 us)

commit v3 on v2

--- a/solution.py
+++ b/solution.py
@@ -13,7 +13,8 @@
 ANY = pl.BlockSpec(memory_space=pl.ANY)
 SMEM = pl.BlockSpec(memory_space=pltpu.SMEM)
 VMEM = pl.BlockSpec(memory_space=pltpu.VMEM)
-VMEM_LIMIT = 62 * 1024 * 1024
+MIB = 1024 * 1024
+VMEM_LIMIT = 62 * MIB
 
 
 def split_bf16(x):
@@ -398,17 +399,17 @@
 
 
 def closing_kernel(ids, weights, *refs):
-    diag_out, sums = refs[-2:]
+    diag_out, spread_out, trial_out = refs[-3:]
     order = diag_out.shape[2]
     spread, trial = jnp.float32(0.0), jnp.float32(0.0)
-    for k, ref in enumerate(refs[:-2]):
+    for k, ref in enumerate(refs[:-3]):
         group = jnp.bitwise_xor(ids[0], k)
         re, im = ref[0:1, :], ref[1:2, :]
         diag_out[group] = ref[0:2, :]
         spread = spread + ref[2, 0]
         trial = trial + weights[group] * jnp.sum(1.0 - re * re - im * im)
-    sums[0] = spread
-    sums[1] = trial / order
+    spread_out[0] = spread
+    trial_out[0] = trial / order
 
 
 def lookup_weights(bvec_index, weight_table):
@@ -453,6 +454,7 @@
         in_specs=[SMEM, ANY, ANY], out_specs=VMEM,
         scratch_shapes=[pltpu.VMEM((2, local_cols, local_cols), jnp.float32), pltpu.VMEM(grad_prev.shape, jnp.float32),
                         pltpu.SemaphoreType.DMA((3,))],
+        compiler_params=pltpu.CompilerParams(vmem_limit_bytes=8 * MIB),
         cost_estimate=pl.CostEstimate(flops=10**6, bytes_accessed=1 << 22, transcendentals=0),
     )(ids, m, grad_prev)
     packet = packet + send(packet, core)
@@ -461,6 +463,7 @@
         quarter_kernel, out_shape=[jax.ShapeDtypeStruct((n, size, size), jnp.float32) for n in (4, 2)],
         in_specs=[SMEM, ANY, ANY], out_specs=[VMEM] * 2,
         scratch_shapes=[pltpu.VMEM((5, size, size), jnp.float32), pltpu.SemaphoreType.DMA((5,))],
+        compiler_params=pltpu.CompilerParams(vmem_limit_bytes=8 * MIB),
         cost_estimate=pl.CostEstimate(flops=0, bytes_accessed=1 << 20, transcendentals=0),
     )(ids, dir_prev, d_oth)
     packet, d_half = lax.optimization_barrier((packet, d_half))
@@ -477,6 +480,7 @@
                         pltpu.VMEM((4, size, size), jnp.float32),
                         pltpu.SemaphoreType.DMA((2, 5)), pltpu.SemaphoreType.DMA((4,)),
                         pltpu.SemaphoreType.DMA((2, 5))],
+        compiler_params=pltpu.CompilerParams(vmem_limit_bytes=12 * MIB),
         cost_estimate=pl.CostEstimate(flops=10**9, bytes_accessed=1 << 22, transcendentals=0),
     )(ids, weight_all, diags, m, m_oth)
     parts = [send(terms[k], over_b(k)) for k in range(1, n_b)]
@@ -515,7 +519,7 @@
                         pltpu.VMEM((order, order), jnp.bfloat16), pltpu.VMEM((order, order), jnp.bfloat16),
                         pltpu.VMEM((2, order, size), jnp.bfloat16), pltpu.VMEM((2, order, size), jnp.bfloat16),
                         pltpu.SemaphoreType.DMA((2, 2 * n_col))],
-        compiler_params=pltpu.CompilerParams(vmem_limit_bytes=VMEM_LIMIT),
+        compiler_params=pltpu.CompilerParams(vmem_limit_bytes=46 * MIB),
         cost_estimate=pl.CostEstimate(flops=7 * 3 * 2 * order * order * size, bytes_accessed=1 << 25, transcendentals=0),
     )(ids, prev_square, *g_groups, *d_groups)
     outputs = pl.pallas_call(
@@ -537,7 +541,7 @@
         scratch_shapes=[pltpu.VMEM((order, size), f32), pltpu.VMEM((order, size), jnp.bfloat16),
                         pltpu.VMEM((order, size), jnp.bfloat16),
                         pltpu.VMEM((3, 5, size, size), f32), pltpu.SemaphoreType.DMA((3,))],
-        compiler_params=pltpu.CompilerParams(vmem_limit_bytes=VMEM_LIMIT // 2),
+        compiler_params=pltpu.CompilerParams(vmem_limit_bytes=20 * MIB),
         cost_estimate=pl.CostEstimate(flops=3 * 2 * order * order * size, bytes_accessed=1 << 24, transcendentals=0),
     )
     t_own = trial(ids, *exp_own, *chosen_set)
@@ -554,11 +558,13 @@
     t = jnp.transpose(t, (3, 1, 2, 0, 4)).reshape(2, order)
     t = jnp.concatenate([t, jnp.full((1, order), spread_own)], axis=0)
     every = [t] + [send(t, over_b(k)) for k in range(1, n_b)]
-    trial_diag, sums = pl.pallas_call(
-        closing_kernel, out_shape=[jax.ShapeDtypeStruct((n_b, 2, order), f32), jax.ShapeDtypeStruct((2,), f32)],
-        in_specs=[SMEM, SMEM] + [VMEM] * n_b, out_specs=[VMEM, SMEM],
+    one = jax.ShapeDtypeStruct((1,), f32)
+    trial_diag, spread, trial_spread = pl.pallas_call(
+        closing_kernel, out_shape=[jax.ShapeDtypeStruct((n_b, 2, order), f32), one, one],
+        in_specs=[SMEM, SMEM] + [VMEM] * n_b, out_specs=[VMEM, SMEM, SMEM],
+        compiler_params=pltpu.CompilerParams(vmem_limit_bytes=4 * MIB),
     )(ids, weight_all, *every)
-    return (sums[0], sums[1], grad, direction, trial_diag)
+    return (spread.reshape(()), trial_spread.reshape(()), grad, direction, trial_diag)
 
 
 def product(left, right):

time: 277 us -> 269 us (0.971)
  Pallas kernels: 102 us -> 94.3 us
  other arithmetic: 4.93 us -> 2.01 us
    unnamed x64 -> x56, local copies, waits for them, and re-layouts: 5.02 us -> 5.73 us
  transfers between devices with their start and end apart: 54 -> 54, of which waited for: 27 -> 26; matrix products, arithmetic and copies ran while one was open for 2% -> 1% of each run, Pallas kernels for 30% -> 28%
where the time goes in v3:
time: 269 us
  waiting for transfers between devices  108 us (40%)
  Pallas kernels  94.3 us (35%)
  starting transfers between devices  55.4 us (21%)
  local copies, waits for them, and re-layouts  6.6 us (2%)
    ppermute x54, waiting for transfers between devices, send(): return lax.ppermute(x, AXES, pairs)  108 us
    pallas_call x1, Pallas kernels, paired(): pl.pallas_call(solve_kernel, out_shape=[jax.ShapeDtypeStruct((8, 128), f3...  61.9 us
    ppermute x54, starting transfers between devices, send(): return lax.ppermute(x, AXES, pairs)  55.4 us
    pallas_call x1, Pallas kernels, paired(): t_own = trial(ids, *exp_own, *chosen_set)  8.88 us
    pallas_call x1, Pallas kernels, paired(): t_in = trial(ids, *exp_in, *chosen_set)  8.87 us
    pallas_call x1, Pallas kernels, paired(): grad, direction = outputs(ids, beta, dir_prev, *g_groups)  8.29 us
    unnamed x56, local copies, waits for them, and re-layouts  5.73 us
  transfers between devices with their start and end apart: 54, of which 26 were waited for; matrix products, arithmetic and copies ran while one was open for 1% of the time, Pallas kernels for 28%

profile of v3, /device:TPU:0, one launch (start us, length us, event | category | flops | bytes accessed | tf_op | source)
XLA Modules:
  0.0 268.7 jit_solution(12884049677933521563)
XLA Ops:
  6.7 4.5 %collective-permute-done = f32[3,512]{1,0:T(4,128)S(1)} collective-permute-done((f32[3,512]{1,0:T(4,128)S(1)}, f32[3,512]{1,0:T(4,128)S(1)}, u32[]{:S(2)}, u32[]{:S(2)}) %collective-permute-start) | collective-permute-done | bytes 6176 | tf_op jit(solution)/shard_map/ppermute | solution.py:440
  12.2 5.0 %collective-permute-start.34 = (f32[2,256,256]{2,1,0:T(8,128)S(1)}, f32[2,256,256]{2,1,0:T(8,128)S(1)}, u32[]{:S(2)}, u32[]{:S(2)}) collective-permute-start(f32[2,256,256]{2,1,0:T(8,128)S(1)} %get-tuple-element.39), channel_id=1, source_target_pairs={{0,3},{1,0},{2,1},{3,2},{4,7},{5,4},{6,5},{7,6},{8,11},{9,8},{10,9... | collective-permute-start | bytes 1572872 | tf_op jit(solution)/shard_map/ppermute | solution.py:440
  19.3 9.9 %collective-permute-done.4 = f32[3,512]{1,0:T(4,128)S(1)} collective-permute-done((f32[3,512]{1,0:T(4,128)S(1)}, f32[3,512]{1,0:T(4,128)S(1)}, u32[]{:S(2)}, u32[]{:S(2)}) %collective-permute-start.4) | collective-permute-done | bytes 6176 | tf_op jit(solution)/shard_map/ppermute | solution.py:440
  30.7 3.5 %collective-permute-start.28 = (f32[2,256,256]{2,1,0:T(8,128)S(1)}, f32[2,256,256]{2,1,0:T(8,128)S(1)}, u32[]{:S(2)}, u32[]{:S(2)}) collective-permute-start(f32[2,256,256]{2,1,0:T(8,128)S(1)} %get-tuple-element.39), channel_id=1, source_target_pairs={{0,1},{1,2},{2,3},{3,0},{4,5},{5,6},{6,7},{7,4},{8,9},{9,10},{10,1... | collective-permute-start | bytes 1572872 | tf_op jit(solution)/shard_map/ppermute | solution.py:440
  35.9 2.8 %shard_map.94 = (f32[256,256]{1,0:T(8,128)S(1)}, f32[256,256]{1,0:T(8,128)S(1)}, f32[256,256]{1,0:T(8,128)S(1)}, f32[256,256]{1,0:T(8,128)S(1)}, f32[2,5,256,256]{3,2,1,0:T(8,128)}) custom-call(s32[5]{0:T(128)S(1)} %stack.146.ids, f32[4]{0:T(128)S(1)} %select_reduce_fusion.weight.weights, f32[4,3,512]{2,1,0:T(4,128)S(1)} %pad_maximum_fusion.4.diags, ...), custom_call_target="tpu_custom_call" | custom-call | flops 1000000000 | bytes 4194304 | tf_op jit(solution)/shard_map/pallas_call | solution.py:476
  40.8 24.6 %collective-permute-done.31 = f32[2,256,256]{2,1,0:T(8,128)S(1)} collective-permute-done((f32[2,256,256]{2,1,0:T(8,128)S(1)}, f32[2,256,256]{2,1,0:T(8,128)S(1)}, u32[]{:S(2)}, u32[]{:S(2)}) %collective-permute-start.31) | collective-permute-done | bytes 524320 | tf_op jit(solution)/shard_map/ppermute | solution.py:440
  70.7 4.9 %collective-permute-done.8 = f32[256,256]{1,0:T(8,128)S(1)} collective-permute-done((f32[256,256]{1,0:T(8,128)S(1)}, f32[256,256]{1,0:T(8,128)S(1)}, u32[]{:S(2)}, u32[]{:S(2)}) %collective-permute-start.8) | collective-permute-done | bytes 262176 | tf_op jit(solution)/shard_map/ppermute | solution.py:440
  81.2 5.6 %collective-permute-done.32 = f32[1,256,256]{2,1,0:T(8,128)S(1)} collective-permute-done((f32[1,256,256]{2,1,0:T(8,128)S(1)}, f32[1,256,256]{2,1,0:T(8,128)S(1)}, u32[]{:S(2)}, u32[]{:S(2)}) %collective-permute-start.32) | collective-permute-done | bytes 262176 | tf_op jit(solution)/shard_map/ppermute | solution.py:440
  91.9 8.7 %collective-permute-done.16 = f32[256,256]{1,0:T(8,128)S(1)} collective-permute-done((f32[256,256]{1,0:T(8,128)S(1)}, f32[256,256]{1,0:T(8,128)S(1)}, u32[]{:S(2)}, u32[]{:S(2)}) %collective-permute-start.16) | collective-permute-done | bytes 262176 | tf_op jit(solution)/shard_map/ppermute | solution.py:440
  105.5 3.0 %collective-permute-done.21 = f32[256,256]{1,0:T(8,128)S(1)} collective-permute-done((f32[256,256]{1,0:T(8,128)S(1)}, f32[256,256]{1,0:T(8,128)S(1)}, u32[]{:S(2)}, u32[]{:S(2)}) %collective-permute-start.21) | collective-permute-done | bytes 262176 | tf_op jit(solution)/shard_map/ppermute | solution.py:440
  108.5 2.7 %collective-permute-done.18 = f32[256,256]{1,0:T(8,128)S(1)} collective-permute-done((f32[256,256]{1,0:T(8,128)S(1)}, f32[256,256]{1,0:T(8,128)S(1)}, u32[]{:S(2)}, u32[]{:S(2)}) %collective-permute-start.18) | collective-permute-done | bytes 262176 | tf_op jit(solution)/shard_map/ppermute | solution.py:440
  111.8 4.3 %collective-permute-done.14 = f32[256,256]{1,0:T(8,128)S(1)} collective-permute-done((f32[256,256]{1,0:T(8,128)S(1)}, f32[256,256]{1,0:T(8,128)S(1)}, u32[]{:S(2)}, u32[]{:S(2)}) %collective-permute-start.14) | collective-permute-done | bytes 262176 | tf_op jit(solution)/shard_map/ppermute | solution.py:440
  117.3 3.6 %collective-permute-done.11 = f32[256,256]{1,0:T(8,128)S(1)} collective-permute-done((f32[256,256]{1,0:T(8,128)S(1)}, f32[256,256]{1,0:T(8,128)S(1)}, u32[]{:S(2)}, u32[]{:S(2)}) %collective-permute-start.11) | collective-permute-done | bytes 262176 | tf_op jit(solution)/shard_map/ppermute | solution.py:440
  124.3 5.8 %collective-permute-done.19 = f32[256,256]{1,0:T(8,128)S(1)} collective-permute-done((f32[256,256]{1,0:T(8,128)S(1)}, f32[256,256]{1,0:T(8,128)S(1)}, u32[]{:S(2)}, u32[]{:S(2)}) %collective-permute-start.19) | collective-permute-done | bytes 262176 | tf_op jit(solution)/shard_map/ppermute | solution.py:440
  130.7 3.4 %collective-permute-done.13 = f32[256,256]{1,0:T(8,128)S(1)} collective-permute-done((f32[256,256]{1,0:T(8,128)S(1)}, f32[256,256]{1,0:T(8,128)S(1)}, u32[]{:S(2)}, u32[]{:S(2)}) %collective-permute-start.13) | collective-permute-done | bytes 262176 | tf_op jit(solution)/shard_map/ppermute | solution.py:440
  134.1 2.8 %collective-permute-done.15 = f32[256,256]{1,0:T(8,128)S(1)} collective-permute-done((f32[256,256]{1,0:T(8,128)S(1)}, f32[256,256]{1,0:T(8,128)S(1)}, u32[]{:S(2)}, u32[]{:S(2)}) %collective-permute-start.15) | collective-permute-done | bytes 262176 | tf_op jit(solution)/shard_map/ppermute | solution.py:440
  139.5 4.0 %collective-permute-start.41 = (f32[2,5,256,256]{3,2,1,0:T(8,128)}, f32[2,5,256,256]{3,2,1,0:T(8,128)}, u32[]{:S(2)}, u32[]{:S(2)}) collective-permute-start(f32[2,5,256,256]{3,2,1,0:T(8,128)} %get-tuple-element.43.m0), channel_id=1, source_target_pairs={{0,1},{1,0},{2,3},{3,2},{4,5},{5,4},{6,7},{7,6},{8,9},{9,8},{10,11... | collective-permute-start | bytes 7864328 | tf_op jit(solution)/shard_map/ppermute | solution.py:440
  145.2 61.9 %shard_map.95 = (f32[8,128]{1,0:T(8,128)S(1)}, f32[832,256]{1,0:T(8,128)S(1)}, f32[832,256]{1,0:T(8,128)}, f32[384,256]{1,0:T(8,128)}) custom-call(s32[5]{0:T(128)S(1)} %stack.146.ids, f32[1]{0:T(128)} %bitcast.10.prev_square, f32[4,256,256]{2,1,0:T(8,128)S(1)} %pad_maximum_fusion.refs_0_, f32[4,256,256]{2,1,0:T(8,128)S(1)} %pad_maximum_fusion.1.refs_1_, ...), custom_call_target="tpu_custom_call" | custom-call | flops 45097156608 | bytes 33554432 | tf_op jit(solution)/shard_map/pallas_call | solution.py:514
  210.4 2.9 %collective-permute-start.46 = (f32[384,256]{1,0:T(8,128)}, f32[384,256]{1,0:T(8,128)}, u32[]{:S(2)}, u32[]{:S(2)}) collective-permute-start(f32[384,256]{1,0:T(8,128)} %get-tuple-element.46.exp_c), channel_id=1, source_target_pairs={{0,2},{1,3},{2,0},{3,1},{4,6},{5,7},{6,4},{7,5},{8,10},{9,11},{10,... | collective-permute-start | bytes 1179656 | tf_op jit(solution)/shard_map/ppermute | solution.py:440
  213.9 8.3 %shard_map.97 = (f32[1024,512]{1,0:T(8,128)}, f32[1024,512]{1,0:T(8,128)}) custom-call(s32[5]{0:T(128)} %copy-done.9, f32[8,128]{1,0:T(8,128)} %copy-done.11, f32[1024,512]{1,0:T(8,128)} %dprev.1, f32[4,256,256]{2,1,0:T(8,128)} %copy-done.3, f32[4,256,256]{2,1,0:T(8,128)} %copy-done.6, f32[4,256,256]{2,1,0:T(8,128)} %copy-done.5, f32[4,256,256]{2,1,0:T(8,128)} %copy-done.4, ...), custom_call_target="tpu_custom_call" | custom-call | flops 1000000000 | bytes 16777216 | tf_op jit(solution)/shard_map/pallas_call | solution.py:532
  222.2 8.9 %collective-permute-done.46.exp_c = f32[384,256]{1,0:T(8,128)} collective-permute-done((f32[384,256]{1,0:T(8,128)}, f32[384,256]{1,0:T(8,128)}, u32[]{:S(2)}, u32[]{:S(2)}) %collective-permute-start.46) | collective-permute-done | bytes 393248 | tf_op jit(solution)/shard_map/ppermute | solution.py:440
  231.2 8.9 %shard_map.96 = f32[2,256]{1,0:T(2,128)S(1)} custom-call(s32[5]{0:T(128)S(1)} %copy-done.10, f32[832,256]{1,0:T(8,128)S(1)} %get-tuple-element.44.exp_a, f32[832,256]{1,0:T(8,128)} %get-tuple-element.45.exp_b, f32[384,256]{1,0:T(8,128)} %get-tuple-element.46.exp_c, f32[2,5,256,256]{3,2,1,0:T(8,128)} %get-tuple-element.43.m0, ...), custom_call_target="tpu_custom_call" | custom-call | flops 6442450944 | bytes 16777216 | tf_op jit(solution)/shard_map/pallas_call | solution.py:547
  240.1 8.9 %shard_map.98 = f32[2,256]{1,0:T(2,128)S(1)} custom-call(s32[5]{0:T(128)S(1)} %copy-done.10, f32[832,256]{1,0:T(8,128)S(1)} %collective-permute-done.44.exp_a, f32[832,256]{1,0:T(8,128)} %collective-permute-done.45.exp_b, f32[384,256]{1,0:T(8,128)} %collective-permute-done.46.exp_c, f32[2,5,256,256]{3,2,1,0:T(8,128)} %get-tuple-element.43.m0, ...), custom_call_target="tpu_custom_call" | custom-call | flops 6442450944 | bytes 16777216 | tf_op jit(solution)/shard_map/pallas_call | solution.py:549
  249.0 3.0 %collective-permute-start.47 = (f32[2,2,256]{2,1,0:T(2,128)S(1)}, f32[2,2,256]{2,1,0:T(2,128)S(1)}, u32[]{:S(2)}, u32[]{:S(2)}) collective-permute-start(f32[2,2,256]{2,1,0:T(2,128)S(1)} %maximum_select_fusion.3), channel_id=1, source_target_pairs={{0,2},{1,3},{2,0},{3,1},{4,6},{5,7},{6,4},{7,5},{8,10},{9,11},{10,... | collective-permute-start | bytes 12296 | tf_op jit(solution)/shard_map/ppermute | solution.py:440
  (175 shorter events, 64.0 us)
Async XLA Ops:
  0.6 35.3 %collective-permute-start.5 = (f32[2,1024,512]{2,1,0:T(8,128)}, f32[2,1024,512]{2,1,0:T(8,128)}, u32[]{:S(2)}, u32[]{:S(2)}) collective-permute-start(f32[2,1024,512]{2,1,0:T(8,128)} %bitcast.43), channel_id=1, source_target_pairs={{0,4},{1,5},{2,6},{3,7},{4,0},{5,1},{6,2},{7,3},{8,12},{9,13},{10,... | collective-permute-start | bytes 12582920 | tf_op jit(solution)/shard_map/ppermute | solution.py:440
  12.2 22.0 %collective-permute-start.34 = (f32[2,256,256]{2,1,0:T(8,128)S(1)}, f32[2,256,256]{2,1,0:T(8,128)S(1)}, u32[]{:S(2)}, u32[]{:S(2)}) collective-permute-start(f32[2,256,256]{2,1,0:T(8,128)S(1)} %get-tuple-element.39), channel_id=1, source_target_pairs={{0,3},{1,0},{2,1},{3,2},{4,7},{5,4},{6,5},{7,6},{8,11},{9,8},{10,9... | collective-permute-start | bytes 1572872 | tf_op jit(solution)/shard_map/ppermute | solution.py:440
  17.7 16.6 %collective-permute-start.2 = (f32[3,512]{1,0:T(4,128)S(1)}, f32[3,512]{1,0:T(4,128)S(1)}, u32[]{:S(2)}, u32[]{:S(2)}) collective-permute-start(f32[3,512]{1,0:T(4,128)S(1)} %add.37), channel_id=1, source_target_pairs={{0,1},{1,2},{2,3},{3,0},{4,5},{5,6},{6,7},{7,4},{8,9},{9,10},{10,1... | collective-permute-start | bytes 18440 | tf_op jit(solution)/shard_map/ppermute | solution.py:440
  29.1 36.3 %collective-permute-start.31 = (f32[2,256,256]{2,1,0:T(8,128)S(1)}, f32[2,256,256]{2,1,0:T(8,128)S(1)}, u32[]{:S(2)}, u32[]{:S(2)}) collective-permute-start(f32[2,256,256]{2,1,0:T(8,128)S(1)} %get-tuple-element.39), channel_id=1, source_target_pairs={{0,2},{1,3},{2,0},{3,1},{4,6},{5,7},{6,4},{7,5},{8,10},{9,11},{10,... | collective-permute-start | bytes 1572872 | tf_op jit(solution)/shard_map/ppermute | solution.py:440
  30.7 37.2 %collective-permute-start.28 = (f32[2,256,256]{2,1,0:T(8,128)S(1)}, f32[2,256,256]{2,1,0:T(8,128)S(1)}, u32[]{:S(2)}, u32[]{:S(2)}) collective-permute-start(f32[2,256,256]{2,1,0:T(8,128)S(1)} %get-tuple-element.39), channel_id=1, source_target_pairs={{0,1},{1,2},{2,3},{3,0},{4,5},{5,6},{6,7},{7,4},{8,9},{9,10},{10,1... | collective-permute-start | bytes 1572872 | tf_op jit(solution)/shard_map/ppermute | solution.py:440
  34.3 42.8 %collective-permute-start.36 = (f32[1,256,256]{2,1,0:T(8,128)S(1)}, f32[1,256,256]{2,1,0:T(8,128)S(1)}, u32[]{:S(2)}, u32[]{:S(2)}) collective-permute-start(f32[1,256,256]{2,1,0:T(8,128)S(1)} %get-tuple-element.59), channel_id=1, source_target_pairs={{0,16},{1,17},{2,18},{3,19},{4,20},{5,21},{6,22},{7,23},{8,24},{9,... | collective-permute-start | bytes 786440 | tf_op jit(solution)/shard_map/ppermute | solution.py:440
  38.7 29.8 %collective-permute-start.6 = (f32[256,256]{1,0:T(8,128)S(1)}, f32[256,256]{1,0:T(8,128)S(1)}, u32[]{:S(2)}, u32[]{:S(2)}) collective-permute-start(f32[256,256]{1,0:T(8,128)S(1)} %get-tuple-element.35), channel_id=1, source_target_pairs={{0,8},{1,9},{2,10},{3,11},{4,12},{5,13},{6,14},{7,15},{8,0},{9,1},... | collective-permute-start | bytes 786440 | tf_op jit(solution)/shard_map/ppermute | solution.py:440
  40.3 28.9 %collective-permute-start.7 = (f32[256,256]{1,0:T(8,128)S(1)}, f32[256,256]{1,0:T(8,128)S(1)}, u32[]{:S(2)}, u32[]{:S(2)}) collective-permute-start(f32[256,256]{1,0:T(8,128)S(1)} %get-tuple-element.36), channel_id=1, source_target_pairs={{0,16},{1,17},{2,18},{3,19},{4,20},{5,21},{6,22},{7,23},{8,24},{9,... | collective-permute-start | bytes 786440 | tf_op jit(solution)/shard_map/ppermute | solution.py:440
  69.2 17.7 %collective-permute-start.32 = (f32[1,256,256]{2,1,0:T(8,128)S(1)}, f32[1,256,256]{2,1,0:T(8,128)S(1)}, u32[]{:S(2)}, u32[]{:S(2)}) collective-permute-start(f32[1,256,256]{2,1,0:T(8,128)S(1)} %get-tuple-element.62), channel_id=1, source_target_pairs={{0,8},{1,9},{2,10},{3,11},{4,12},{5,13},{6,14},{7,15},{8,0},{9,1},... | collective-permute-start | bytes 786440 | tf_op jit(solution)/shard_map/ppermute | solution.py:440
  81.2 19.3 %collective-permute-start.16 = (f32[256,256]{1,0:T(8,128)S(1)}, f32[256,256]{1,0:T(8,128)S(1)}, u32[]{:S(2)}, u32[]{:S(2)}) collective-permute-start(f32[256,256]{1,0:T(8,128)S(1)} %add_add_fusion), channel_id=1, source_target_pairs={{0,2},{1,3},{2,0},{3,1},{4,6},{5,7},{6,4},{7,5},{8,10},{9,11},{10,... | collective-permute-start | bytes 786440 | tf_op jit(solution)/shard_map/ppermute | solution.py:440
  86.8 15.2 %collective-permute-start.12 = (f32[256,256]{1,0:T(8,128)S(1)}, f32[256,256]{1,0:T(8,128)S(1)}, u32[]{:S(2)}, u32[]{:S(2)}) collective-permute-start(f32[256,256]{1,0:T(8,128)S(1)} %add_add_fusion), channel_id=1, source_target_pairs={{0,1},{1,2},{2,3},{3,0},{4,5},{5,6},{6,7},{7,4},{8,9},{9,10},{10,1... | collective-permute-start | bytes 786440 | tf_op jit(solution)/shard_map/ppermute | solution.py:440
  86.8 15.9 %collective-permute-start.10 = (f32[256,256]{1,0:T(8,128)S(1)}, f32[256,256]{1,0:T(8,128)S(1)}, u32[]{:S(2)}, u32[]{:S(2)}) collective-permute-start(f32[256,256]{1,0:T(8,128)S(1)} %add_add_fusion), channel_id=1, source_target_pairs={{0,16},{1,17},{2,18},{3,19},{4,20},{5,21},{6,22},{7,23},{8,24},{9,... | collective-permute-start | bytes 786440 | tf_op jit(solution)/shard_map/ppermute | solution.py:440
  89.9 13.4 %collective-permute-start.9 = (f32[256,256]{1,0:T(8,128)S(1)}, f32[256,256]{1,0:T(8,128)S(1)}, u32[]{:S(2)}, u32[]{:S(2)}) collective-permute-start(f32[256,256]{1,0:T(8,128)S(1)} %add_add_fusion), channel_id=1, source_target_pairs={{0,8},{1,9},{2,10},{3,11},{4,12},{5,13},{6,14},{7,15},{8,0},{9,1},... | collective-permute-start | bytes 786440 | tf_op jit(solution)/shard_map/ppermute | solution.py:440
  91.4 13.4 %collective-permute-start.22 = (f32[256,256]{1,0:T(8,128)S(1)}, f32[256,256]{1,0:T(8,128)S(1)}, u32[]{:S(2)}, u32[]{:S(2)}) collective-permute-start(f32[256,256]{1,0:T(8,128)S(1)} %collective-permute-done.20), channel_id=1, source_target_pairs={{0,16},{1,17},{2,18},{3,19},{4,20},{5,21},{6,22},{7,23},{8,24},{9,... | collective-permute-start | bytes 786440 | tf_op jit(solution)/shard_map/ppermute | solution.py:440
  104.7 16.2 %collective-permute-start.11 = (f32[256,256]{1,0:T(8,128)S(1)}, f32[256,256]{1,0:T(8,128)S(1)}, u32[]{:S(2)}, u32[]{:S(2)}) collective-permute-start(f32[256,256]{1,0:T(8,128)S(1)} %collective-permute-done.9), channel_id=1, source_target_pairs={{0,16},{1,17},{2,18},{3,19},{4,20},{5,21},{6,22},{7,23},{8,24},{9,... | collective-permute-start | bytes 786440 | tf_op jit(solution)/shard_map/ppermute | solution.py:440
  108.5 28.5 %collective-permute-start.37 = (f32[4,256,256]{2,1,0:T(8,128)S(1)}, f32[4,256,256]{2,1,0:T(8,128)S(1)}, u32[]{:S(2)}, u32[]{:S(2)}) collective-permute-start(f32[4,256,256]{2,1,0:T(8,128)S(1)} %get-tuple-element.38.refs_8_), channel_id=1, source_target_pairs={{0,4},{1,5},{2,6},{3,7},{4,0},{5,1},{6,2},{7,3},{8,12},{9,13},{10,... | collective-permute-start | bytes 3145736 | tf_op jit(solution)/shard_map/ppermute | solution.py:440
  111.2 26.3 %collective-permute-start.38 = (f32[4,256,256]{2,1,0:T(8,128)S(1)}, f32[4,256,256]{2,1,0:T(8,128)S(1)}, u32[]{:S(2)}, u32[]{:S(2)}) collective-permute-start(f32[4,256,256]{2,1,0:T(8,128)S(1)} %constant_dynamic-update-slice_fusion.refs_9_), channel_id=1, source_target_pairs={{0,4},{1,5},{2,6},{3,7},{4,0},{5,1},{6,2},{7,3},{8,12},{9,13},{10,... | collective-permute-start | bytes 3145736 | tf_op jit(solution)/shard_map/ppermute | solution.py:440
  111.3 26.4 %collective-permute-start.39 = (f32[4,256,256]{2,1,0:T(8,128)S(1)}, f32[4,256,256]{2,1,0:T(8,128)S(1)}, u32[]{:S(2)}, u32[]{:S(2)}) collective-permute-start(f32[4,256,256]{2,1,0:T(8,128)S(1)} %constant_dynamic-update-slice_fusion.3.refs_10_), channel_id=1, source_target_pairs={{0,4},{1,5},{2,6},{3,7},{4,0},{5,1},{6,2},{7,3},{8,12},{9,13},{10,... | collective-permute-start | bytes 3145736 | tf_op jit(solution)/shard_map/ppermute | solution.py:440
  138.9 92.3 %collective-permute-start.42 = (f32[2,5,256,256]{3,2,1,0:T(8,128)}, f32[2,5,256,256]{3,2,1,0:T(8,128)}, u32[]{:S(2)}, u32[]{:S(2)}) collective-permute-start(f32[2,5,256,256]{3,2,1,0:T(8,128)} %get-tuple-element.43.m0), channel_id=1, source_target_pairs={{0,4},{1,5},{2,6},{3,7},{4,0},{5,1},{6,2},{7,3},{8,12},{9,13},{10,... | collective-permute-start | bytes 7864328 | tf_op jit(solution)/shard_map/ppermute | solution.py:440
  139.5 68.2 %collective-permute-start.41 = (f32[2,5,256,256]{3,2,1,0:T(8,128)}, f32[2,5,256,256]{3,2,1,0:T(8,128)}, u32[]{:S(2)}, u32[]{:S(2)}) collective-permute-start(f32[2,5,256,256]{3,2,1,0:T(8,128)} %get-tuple-element.43.m0), channel_id=1, source_target_pairs={{0,1},{1,0},{2,3},{3,2},{4,5},{5,4},{6,7},{7,6},{8,9},{9,8},{10,11... | collective-permute-start | bytes 7864328 | tf_op jit(solution)/shard_map/ppermute | solution.py:440
  207.7 23.5 %collective-permute-start.43 = (f32[2,5,256,256]{3,2,1,0:T(8,128)}, f32[2,5,256,256]{3,2,1,0:T(8,128)}, u32[]{:S(2)}, u32[]{:S(2)}) collective-permute-start(f32[2,5,256,256]{3,2,1,0:T(8,128)} %collective-permute-done.41.m2), channel_id=1, source_target_pairs={{0,4},{1,5},{2,6},{3,7},{4,0},{5,1},{6,2},{7,3},{8,12},{9,13},{10,... | collective-permute-start | bytes 7864328 | tf_op jit(solution)/shard_map/ppermute | solution.py:440
  207.8 23.4 %collective-permute-start.44 = (f32[832,256]{1,0:T(8,128)S(1)}, f32[832,256]{1,0:T(8,128)S(1)}, u32[]{:S(2)}, u32[]{:S(2)}) collective-permute-start(f32[832,256]{1,0:T(8,128)S(1)} %get-tuple-element.44.exp_a), channel_id=1, source_target_pairs={{0,8},{1,9},{2,10},{3,11},{4,12},{5,13},{6,14},{7,15},{8,0},{9,1},... | collective-permute-start | bytes 2555912 | tf_op jit(solution)/shard_map/ppermute | solution.py:440
  209.2 21.9 %collective-permute-start.45 = (f32[832,256]{1,0:T(8,128)}, f32[832,256]{1,0:T(8,128)}, u32[]{:S(2)}, u32[]{:S(2)}) collective-permute-start(f32[832,256]{1,0:T(8,128)} %get-tuple-element.45.exp_b), channel_id=1, source_target_pairs={{0,16},{1,17},{2,18},{3,19},{4,20},{5,21},{6,22},{7,23},{8,24},{9,... | collective-permute-start | bytes 2555912 | tf_op jit(solution)/shard_map/ppermute | solution.py:440
  210.4 20.8 %collective-permute-start.46 = (f32[384,256]{1,0:T(8,128)}, f32[384,256]{1,0:T(8,128)}, u32[]{:S(2)}, u32[]{:S(2)}) collective-permute-start(f32[384,256]{1,0:T(8,128)} %get-tuple-element.46.exp_c), channel_id=1, source_target_pairs={{0,2},{1,3},{2,0},{3,1},{4,6},{5,7},{6,4},{7,5},{8,10},{9,11},{10,... | collective-permute-start | bytes 1179656 | tf_op jit(solution)/shard_map/ppermute | solution.py:440
  (55 other events, 973.1 us)

commit v4 on v3

--- a/solution.py
+++ b/solution.py
@@ -164,7 +164,7 @@
     out = []
     for i, ref in enumerate(ins):
         s, c = i % groups, i // groups
-        j = lax.rem(z - s + groups, groups) * 2 + (r if c == 0 else 1 - r)
+        j = jnp.bitwise_xor(z, s) * 2 + (r if c == 0 else 1 - r)
         for k in range(4):
             rows = pl.ds(pl.multiple_of(place(s, k) * quarter, quarter), quarter)
             out.append(pltpu.make_async_copy(ref.at[k], dst.at[j, rows], sem.at[i]))
@@ -204,7 +204,7 @@
             at = pl.ds(k * quarter, quarter)
             pltpu.make_async_copy(g_in[0].at[k], pg.at[0, at], sem.at[which, i]).wait()
         core = lax.div(i, groups)
-        column = lax.rem(ids[2] - lax.rem(i, groups) + groups, groups) * 2
+        column = jnp.bitwise_xor(ids[2], lax.rem(i, groups)) * 2
         return column + jnp.where(core == 0, ids[1], 1 - ids[1])
 
     def norm_body(i, acc):
@@ -472,7 +472,7 @@
     spread_own = weight_own[0] * jnp.sum(1.0 - diags[:, 0] ** 2 - diags[:, 1] ** 2) / order
 
     quarter = jax.ShapeDtypeStruct((size, size), jnp.float32)
-    d_by_z = {s: send(d_half, over_z(s)) for s in (1, 3, 2)}
+    d_by_z = {s: send(d_half, flip_z(s)) for s in (1, 3, 2)}
     terms = pl.pallas_call(
         term_kernel, out_shape=[quarter] * 4 + [jax.ShapeDtypeStruct((2, 5, size, size), jnp.float32)],
         in_specs=[SMEM, SMEM, VMEM, ANY, ANY], out_specs=[ANY] * 5,
@@ -493,7 +493,7 @@
     d_groups = d_groups + [send(g, core) for g in d_groups]
     g_by_z = {0: g_quarter}
     for s in (1, 3, 2):
-        g_by_z[s] = send(g_quarter, over_z(s))
+        g_by_z[s] = send(g_quarter, flip_z(s))
     g_groups = []
     for s in range(n_col):
         piece = g_by_z[s]

time: 269 us -> 270 us (level)
  transfers between devices with their start and end apart: 54 -> 54, of which waited for: 26 -> 31; matrix products, arithmetic and copies ran while one was open for 1% -> 1% of each run, Pallas kernels for 28% -> 28%
where the time goes in v4:
time: 270 us; the launch traced here: 269 us
  waiting for transfers between devices  108 us (40%)
  Pallas kernels  94.2 us (35%)
  starting transfers between devices  56.1 us (21%)
  local copies, waits for them, and re-layouts  6.46 us (2%)
    ppermute x54, waiting for transfers between devices, send(): return lax.ppermute(x, AXES, pairs)  108 us
    pallas_call x1, Pallas kernels, paired(): pl.pallas_call(solve_kernel, out_shape=[jax.ShapeDtypeStruct((8, 128), f3...  61.9 us
    ppermute x54, starting transfers between devices, send(): return lax.ppermute(x, AXES, pairs)  56.1 us
    pallas_call x1, Pallas kernels, paired(): t_in = trial(ids, *exp_in, *chosen_set)  8.87 us
    pallas_call x1, Pallas kernels, paired(): t_own = trial(ids, *exp_own, *chosen_set)  8.87 us
    pallas_call x1, Pallas kernels, paired(): grad, direction = outputs(ids, beta, dir_prev, *g_groups)  8.28 us
    unnamed x56, local copies, waits for them, and re-layouts  5.59 us
  transfers between devices with their start and end apart: 54, of which 31 were waited for; matrix products, arithmetic and copies ran while one was open for 1% of the time, Pallas kernels for 28%

profile of v4, /device:TPU:0, one launch (start us, length us, event | category | flops | bytes accessed | tf_op | source)
XLA Modules:
  0.0 269.4 jit_solution(245608785974830214)
XLA Ops:
  6.7 4.5 %collective-permute-done = f32[3,512]{1,0:T(4,128)S(1)} collective-permute-done((f32[3,512]{1,0:T(4,128)S(1)}, f32[3,512]{1,0:T(4,128)S(1)}, u32[]{:S(2)}, u32[]{:S(2)}) %collective-permute-start) | collective-permute-done | bytes 6176 | tf_op jit(solution)/shard_map/ppermute | solution.py:440
  12.2 5.0 %collective-permute-start.34 = (f32[2,256,256]{2,1,0:T(8,128)S(1)}, f32[2,256,256]{2,1,0:T(8,128)S(1)}, u32[]{:S(2)}, u32[]{:S(2)}) collective-permute-start(f32[2,256,256]{2,1,0:T(8,128)S(1)} %get-tuple-element.39), channel_id=1, source_target_pairs={{0,3},{1,2},{2,1},{3,0},{4,7},{5,6},{6,5},{7,4},{8,11},{9,10},{10,... | collective-permute-start | bytes 1572872 | tf_op jit(solution)/shard_map/ppermute | solution.py:440
  19.3 10.6 %collective-permute-done.4 = f32[3,512]{1,0:T(4,128)S(1)} collective-permute-done((f32[3,512]{1,0:T(4,128)S(1)}, f32[3,512]{1,0:T(4,128)S(1)}, u32[]{:S(2)}, u32[]{:S(2)}) %collective-permute-start.4) | collective-permute-done | bytes 6176 | tf_op jit(solution)/shard_map/ppermute | solution.py:440
  29.8 10.6 %collective-permute-start.31 = (f32[2,256,256]{2,1,0:T(8,128)S(1)}, f32[2,256,256]{2,1,0:T(8,128)S(1)}, u32[]{:S(2)}, u32[]{:S(2)}) collective-permute-start(f32[2,256,256]{2,1,0:T(8,128)S(1)} %get-tuple-element.39), channel_id=1, source_target_pairs={{0,2},{1,3},{2,0},{3,1},{4,6},{5,7},{6,4},{7,5},{8,10},{9,11},{10,... | collective-permute-start | bytes 1572872 | tf_op jit(solution)/shard_map/ppermute | solution.py:440
  43.4 2.8 %shard_map.94 = (f32[256,256]{1,0:T(8,128)S(1)}, f32[256,256]{1,0:T(8,128)S(1)}, f32[256,256]{1,0:T(8,128)S(1)}, f32[256,256]{1,0:T(8,128)S(1)}, f32[2,5,256,256]{3,2,1,0:T(8,128)}) custom-call(s32[5]{0:T(128)S(1)} %stack.146.ids, f32[4]{0:T(128)S(1)} %select_reduce_fusion.weight.weights, f32[4,3,512]{2,1,0:T(4,128)S(1)} %pad_maximum_fusion.4.diags, ...), custom_call_target="tpu_custom_call" | custom-call | flops 1000000000 | bytes 4194304 | tf_op jit(solution)/shard_map/pallas_call | solution.py:476
  48.3 14.8 %collective-permute-done.31 = f32[2,256,256]{2,1,0:T(8,128)S(1)} collective-permute-done((f32[2,256,256]{2,1,0:T(8,128)S(1)}, f32[2,256,256]{2,1,0:T(8,128)S(1)}, u32[]{:S(2)}, u32[]{:S(2)}) %collective-permute-start.31) | collective-permute-done | bytes 524320 | tf_op jit(solution)/shard_map/ppermute | solution.py:440
  68.2 4.9 %collective-permute-done.8 = f32[256,256]{1,0:T(8,128)S(1)} collective-permute-done((f32[256,256]{1,0:T(8,128)S(1)}, f32[256,256]{1,0:T(8,128)S(1)}, u32[]{:S(2)}, u32[]{:S(2)}) %collective-permute-start.8) | collective-permute-done | bytes 262176 | tf_op jit(solution)/shard_map/ppermute | solution.py:440
  78.8 3.0 %collective-permute-start.20 = (f32[256,256]{1,0:T(8,128)S(1)}, f32[256,256]{1,0:T(8,128)S(1)}, u32[]{:S(2)}, u32[]{:S(2)}) collective-permute-start(f32[256,256]{1,0:T(8,128)S(1)} %add_add_fusion), channel_id=1, source_target_pairs={{0,3},{1,2},{2,1},{3,0},{4,7},{5,6},{6,5},{7,4},{8,11},{9,10},{10,... | collective-permute-start | bytes 786440 | tf_op jit(solution)/shard_map/ppermute | solution.py:440
  81.8 2.6 collective-permute-done.32
  85.1 2.7 collective-permute-done.29
  90.3 11.0 %collective-permute-done.16 = f32[256,256]{1,0:T(8,128)S(1)} collective-permute-done((f32[256,256]{1,0:T(8,128)S(1)}, f32[256,256]{1,0:T(8,128)S(1)}, u32[]{:S(2)}, u32[]{:S(2)}) %collective-permute-start.16) | collective-permute-done | bytes 262176 | tf_op jit(solution)/shard_map/ppermute | solution.py:440
  106.0 4.4 %collective-permute-done.21 = f32[256,256]{1,0:T(8,128)S(1)} collective-permute-done((f32[256,256]{1,0:T(8,128)S(1)}, f32[256,256]{1,0:T(8,128)S(1)}, u32[]{:S(2)}, u32[]{:S(2)}) %collective-permute-start.21) | collective-permute-done | bytes 262176 | tf_op jit(solution)/shard_map/ppermute | solution.py:440
  113.6 4.0 %collective-permute-done.14 = f32[256,256]{1,0:T(8,128)S(1)} collective-permute-done((f32[256,256]{1,0:T(8,128)S(1)}, f32[256,256]{1,0:T(8,128)S(1)}, u32[]{:S(2)}, u32[]{:S(2)}) %collective-permute-start.14) | collective-permute-done | bytes 262176 | tf_op jit(solution)/shard_map/ppermute | solution.py:440
  118.1 5.1 %collective-permute-done.11 = f32[256,256]{1,0:T(8,128)S(1)} collective-permute-done((f32[256,256]{1,0:T(8,128)S(1)}, f32[256,256]{1,0:T(8,128)S(1)}, u32[]{:S(2)}, u32[]{:S(2)}) %collective-permute-start.11) | collective-permute-done | bytes 262176 | tf_op jit(solution)/shard_map/ppermute | solution.py:440
  126.6 5.8 %collective-permute-done.19 = f32[256,256]{1,0:T(8,128)S(1)} collective-permute-done((f32[256,256]{1,0:T(8,128)S(1)}, f32[256,256]{1,0:T(8,128)S(1)}, u32[]{:S(2)}, u32[]{:S(2)}) %collective-permute-start.19) | collective-permute-done | bytes 262176 | tf_op jit(solution)/shard_map/ppermute | solution.py:440
  133.0 4.2 %collective-permute-done.13 = f32[256,256]{1,0:T(8,128)S(1)} collective-permute-done((f32[256,256]{1,0:T(8,128)S(1)}, f32[256,256]{1,0:T(8,128)S(1)}, u32[]{:S(2)}, u32[]{:S(2)}) %collective-permute-start.13) | collective-permute-done | bytes 262176 | tf_op jit(solution)/shard_map/ppermute | solution.py:440
  137.1 2.8 %collective-permute-done.15 = f32[256,256]{1,0:T(8,128)S(1)} collective-permute-done((f32[256,256]{1,0:T(8,128)S(1)}, f32[256,256]{1,0:T(8,128)S(1)}, u32[]{:S(2)}, u32[]{:S(2)}) %collective-permute-start.15) | collective-permute-done | bytes 262176 | tf_op jit(solution)/shard_map/ppermute | solution.py:440
  148.1 61.9 %shard_map.95 = (f32[8,128]{1,0:T(8,128)S(1)}, f32[832,256]{1,0:T(8,128)S(1)}, f32[832,256]{1,0:T(8,128)}, f32[384,256]{1,0:T(8,128)}) custom-call(s32[5]{0:T(128)S(1)} %stack.146.ids, f32[1]{0:T(128)} %bitcast.10.prev_square, f32[4,256,256]{2,1,0:T(8,128)S(1)} %pad_maximum_fusion.refs_0_, f32[4,256,256]{2,1,0:T(8,128)S(1)} %pad_maximum_fusion.1.refs_1_, ...), custom_call_target="tpu_custom_call" | custom-call | flops 45097156608 | bytes 33554432 | tf_op jit(solution)/shard_map/pallas_call | solution.py:514
  213.6 8.3 %shard_map.97 = (f32[1024,512]{1,0:T(8,128)}, f32[1024,512]{1,0:T(8,128)}) custom-call(s32[5]{0:T(128)} %copy-done.9, f32[8,128]{1,0:T(8,128)} %copy-done.11, f32[1024,512]{1,0:T(8,128)} %dprev.1, f32[4,256,256]{2,1,0:T(8,128)} %copy-done.3, f32[4,256,256]{2,1,0:T(8,128)} %copy-done.6, f32[4,256,256]{2,1,0:T(8,128)} %copy-done.5, f32[4,256,256]{2,1,0:T(8,128)} %copy-done.4, ...), custom_call_target="tpu_custom_call" | custom-call | flops 1000000000 | bytes 16777216 | tf_op jit(solution)/shard_map/pallas_call | solution.py:532
  221.9 10.6 %collective-permute-done.46.exp_c = f32[384,256]{1,0:T(8,128)} collective-permute-done((f32[384,256]{1,0:T(8,128)}, f32[384,256]{1,0:T(8,128)}, u32[]{:S(2)}, u32[]{:S(2)}) %collective-permute-start.46) | collective-permute-done | bytes 393248 | tf_op jit(solution)/shard_map/ppermute | solution.py:440
  232.8 8.9 %shard_map.96 = f32[2,256]{1,0:T(2,128)S(1)} custom-call(s32[5]{0:T(128)S(1)} %copy-done.10, f32[832,256]{1,0:T(8,128)S(1)} %get-tuple-element.44.exp_a, f32[832,256]{1,0:T(8,128)} %get-tuple-element.45.exp_b, f32[384,256]{1,0:T(8,128)} %get-tuple-element.46.exp_c, f32[2,5,256,256]{3,2,1,0:T(8,128)} %get-tuple-element.43.m0, ...), custom_call_target="tpu_custom_call" | custom-call | flops 6442450944 | bytes 16777216 | tf_op jit(solution)/shard_map/pallas_call | solution.py:547
  241.7 8.9 %shard_map.98 = f32[2,256]{1,0:T(2,128)S(1)} custom-call(s32[5]{0:T(128)S(1)} %copy-done.10, f32[832,256]{1,0:T(8,128)S(1)} %collective-permute-done.44.exp_a, f32[832,256]{1,0:T(8,128)} %collective-permute-done.45.exp_b, f32[384,256]{1,0:T(8,128)} %collective-permute-done.46.exp_c, f32[2,5,256,256]{3,2,1,0:T(8,128)} %get-tuple-element.43.m0, ...), custom_call_target="tpu_custom_call" | custom-call | flops 6442450944 | bytes 16777216 | tf_op jit(solution)/shard_map/pallas_call | solution.py:549
  254.4 2.6 collective-permute-start.49
  257.3 2.5 collective-permute-done.49
  (175 shorter events, 64.4 us)
Async XLA Ops:
  0.6 42.7 %collective-permute-start.5 = (f32[2,1024,512]{2,1,0:T(8,128)}, f32[2,1024,512]{2,1,0:T(8,128)}, u32[]{:S(2)}, u32[]{:S(2)}) collective-permute-start(f32[2,1024,512]{2,1,0:T(8,128)} %bitcast.43), channel_id=1, source_target_pairs={{0,4},{1,5},{2,6},{3,7},{4,0},{5,1},{6,2},{7,3},{8,12},{9,13},{10,... | collective-permute-start | bytes 12582920 | tf_op jit(solution)/shard_map/ppermute | solution.py:440
  12.2 29.5 %collective-permute-start.34 = (f32[2,256,256]{2,1,0:T(8,128)S(1)}, f32[2,256,256]{2,1,0:T(8,128)S(1)}, u32[]{:S(2)}, u32[]{:S(2)}) collective-permute-start(f32[2,256,256]{2,1,0:T(8,128)S(1)} %get-tuple-element.39), channel_id=1, source_target_pairs={{0,3},{1,2},{2,1},{3,0},{4,7},{5,6},{6,5},{7,4},{8,11},{9,10},{10,... | collective-permute-start | bytes 1572872 | tf_op jit(solution)/shard_map/ppermute | solution.py:440
  17.3 23.7 %collective-permute-start.3 = (f32[3,512]{1,0:T(4,128)S(1)}, f32[3,512]{1,0:T(4,128)S(1)}, u32[]{:S(2)}, u32[]{:S(2)}) collective-permute-start(f32[3,512]{1,0:T(4,128)S(1)} %add.37), channel_id=1, source_target_pairs={{0,2},{1,3},{2,0},{3,1},{4,6},{5,7},{6,4},{7,5},{8,10},{9,11},{10,... | collective-permute-start | bytes 18440 | tf_op jit(solution)/shard_map/ppermute | solution.py:440
  18.2 23.4 %collective-permute-start.2 = (f32[3,512]{1,0:T(4,128)S(1)}, f32[3,512]{1,0:T(4,128)S(1)}, u32[]{:S(2)}, u32[]{:S(2)}) collective-permute-start(f32[3,512]{1,0:T(4,128)S(1)} %add.37), channel_id=1, source_target_pairs={{0,1},{1,2},{2,3},{3,0},{4,5},{5,6},{6,7},{7,4},{8,9},{9,10},{10,1... | collective-permute-start | bytes 18440 | tf_op jit(solution)/shard_map/ppermute | solution.py:440
  29.8 33.2 %collective-permute-start.31 = (f32[2,256,256]{2,1,0:T(8,128)S(1)}, f32[2,256,256]{2,1,0:T(8,128)S(1)}, u32[]{:S(2)}, u32[]{:S(2)}) collective-permute-start(f32[2,256,256]{2,1,0:T(8,128)S(1)} %get-tuple-element.39), channel_id=1, source_target_pairs={{0,2},{1,3},{2,0},{3,1},{4,6},{5,7},{6,4},{7,5},{8,10},{9,11},{10,... | collective-permute-start | bytes 1572872 | tf_op jit(solution)/shard_map/ppermute | solution.py:440
  41.0 24.5 %collective-permute-start.28 = (f32[2,256,256]{2,1,0:T(8,128)S(1)}, f32[2,256,256]{2,1,0:T(8,128)S(1)}, u32[]{:S(2)}, u32[]{:S(2)}) collective-permute-start(f32[2,256,256]{2,1,0:T(8,128)S(1)} %get-tuple-element.39), channel_id=1, source_target_pairs={{0,1},{1,0},{2,3},{3,2},{4,5},{5,4},{6,7},{7,6},{8,9},{9,8},{10,11... | collective-permute-start | bytes 1572872 | tf_op jit(solution)/shard_map/ppermute | solution.py:440
  41.8 33.0 %collective-permute-start.36 = (f32[1,256,256]{2,1,0:T(8,128)S(1)}, f32[1,256,256]{2,1,0:T(8,128)S(1)}, u32[]{:S(2)}, u32[]{:S(2)}) collective-permute-start(f32[1,256,256]{2,1,0:T(8,128)S(1)} %get-tuple-element.59), channel_id=1, source_target_pairs={{0,16},{1,17},{2,18},{3,19},{4,20},{5,21},{6,22},{7,23},{8,24},{9,... | collective-permute-start | bytes 786440 | tf_op jit(solution)/shard_map/ppermute | solution.py:440
  46.2 20.0 %collective-permute-start.6 = (f32[256,256]{1,0:T(8,128)S(1)}, f32[256,256]{1,0:T(8,128)S(1)}, u32[]{:S(2)}, u32[]{:S(2)}) collective-permute-start(f32[256,256]{1,0:T(8,128)S(1)} %get-tuple-element.35), channel_id=1, source_target_pairs={{0,8},{1,9},{2,10},{3,11},{4,12},{5,13},{6,14},{7,15},{8,0},{9,1},... | collective-permute-start | bytes 786440 | tf_op jit(solution)/shard_map/ppermute | solution.py:440
  47.8 19.0 %collective-permute-start.7 = (f32[256,256]{1,0:T(8,128)S(1)}, f32[256,256]{1,0:T(8,128)S(1)}, u32[]{:S(2)}, u32[]{:S(2)}) collective-permute-start(f32[256,256]{1,0:T(8,128)S(1)} %get-tuple-element.36), channel_id=1, source_target_pairs={{0,16},{1,17},{2,18},{3,19},{4,20},{5,21},{6,22},{7,23},{8,24},{9,... | collective-permute-start | bytes 786440 | tf_op jit(solution)/shard_map/ppermute | solution.py:440
  66.7 17.7 %collective-permute-start.32 = (f32[1,256,256]{2,1,0:T(8,128)S(1)}, f32[1,256,256]{2,1,0:T(8,128)S(1)}, u32[]{:S(2)}, u32[]{:S(2)}) collective-permute-start(f32[1,256,256]{2,1,0:T(8,128)S(1)} %get-tuple-element.62), channel_id=1, source_target_pairs={{0,8},{1,9},{2,10},{3,11},{4,12},{5,13},{6,14},{7,15},{8,0},{9,1},... | collective-permute-start | bytes 786440 | tf_op jit(solution)/shard_map/ppermute | solution.py:440
  81.8 19.5 %collective-permute-start.16 = (f32[256,256]{1,0:T(8,128)S(1)}, f32[256,256]{1,0:T(8,128)S(1)}, u32[]{:S(2)}, u32[]{:S(2)}) collective-permute-start(f32[256,256]{1,0:T(8,128)S(1)} %add_add_fusion), channel_id=1, source_target_pairs={{0,2},{1,3},{2,0},{3,1},{4,6},{5,7},{6,4},{7,5},{8,10},{9,11},{10,... | collective-permute-start | bytes 786440 | tf_op jit(solution)/shard_map/ppermute | solution.py:440
  84.4 18.4 %collective-permute-start.12 = (f32[256,256]{1,0:T(8,128)S(1)}, f32[256,256]{1,0:T(8,128)S(1)}, u32[]{:S(2)}, u32[]{:S(2)}) collective-permute-start(f32[256,256]{1,0:T(8,128)S(1)} %add_add_fusion), channel_id=1, source_target_pairs={{0,1},{1,0},{2,3},{3,2},{4,5},{5,4},{6,7},{7,6},{8,9},{9,8},{10,11... | collective-permute-start | bytes 786440 | tf_op jit(solution)/shard_map/ppermute | solution.py:440
  84.5 18.8 %collective-permute-start.10 = (f32[256,256]{1,0:T(8,128)S(1)}, f32[256,256]{1,0:T(8,128)S(1)}, u32[]{:S(2)}, u32[]{:S(2)}) collective-permute-start(f32[256,256]{1,0:T(8,128)S(1)} %add_add_fusion), channel_id=1, source_target_pairs={{0,16},{1,17},{2,18},{3,19},{4,20},{5,21},{6,22},{7,23},{8,24},{9,... | collective-permute-start | bytes 786440 | tf_op jit(solution)/shard_map/ppermute | solution.py:440
  87.8 16.1 %collective-permute-start.9 = (f32[256,256]{1,0:T(8,128)S(1)}, f32[256,256]{1,0:T(8,128)S(1)}, u32[]{:S(2)}, u32[]{:S(2)}) collective-permute-start(f32[256,256]{1,0:T(8,128)S(1)} %add_add_fusion), channel_id=1, source_target_pairs={{0,8},{1,9},{2,10},{3,11},{4,12},{5,13},{6,14},{7,15},{8,0},{9,1},... | collective-permute-start | bytes 786440 | tf_op jit(solution)/shard_map/ppermute | solution.py:440
  105.5 17.7 %collective-permute-start.11 = (f32[256,256]{1,0:T(8,128)S(1)}, f32[256,256]{1,0:T(8,128)S(1)}, u32[]{:S(2)}, u32[]{:S(2)}) collective-permute-start(f32[256,256]{1,0:T(8,128)S(1)} %collective-permute-done.9), channel_id=1, source_target_pairs={{0,16},{1,17},{2,18},{3,19},{4,20},{5,21},{6,22},{7,23},{8,24},{9,... | collective-permute-start | bytes 786440 | tf_op jit(solution)/shard_map/ppermute | solution.py:440
  110.5 29.6 %collective-permute-start.37 = (f32[4,256,256]{2,1,0:T(8,128)S(1)}, f32[4,256,256]{2,1,0:T(8,128)S(1)}, u32[]{:S(2)}, u32[]{:S(2)}) collective-permute-start(f32[4,256,256]{2,1,0:T(8,128)S(1)} %get-tuple-element.38.refs_8_), channel_id=1, source_target_pairs={{0,4},{1,5},{2,6},{3,7},{4,0},{5,1},{6,2},{7,3},{8,12},{9,13},{10,... | collective-permute-start | bytes 3145736 | tf_op jit(solution)/shard_map/ppermute | solution.py:440
  112.0 28.7 %collective-permute-start.38 = (f32[4,256,256]{2,1,0:T(8,128)S(1)}, f32[4,256,256]{2,1,0:T(8,128)S(1)}, u32[]{:S(2)}, u32[]{:S(2)}) collective-permute-start(f32[4,256,256]{2,1,0:T(8,128)S(1)} %constant_dynamic-update-slice_fusion.refs_9_), channel_id=1, source_target_pairs={{0,4},{1,5},{2,6},{3,7},{4,0},{5,1},{6,2},{7,3},{8,12},{9,13},{10,... | collective-permute-start | bytes 3145736 | tf_op jit(solution)/shard_map/ppermute | solution.py:440
  113.6 27.2 %collective-permute-start.39 = (f32[4,256,256]{2,1,0:T(8,128)S(1)}, f32[4,256,256]{2,1,0:T(8,128)S(1)}, u32[]{:S(2)}, u32[]{:S(2)}) collective-permute-start(f32[4,256,256]{2,1,0:T(8,128)S(1)} %constant_dynamic-update-slice_fusion.3.refs_10_), channel_id=1, source_target_pairs={{0,4},{1,5},{2,6},{3,7},{4,0},{5,1},{6,2},{7,3},{8,12},{9,13},{10,... | collective-permute-start | bytes 3145736 | tf_op jit(solution)/shard_map/ppermute | solution.py:440
  141.9 90.9 %collective-permute-start.42 = (f32[2,5,256,256]{3,2,1,0:T(8,128)}, f32[2,5,256,256]{3,2,1,0:T(8,128)}, u32[]{:S(2)}, u32[]{:S(2)}) collective-permute-start(f32[2,5,256,256]{3,2,1,0:T(8,128)} %get-tuple-element.43.m0), channel_id=1, source_target_pairs={{0,4},{1,5},{2,6},{3,7},{4,0},{5,1},{6,2},{7,3},{8,12},{9,13},{10,... | collective-permute-start | bytes 7864328 | tf_op jit(solution)/shard_map/ppermute | solution.py:440
  142.6 68.1 %collective-permute-start.41 = (f32[2,5,256,256]{3,2,1,0:T(8,128)}, f32[2,5,256,256]{3,2,1,0:T(8,128)}, u32[]{:S(2)}, u32[]{:S(2)}) collective-permute-start(f32[2,5,256,256]{3,2,1,0:T(8,128)} %get-tuple-element.43.m0), channel_id=1, source_target_pairs={{0,1},{1,0},{2,3},{3,2},{4,5},{5,4},{6,7},{7,6},{8,9},{9,8},{10,11... | collective-permute-start | bytes 7864328 | tf_op jit(solution)/shard_map/ppermute | solution.py:440
  210.7 22.1 %collective-permute-start.43 = (f32[2,5,256,256]{3,2,1,0:T(8,128)}, f32[2,5,256,256]{3,2,1,0:T(8,128)}, u32[]{:S(2)}, u32[]{:S(2)}) collective-permute-start(f32[2,5,256,256]{3,2,1,0:T(8,128)} %collective-permute-done.41.m2), channel_id=1, source_target_pairs={{0,4},{1,5},{2,6},{3,7},{4,0},{5,1},{6,2},{7,3},{8,12},{9,13},{10,... | collective-permute-start | bytes 7864328 | tf_op jit(solution)/shard_map/ppermute | solution.py:440
  210.8 21.7 %collective-permute-start.44 = (f32[832,256]{1,0:T(8,128)S(1)}, f32[832,256]{1,0:T(8,128)S(1)}, u32[]{:S(2)}, u32[]{:S(2)}) collective-permute-start(f32[832,256]{1,0:T(8,128)S(1)} %get-tuple-element.44.exp_a), channel_id=1, source_target_pairs={{0,8},{1,9},{2,10},{3,11},{4,12},{5,13},{6,14},{7,15},{8,0},{9,1},... | collective-permute-start | bytes 2555912 | tf_op jit(solution)/shard_map/ppermute | solution.py:440
  211.5 21.3 %collective-permute-start.45 = (f32[832,256]{1,0:T(8,128)}, f32[832,256]{1,0:T(8,128)}, u32[]{:S(2)}, u32[]{:S(2)}) collective-permute-start(f32[832,256]{1,0:T(8,128)} %get-tuple-element.45.exp_b), channel_id=1, source_target_pairs={{0,16},{1,17},{2,18},{3,19},{4,20},{5,21},{6,22},{7,23},{8,24},{9,... | collective-permute-start | bytes 2555912 | tf_op jit(solution)/shard_map/ppermute | solution.py:440
  212.0 20.5 %collective-permute-start.46 = (f32[384,256]{1,0:T(8,128)}, f32[384,256]{1,0:T(8,128)}, u32[]{:S(2)}, u32[]{:S(2)}) collective-permute-start(f32[384,256]{1,0:T(8,128)} %get-tuple-element.46.exp_c), channel_id=1, source_target_pairs={{0,2},{1,3},{2,0},{3,1},{4,6},{5,7},{6,4},{7,5},{8,10},{9,11},{10,... | collective-permute-start | bytes 1179656 | tf_op jit(solution)/shard_map/ppermute | solution.py:440
  (55 other events, 1024.5 us)

commit v5 on v4

--- a/solution.py
+++ b/solution.py
@@ -310,16 +310,25 @@
 
 
 def output_kernel(ids, beta, dprev, *refs):
-    g_in = refs[:-4]
-    grad_out, dir_out, pg, sem = refs[-4:]
+    g_in = refs[:-8]
+    grad_to, dir_to, pg, prev, grad_out, dir_out, sem, out_sem = refs[-8:]
     r, z = ids[1], ids[2]
     blocks, _, size = pg.shape
     per_core = grad_out.shape[0] // size
     per_chip = grad_out.shape[1] // size
-    for c in group_copies(ids, g_in, pg, sem, terms_place(ids)):
-        c.start()
-    for c in group_copies(ids, g_in, pg, sem, terms_place(ids)):
-        c.wait()
+    groups = len(g_in) // 2
+    prev_copy = pltpu.make_async_copy(dprev, prev, out_sem.at[2, 0])
+    copies = group_copies(ids, g_in, pg, sem, terms_place(ids))
+
+    def needed(n):
+        return jnp.bitwise_xor(z, n // 4 % groups) != lax.rem(z + 1, groups)
+
+    for n, c in enumerate(copies):
+        pl.when(needed(n))(c.start)
+    prev_copy.start()
+    for n, c in enumerate(copies):
+        pl.when(needed(n))(c.wait)
+    prev_copy.wait()
 
     def out_body(t, carry):
         i, jx = lax.div(t, per_chip), lax.rem(t, per_chip)
@@ -352,10 +361,18 @@
         def _():
             grad_out[rows, cols] = jnp.concatenate([-pg[rb, 7 * n:, :], pg[cb, 7 * n:, :]], axis=0).T
 
-        dir_out[rows, cols] = beta[0:1, 0:1] * dprev[rows, cols] - grad_out[rows, cols]
+        dir_out[rows, cols] = beta[0:1, 0:1] * prev[rows, cols] - grad_out[rows, cols]
+        pltpu.make_async_copy(grad_out.at[rows, cols], grad_to.at[rows, cols], out_sem.at[0, t]).start()
+        pltpu.make_async_copy(dir_out.at[rows, cols], dir_to.at[rows, cols], out_sem.at[1, t]).start()
         return carry
 
-    lax.fori_loop(0, per_core * per_chip, out_body, 0)
+    count = per_core * per_chip
+    lax.fori_loop(0, count, out_body, 0)
+    for t in range(count):
+        rows = pl.ds(t // per_chip * size, size)
+        cols = pl.ds(t % per_chip * size, size)
+        pltpu.make_async_copy(grad_out.at[rows, cols], grad_to.at[rows, cols], out_sem.at[0, t]).wait()
+        pltpu.make_async_copy(dir_out.at[rows, cols], dir_to.at[rows, cols], out_sem.at[1, t]).wait()
 
 
 def trial_kernel(ids, exp_a, exp_b, exp_c, m0, m1, m2, m3, out, e, ehi, elo, mbuf, sem):
@@ -509,7 +526,7 @@
 
     f32 = jnp.float32
     held = pltpu.VMEM((2 * n_col, 4 * size, size), f32)
-    by_plane = 13 * order // 32 // 8 * 8
+    by_plane = 27 * order // 64 // 8 * 8
     shares = (by_plane, by_plane, order - 2 * by_plane)
     beta, *exp_own = pl.pallas_call(
         solve_kernel,
@@ -524,8 +541,9 @@
     )(ids, prev_square, *g_groups, *d_groups)
     outputs = pl.pallas_call(
         output_kernel, out_shape=[jax.ShapeDtypeStruct((local_rows, local_cols), f32)] * 2,
-        in_specs=[SMEM, VMEM, VMEM] + [ANY] * (2 * n_col), out_specs=[VMEM] * 2,
-        scratch_shapes=[held, pltpu.SemaphoreType.DMA((2 * n_col,))],
+        in_specs=[SMEM, VMEM, ANY] + [ANY] * (2 * n_col), out_specs=[ANY] * 2,
+        scratch_shapes=[held] + [pltpu.VMEM((local_rows, local_cols), f32)] * 3 + [
+            pltpu.SemaphoreType.DMA((2 * n_col,)), pltpu.SemaphoreType.DMA((3, 2 * n_col))],
         compiler_params=pltpu.CompilerParams(vmem_limit_bytes=VMEM_LIMIT),
         cost_estimate=pl.CostEstimate(flops=10**9, bytes_accessed=1 << 24, transcendentals=0),
     )

time: 270 us -> 270 us (level)
  transfers between devices with their start and end apart: 54 -> 54, of which waited for: 31 -> 32; matrix products, arithmetic and copies ran while one was open for 1% -> 1% of each run, Pallas kernels for 28% -> 27%
where the time goes in v5:
time: 270 us
  waiting for transfers between devices  110 us (41%)
  Pallas kernels  92.7 us (34%)
  starting transfers between devices  56.1 us (21%)
  local copies, waits for them, and re-layouts  6.45 us (2%)
    ppermute x54, waiting for transfers between devices, send(): return lax.ppermute(x, AXES, pairs)  110 us
    pallas_call x1, Pallas kernels, paired(): pl.pallas_call(solve_kernel, out_shape=[jax.ShapeDtypeStruct((8, 128), f3...  61.9 us
    ppermute x54, starting transfers between devices, send(): return lax.ppermute(x, AXES, pairs)  56.1 us
    pallas_call x1, Pallas kernels, paired(): t_own = trial(ids, *exp_own, *chosen_set)  8.86 us
    pallas_call x1, Pallas kernels, paired(): t_in = trial(ids, *exp_in, *chosen_set)  8.86 us
    pallas_call x1, Pallas kernels, paired(): grad, direction = outputs(ids, beta, dir_prev, *g_groups)  6.81 us
    unnamed x56, local copies, waits for them, and re-layouts  5.58 us
  transfers between devices with their start and end apart: 54, of which 32 were waited for; matrix products, arithmetic and copies ran while one was open for 1% of the time, Pallas kernels for 27%

profile of v5, /device:TPU:0, one launch (start us, length us, event | category | flops | bytes accessed | tf_op | source)
XLA Modules:
  0.0 270.0 jit_solution(10781043062972198342)
XLA Ops:
  6.7 4.5 %collective-permute-done = f32[3,512]{1,0:T(4,128)S(1)} collective-permute-done((f32[3,512]{1,0:T(4,128)S(1)}, f32[3,512]{1,0:T(4,128)S(1)}, u32[]{:S(2)}, u32[]{:S(2)}) %collective-permute-start) | collective-permute-done | bytes 6176 | tf_op jit(solution)/shard_map/ppermute | solution.py:457
  12.2 5.0 %collective-permute-start.34 = (f32[2,256,256]{2,1,0:T(8,128)S(1)}, f32[2,256,256]{2,1,0:T(8,128)S(1)}, u32[]{:S(2)}, u32[]{:S(2)}) collective-permute-start(f32[2,256,256]{2,1,0:T(8,128)S(1)} %get-tuple-element.39), channel_id=1, source_target_pairs={{0,3},{1,2},{2,1},{3,0},{4,7},{5,6},{6,5},{7,4},{8,11},{9,10},{10,... | collective-permute-start | bytes 1572872 | tf_op jit(solution)/shard_map/ppermute | solution.py:457
  19.3 10.6 %collective-permute-done.4 = f32[3,512]{1,0:T(4,128)S(1)} collective-permute-done((f32[3,512]{1,0:T(4,128)S(1)}, f32[3,512]{1,0:T(4,128)S(1)}, u32[]{:S(2)}, u32[]{:S(2)}) %collective-permute-start.4) | collective-permute-done | bytes 6176 | tf_op jit(solution)/shard_map/ppermute | solution.py:457
  29.8 10.6 %collective-permute-start.31 = (f32[2,256,256]{2,1,0:T(8,128)S(1)}, f32[2,256,256]{2,1,0:T(8,128)S(1)}, u32[]{:S(2)}, u32[]{:S(2)}) collective-permute-start(f32[2,256,256]{2,1,0:T(8,128)S(1)} %get-tuple-element.39), channel_id=1, source_target_pairs={{0,2},{1,3},{2,0},{3,1},{4,6},{5,7},{6,4},{7,5},{8,10},{9,11},{10,... | collective-permute-start | bytes 1572872 | tf_op jit(solution)/shard_map/ppermute | solution.py:457
  43.4 2.8 %shard_map.94 = (f32[256,256]{1,0:T(8,128)S(1)}, f32[256,256]{1,0:T(8,128)S(1)}, f32[256,256]{1,0:T(8,128)S(1)}, f32[256,256]{1,0:T(8,128)S(1)}, f32[2,5,256,256]{3,2,1,0:T(8,128)}) custom-call(s32[5]{0:T(128)S(1)} %stack.146.ids, f32[4]{0:T(128)S(1)} %select_reduce_fusion.weight.weights, f32[4,3,512]{2,1,0:T(4,128)S(1)} %pad_maximum_fusion.4.diags, ...), custom_call_target="tpu_custom_call" | custom-call | flops 1000000000 | bytes 4194304 | tf_op jit(solution)/shard_map/pallas_call | solution.py:493
  48.3 14.8 %collective-permute-done.31 = f32[2,256,256]{2,1,0:T(8,128)S(1)} collective-permute-done((f32[2,256,256]{2,1,0:T(8,128)S(1)}, f32[2,256,256]{2,1,0:T(8,128)S(1)}, u32[]{:S(2)}, u32[]{:S(2)}) %collective-permute-start.31) | collective-permute-done | bytes 524320 | tf_op jit(solution)/shard_map/ppermute | solution.py:457
  68.2 4.9 %collective-permute-done.8 = f32[256,256]{1,0:T(8,128)S(1)} collective-permute-done((f32[256,256]{1,0:T(8,128)S(1)}, f32[256,256]{1,0:T(8,128)S(1)}, u32[]{:S(2)}, u32[]{:S(2)}) %collective-permute-start.8) | collective-permute-done | bytes 262176 | tf_op jit(solution)/shard_map/ppermute | solution.py:457
  78.8 3.0 %collective-permute-start.20 = (f32[256,256]{1,0:T(8,128)S(1)}, f32[256,256]{1,0:T(8,128)S(1)}, u32[]{:S(2)}, u32[]{:S(2)}) collective-permute-start(f32[256,256]{1,0:T(8,128)S(1)} %add_add_fusion), channel_id=1, source_target_pairs={{0,3},{1,2},{2,1},{3,0},{4,7},{5,6},{6,5},{7,4},{8,11},{9,10},{10,... | collective-permute-start | bytes 786440 | tf_op jit(solution)/shard_map/ppermute | solution.py:457
  81.8 2.6 collective-permute-done.32
  85.1 2.7 collective-permute-done.29
  90.3 11.0 %collective-permute-done.16 = f32[256,256]{1,0:T(8,128)S(1)} collective-permute-done((f32[256,256]{1,0:T(8,128)S(1)}, f32[256,256]{1,0:T(8,128)S(1)}, u32[]{:S(2)}, u32[]{:S(2)}) %collective-permute-start.16) | collective-permute-done | bytes 262176 | tf_op jit(solution)/shard_map/ppermute | solution.py:457
  106.0 4.4 %collective-permute-done.21 = f32[256,256]{1,0:T(8,128)S(1)} collective-permute-done((f32[256,256]{1,0:T(8,128)S(1)}, f32[256,256]{1,0:T(8,128)S(1)}, u32[]{:S(2)}, u32[]{:S(2)}) %collective-permute-start.21) | collective-permute-done | bytes 262176 | tf_op jit(solution)/shard_map/ppermute | solution.py:457
  113.6 4.0 %collective-permute-done.14 = f32[256,256]{1,0:T(8,128)S(1)} collective-permute-done((f32[256,256]{1,0:T(8,128)S(1)}, f32[256,256]{1,0:T(8,128)S(1)}, u32[]{:S(2)}, u32[]{:S(2)}) %collective-permute-start.14) | collective-permute-done | bytes 262176 | tf_op jit(solution)/shard_map/ppermute | solution.py:457
  118.1 5.1 %collective-permute-done.11 = f32[256,256]{1,0:T(8,128)S(1)} collective-permute-done((f32[256,256]{1,0:T(8,128)S(1)}, f32[256,256]{1,0:T(8,128)S(1)}, u32[]{:S(2)}, u32[]{:S(2)}) %collective-permute-start.11) | collective-permute-done | bytes 262176 | tf_op jit(solution)/shard_map/ppermute | solution.py:457
  126.6 5.8 %collective-permute-done.19 = f32[256,256]{1,0:T(8,128)S(1)} collective-permute-done((f32[256,256]{1,0:T(8,128)S(1)}, f32[256,256]{1,0:T(8,128)S(1)}, u32[]{:S(2)}, u32[]{:S(2)}) %collective-permute-start.19) | collective-permute-done | bytes 262176 | tf_op jit(solution)/shard_map/ppermute | solution.py:457
  133.0 4.2 %collective-permute-done.13 = f32[256,256]{1,0:T(8,128)S(1)} collective-permute-done((f32[256,256]{1,0:T(8,128)S(1)}, f32[256,256]{1,0:T(8,128)S(1)}, u32[]{:S(2)}, u32[]{:S(2)}) %collective-permute-start.13) | collective-permute-done | bytes 262176 | tf_op jit(solution)/shard_map/ppermute | solution.py:457
  137.1 2.8 %collective-permute-done.15 = f32[256,256]{1,0:T(8,128)S(1)} collective-permute-done((f32[256,256]{1,0:T(8,128)S(1)}, f32[256,256]{1,0:T(8,128)S(1)}, u32[]{:S(2)}, u32[]{:S(2)}) %collective-permute-start.15) | collective-permute-done | bytes 262176 | tf_op jit(solution)/shard_map/ppermute | solution.py:457
  148.1 61.9 %shard_map.95 = (f32[8,128]{1,0:T(8,128)S(1)}, f32[864,256]{1,0:T(8,128)S(1)}, f32[864,256]{1,0:T(8,128)}, f32[320,256]{1,0:T(8,128)}) custom-call(s32[5]{0:T(128)S(1)} %stack.146.ids, f32[1]{0:T(128)} %bitcast.10.prev_square, f32[4,256,256]{2,1,0:T(8,128)S(1)} %pad_maximum_fusion.refs_0_, f32[4,256,256]{2,1,0:T(8,128)S(1)} %pad_maximum_fusion.1.refs_1_, ...), custom_call_target="tpu_custom_call" | custom-call | flops 45097156608 | bytes 33554432 | tf_op jit(solution)/shard_map/pallas_call | solution.py:531
  213.6 6.8 %shard_map.97 = (f32[1024,512]{1,0:T(8,128)}, f32[1024,512]{1,0:T(8,128)}) custom-call(s32[5]{0:T(128)} %copy-done.9, f32[8,128]{1,0:T(8,128)} %copy-done.11, f32[1024,512]{1,0:T(8,128)} %dprev.1, f32[4,256,256]{2,1,0:T(8,128)} %copy-done.3, f32[4,256,256]{2,1,0:T(8,128)} %copy-done.6, f32[4,256,256]{2,1,0:T(8,128)} %copy-done.5, f32[4,256,256]{2,1,0:T(8,128)} %copy-done.4, ...), custom_call_target="tpu_custom_call" | custom-call | flops 1000000000 | bytes 16777216 | tf_op jit(solution)/shard_map/pallas_call | solution.py:550
  220.4 9.3 %collective-permute-done.46.exp_c = f32[320,256]{1,0:T(8,128)} collective-permute-done((f32[320,256]{1,0:T(8,128)}, f32[320,256]{1,0:T(8,128)}, u32[]{:S(2)}, u32[]{:S(2)}) %collective-permute-start.46) | collective-permute-done | bytes 327712 | tf_op jit(solution)/shard_map/ppermute | solution.py:457
  229.7 3.1 %collective-permute-done.44.exp_a = f32[864,256]{1,0:T(8,128)S(1)} collective-permute-done((f32[864,256]{1,0:T(8,128)S(1)}, f32[864,256]{1,0:T(8,128)S(1)}, u32[]{:S(2)}, u32[]{:S(2)}) %collective-permute-start.44) | collective-permute-done | bytes 884768 | tf_op jit(solution)/shard_map/ppermute | solution.py:457
  233.5 8.9 %shard_map.96 = f32[2,256]{1,0:T(2,128)S(1)} custom-call(s32[5]{0:T(128)S(1)} %copy-done.10, f32[864,256]{1,0:T(8,128)S(1)} %get-tuple-element.44.exp_a, f32[864,256]{1,0:T(8,128)} %get-tuple-element.45.exp_b, f32[320,256]{1,0:T(8,128)} %get-tuple-element.46.exp_c, f32[2,5,256,256]{3,2,1,0:T(8,128)} %get-tuple-element.43.m0, ...), custom_call_target="tpu_custom_call" | custom-call | flops 6442450944 | bytes 16777216 | tf_op jit(solution)/shard_map/pallas_call | solution.py:565
  242.3 8.9 %shard_map.98 = f32[2,256]{1,0:T(2,128)S(1)} custom-call(s32[5]{0:T(128)S(1)} %copy-done.10, f32[864,256]{1,0:T(8,128)S(1)} %collective-permute-done.44.exp_a, f32[864,256]{1,0:T(8,128)} %collective-permute-done.45.exp_b, f32[320,256]{1,0:T(8,128)} %collective-permute-done.46.exp_c, f32[2,5,256,256]{3,2,1,0:T(8,128)} %get-tuple-element.43.m0, ...), custom_call_target="tpu_custom_call" | custom-call | flops 6442450944 | bytes 16777216 | tf_op jit(solution)/shard_map/pallas_call | solution.py:567
  255.1 2.6 collective-permute-start.49
  (175 shorter events, 67.4 us)
Async XLA Ops:
  0.6 42.7 %collective-permute-start.5 = (f32[2,1024,512]{2,1,0:T(8,128)}, f32[2,1024,512]{2,1,0:T(8,128)}, u32[]{:S(2)}, u32[]{:S(2)}) collective-permute-start(f32[2,1024,512]{2,1,0:T(8,128)} %bitcast.43), channel_id=1, source_target_pairs={{0,4},{1,5},{2,6},{3,7},{4,0},{5,1},{6,2},{7,3},{8,12},{9,13},{10,... | collective-permute-start | bytes 12582920 | tf_op jit(solution)/shard_map/ppermute | solution.py:457
  12.2 29.5 %collective-permute-start.34 = (f32[2,256,256]{2,1,0:T(8,128)S(1)}, f32[2,256,256]{2,1,0:T(8,128)S(1)}, u32[]{:S(2)}, u32[]{:S(2)}) collective-permute-start(f32[2,256,256]{2,1,0:T(8,128)S(1)} %get-tuple-element.39), channel_id=1, source_target_pairs={{0,3},{1,2},{2,1},{3,0},{4,7},{5,6},{6,5},{7,4},{8,11},{9,10},{10,... | collective-permute-start | bytes 1572872 | tf_op jit(solution)/shard_map/ppermute | solution.py:457
  17.3 23.7 %collective-permute-start.3 = (f32[3,512]{1,0:T(4,128)S(1)}, f32[3,512]{1,0:T(4,128)S(1)}, u32[]{:S(2)}, u32[]{:S(2)}) collective-permute-start(f32[3,512]{1,0:T(4,128)S(1)} %add.37), channel_id=1, source_target_pairs={{0,2},{1,3},{2,0},{3,1},{4,6},{5,7},{6,4},{7,5},{8,10},{9,11},{10,... | collective-permute-start | bytes 18440 | tf_op jit(solution)/shard_map/ppermute | solution.py:457
  18.2 23.4 %collective-permute-start.2 = (f32[3,512]{1,0:T(4,128)S(1)}, f32[3,512]{1,0:T(4,128)S(1)}, u32[]{:S(2)}, u32[]{:S(2)}) collective-permute-start(f32[3,512]{1,0:T(4,128)S(1)} %add.37), channel_id=1, source_target_pairs={{0,1},{1,2},{2,3},{3,0},{4,5},{5,6},{6,7},{7,4},{8,9},{9,10},{10,1... | collective-permute-start | bytes 18440 | tf_op jit(solution)/shard_map/ppermute | solution.py:457
  29.8 33.2 %collective-permute-start.31 = (f32[2,256,256]{2,1,0:T(8,128)S(1)}, f32[2,256,256]{2,1,0:T(8,128)S(1)}, u32[]{:S(2)}, u32[]{:S(2)}) collective-permute-start(f32[2,256,256]{2,1,0:T(8,128)S(1)} %get-tuple-element.39), channel_id=1, source_target_pairs={{0,2},{1,3},{2,0},{3,1},{4,6},{5,7},{6,4},{7,5},{8,10},{9,11},{10,... | collective-permute-start | bytes 1572872 | tf_op jit(solution)/shard_map/ppermute | solution.py:457
  41.0 24.5 %collective-permute-start.28 = (f32[2,256,256]{2,1,0:T(8,128)S(1)}, f32[2,256,256]{2,1,0:T(8,128)S(1)}, u32[]{:S(2)}, u32[]{:S(2)}) collective-permute-start(f32[2,256,256]{2,1,0:T(8,128)S(1)} %get-tuple-element.39), channel_id=1, source_target_pairs={{0,1},{1,0},{2,3},{3,2},{4,5},{5,4},{6,7},{7,6},{8,9},{9,8},{10,11... | collective-permute-start | bytes 1572872 | tf_op jit(solution)/shard_map/ppermute | solution.py:457
  41.8 33.0 %collective-permute-start.36 = (f32[1,256,256]{2,1,0:T(8,128)S(1)}, f32[1,256,256]{2,1,0:T(8,128)S(1)}, u32[]{:S(2)}, u32[]{:S(2)}) collective-permute-start(f32[1,256,256]{2,1,0:T(8,128)S(1)} %get-tuple-element.59), channel_id=1, source_target_pairs={{0,16},{1,17},{2,18},{3,19},{4,20},{5,21},{6,22},{7,23},{8,24},{9,... | collective-permute-start | bytes 786440 | tf_op jit(solution)/shard_map/ppermute | solution.py:457
  46.2 20.0 %collective-permute-start.6 = (f32[256,256]{1,0:T(8,128)S(1)}, f32[256,256]{1,0:T(8,128)S(1)}, u32[]{:S(2)}, u32[]{:S(2)}) collective-permute-start(f32[256,256]{1,0:T(8,128)S(1)} %get-tuple-element.35), channel_id=1, source_target_pairs={{0,8},{1,9},{2,10},{3,11},{4,12},{5,13},{6,14},{7,15},{8,0},{9,1},... | collective-permute-start | bytes 786440 | tf_op jit(solution)/shard_map/ppermute | solution.py:457
  47.8 19.0 %collective-permute-start.7 = (f32[256,256]{1,0:T(8,128)S(1)}, f32[256,256]{1,0:T(8,128)S(1)}, u32[]{:S(2)}, u32[]{:S(2)}) collective-permute-start(f32[256,256]{1,0:T(8,128)S(1)} %get-tuple-element.36), channel_id=1, source_target_pairs={{0,16},{1,17},{2,18},{3,19},{4,20},{5,21},{6,22},{7,23},{8,24},{9,... | collective-permute-start | bytes 786440 | tf_op jit(solution)/shard_map/ppermute | solution.py:457
  66.7 17.7 %collective-permute-start.32 = (f32[1,256,256]{2,1,0:T(8,128)S(1)}, f32[1,256,256]{2,1,0:T(8,128)S(1)}, u32[]{:S(2)}, u32[]{:S(2)}) collective-permute-start(f32[1,256,256]{2,1,0:T(8,128)S(1)} %get-tuple-element.62), channel_id=1, source_target_pairs={{0,8},{1,9},{2,10},{3,11},{4,12},{5,13},{6,14},{7,15},{8,0},{9,1},... | collective-permute-start | bytes 786440 | tf_op jit(solution)/shard_map/ppermute | solution.py:457
  81.8 19.5 %collective-permute-start.16 = (f32[256,256]{1,0:T(8,128)S(1)}, f32[256,256]{1,0:T(8,128)S(1)}, u32[]{:S(2)}, u32[]{:S(2)}) collective-permute-start(f32[256,256]{1,0:T(8,128)S(1)} %add_add_fusion), channel_id=1, source_target_pairs={{0,2},{1,3},{2,0},{3,1},{4,6},{5,7},{6,4},{7,5},{8,10},{9,11},{10,... | collective-permute-start | bytes 786440 | tf_op jit(solution)/shard_map/ppermute | solution.py:457
  84.4 18.4 %collective-permute-start.12 = (f32[256,256]{1,0:T(8,128)S(1)}, f32[256,256]{1,0:T(8,128)S(1)}, u32[]{:S(2)}, u32[]{:S(2)}) collective-permute-start(f32[256,256]{1,0:T(8,128)S(1)} %add_add_fusion), channel_id=1, source_target_pairs={{0,1},{1,0},{2,3},{3,2},{4,5},{5,4},{6,7},{7,6},{8,9},{9,8},{10,11... | collective-permute-start | bytes 786440 | tf_op jit(solution)/shard_map/ppermute | solution.py:457
  84.5 18.8 %collective-permute-start.10 = (f32[256,256]{1,0:T(8,128)S(1)}, f32[256,256]{1,0:T(8,128)S(1)}, u32[]{:S(2)}, u32[]{:S(2)}) collective-permute-start(f32[256,256]{1,0:T(8,128)S(1)} %add_add_fusion), channel_id=1, source_target_pairs={{0,16},{1,17},{2,18},{3,19},{4,20},{5,21},{6,22},{7,23},{8,24},{9,... | collective-permute-start | bytes 786440 | tf_op jit(solution)/shard_map/ppermute | solution.py:457
  87.8 16.1 %collective-permute-start.9 = (f32[256,256]{1,0:T(8,128)S(1)}, f32[256,256]{1,0:T(8,128)S(1)}, u32[]{:S(2)}, u32[]{:S(2)}) collective-permute-start(f32[256,256]{1,0:T(8,128)S(1)} %add_add_fusion), channel_id=1, source_target_pairs={{0,8},{1,9},{2,10},{3,11},{4,12},{5,13},{6,14},{7,15},{8,0},{9,1},... | collective-permute-start | bytes 786440 | tf_op jit(solution)/shard_map/ppermute | solution.py:457
  105.5 17.7 %collective-permute-start.11 = (f32[256,256]{1,0:T(8,128)S(1)}, f32[256,256]{1,0:T(8,128)S(1)}, u32[]{:S(2)}, u32[]{:S(2)}) collective-permute-start(f32[256,256]{1,0:T(8,128)S(1)} %collective-permute-done.9), channel_id=1, source_target_pairs={{0,16},{1,17},{2,18},{3,19},{4,20},{5,21},{6,22},{7,23},{8,24},{9,... | collective-permute-start | bytes 786440 | tf_op jit(solution)/shard_map/ppermute | solution.py:457
  110.5 29.6 %collective-permute-start.37 = (f32[4,256,256]{2,1,0:T(8,128)S(1)}, f32[4,256,256]{2,1,0:T(8,128)S(1)}, u32[]{:S(2)}, u32[]{:S(2)}) collective-permute-start(f32[4,256,256]{2,1,0:T(8,128)S(1)} %get-tuple-element.38.refs_8_), channel_id=1, source_target_pairs={{0,4},{1,5},{2,6},{3,7},{4,0},{5,1},{6,2},{7,3},{8,12},{9,13},{10,... | collective-permute-start | bytes 3145736 | tf_op jit(solution)/shard_map/ppermute | solution.py:457
  112.0 28.7 %collective-permute-start.38 = (f32[4,256,256]{2,1,0:T(8,128)S(1)}, f32[4,256,256]{2,1,0:T(8,128)S(1)}, u32[]{:S(2)}, u32[]{:S(2)}) collective-permute-start(f32[4,256,256]{2,1,0:T(8,128)S(1)} %constant_dynamic-update-slice_fusion.refs_9_), channel_id=1, source_target_pairs={{0,4},{1,5},{2,6},{3,7},{4,0},{5,1},{6,2},{7,3},{8,12},{9,13},{10,... | collective-permute-start | bytes 3145736 | tf_op jit(solution)/shard_map/ppermute | solution.py:457
  113.6 27.2 %collective-permute-start.39 = (f32[4,256,256]{2,1,0:T(8,128)S(1)}, f32[4,256,256]{2,1,0:T(8,128)S(1)}, u32[]{:S(2)}, u32[]{:S(2)}) collective-permute-start(f32[4,256,256]{2,1,0:T(8,128)S(1)} %constant_dynamic-update-slice_fusion.3.refs_10_), channel_id=1, source_target_pairs={{0,4},{1,5},{2,6},{3,7},{4,0},{5,1},{6,2},{7,3},{8,12},{9,13},{10,... | collective-permute-start | bytes 3145736 | tf_op jit(solution)/shard_map/ppermute | solution.py:457
  141.9 91.5 %collective-permute-start.42 = (f32[2,5,256,256]{3,2,1,0:T(8,128)}, f32[2,5,256,256]{3,2,1,0:T(8,128)}, u32[]{:S(2)}, u32[]{:S(2)}) collective-permute-start(f32[2,5,256,256]{3,2,1,0:T(8,128)} %get-tuple-element.43.m0), channel_id=1, source_target_pairs={{0,4},{1,5},{2,6},{3,7},{4,0},{5,1},{6,2},{7,3},{8,12},{9,13},{10,... | collective-permute-start | bytes 7864328 | tf_op jit(solution)/shard_map/ppermute | solution.py:457
  142.6 68.0 %collective-permute-start.41 = (f32[2,5,256,256]{3,2,1,0:T(8,128)}, f32[2,5,256,256]{3,2,1,0:T(8,128)}, u32[]{:S(2)}, u32[]{:S(2)}) collective-permute-start(f32[2,5,256,256]{3,2,1,0:T(8,128)} %get-tuple-element.43.m0), channel_id=1, source_target_pairs={{0,1},{1,0},{2,3},{3,2},{4,5},{5,4},{6,7},{7,6},{8,9},{9,8},{10,11... | collective-permute-start | bytes 7864328 | tf_op jit(solution)/shard_map/ppermute | solution.py:457
  210.7 22.8 %collective-permute-start.43 = (f32[2,5,256,256]{3,2,1,0:T(8,128)}, f32[2,5,256,256]{3,2,1,0:T(8,128)}, u32[]{:S(2)}, u32[]{:S(2)}) collective-permute-start(f32[2,5,256,256]{3,2,1,0:T(8,128)} %collective-permute-done.41.m2), channel_id=1, source_target_pairs={{0,4},{1,5},{2,6},{3,7},{4,0},{5,1},{6,2},{7,3},{8,12},{9,13},{10,... | collective-permute-start | bytes 7864328 | tf_op jit(solution)/shard_map/ppermute | solution.py:457
  210.8 21.9 %collective-permute-start.44 = (f32[864,256]{1,0:T(8,128)S(1)}, f32[864,256]{1,0:T(8,128)S(1)}, u32[]{:S(2)}, u32[]{:S(2)}) collective-permute-start(f32[864,256]{1,0:T(8,128)S(1)} %get-tuple-element.44.exp_a), channel_id=1, source_target_pairs={{0,8},{1,9},{2,10},{3,11},{4,12},{5,13},{6,14},{7,15},{8,0},{9,1},... | collective-permute-start | bytes 2654216 | tf_op jit(solution)/shard_map/ppermute | solution.py:457
  211.5 22.0 %collective-permute-start.45 = (f32[864,256]{1,0:T(8,128)}, f32[864,256]{1,0:T(8,128)}, u32[]{:S(2)}, u32[]{:S(2)}) collective-permute-start(f32[864,256]{1,0:T(8,128)} %get-tuple-element.45.exp_b), channel_id=1, source_target_pairs={{0,16},{1,17},{2,18},{3,19},{4,20},{5,21},{6,22},{7,23},{8,24},{9,... | collective-permute-start | bytes 2654216 | tf_op jit(solution)/shard_map/ppermute | solution.py:457
  212.0 17.7 %collective-permute-start.46 = (f32[320,256]{1,0:T(8,128)}, f32[320,256]{1,0:T(8,128)}, u32[]{:S(2)}, u32[]{:S(2)}) collective-permute-start(f32[320,256]{1,0:T(8,128)} %get-tuple-element.46.exp_c), channel_id=1, source_target_pairs={{0,2},{1,3},{2,0},{3,1},{4,6},{5,7},{6,4},{7,5},{8,10},{9,11},{10,... | collective-permute-start | bytes 983048 | tf_op jit(solution)/shard_map/ppermute | solution.py:457
  (55 other events, 1025.1 us)
